TPU v7x, 128 devices: a whole 4x4x4 slice. The times are simulated.
128 devices in a mesh: py: 16 (over y, x_hi, core), px: 8 (over z, x_lo).
Axes of the slice: x: 4 (x_hi: 2, x_lo: 2; x = x_hi * 2 + x_lo), y: 4, z: 4, core: 2. Of those that a mesh axis runs over, the one named last changes fastest.
Arguments:
- load_terms: float32 [1024, 512, 256], P('py', 'px'), may hold values from -6 to 6
- start_values: float32 [1024, 512, 256], P('py', 'px'), may hold values from -6 to 6
- reaction_rate: float32 [1024, 512, 256], P('py', 'px'), may hold values from 0.1 to 0.9
Outputs:
- corrected: float32 [1024, 512, 256], P('py', 'px')
All inputs are finite; a program needn't handle non-finite values.
Results may differ from a plain program's by a relative error of at most 0.00002.
Values sent between devices are 32-bit elements; how exact they have to be, the bound alone decides.
No kernel may reach another device: no remote copies, remote signals or barrier semaphores. Data moves between devices by JAX's collectives and lax.ppermute only.
A program may use at most 128 MiB of HBM per device.

v0:
```python
import jax
import jax.numpy as jnp
from jax import lax
from jax.sharding import PartitionSpec as P

RATIO = 4
BEFORE = 2
AFTER = 2
INNER = 7


def extended(value, sides, width):
    edges = {}
    for axis, dim in sides:
        size, length = (lax.axis_size(axis), value.shape[dim])
        up = [(i, (i + 1) % size) for i in range(size)]
        last = lax.slice_in_dim(value, length - width, length, axis=dim)
        leading = lax.slice_in_dim(value, 0, width, axis=dim)
        edges[dim] = (
            lax.ppermute(last, axis, up),
            lax.ppermute(leading, axis, [(b, a) for a, b in up]),
        )
    done = []
    for _, dim in sides:
        low, high = edges[dim]
        around = [(width, width) if d in done else (0, 0) for d in range(value.ndim)]
        value = jnp.concatenate([jnp.pad(low, around), value, jnp.pad(high, around)], axis=dim)
        done.append(dim)
    return value


def extended_2(value, sides, width):
    for axis, dim in sides:
        size, length = (lax.axis_size(axis), value.shape[dim])
        up = [(i, (i + 1) % size) for i in range(size)]
        down = [(j, i) for i, j in up]
        last = lax.slice_in_dim(value, length - width, length, axis=dim)
        leading = lax.slice_in_dim(value, 0, width, axis=dim)
        before = lax.ppermute(last, axis, up)
        after = lax.ppermute(leading, axis, down)
        value = jnp.concatenate([before, value, after], axis=dim)
    return value


def around_sum(padded):
    inner_y, inner_x = (padded.shape[0] - 2, padded.shape[1] - 2)
    middle_rows = lax.slice_in_dim(padded, 1, 1 + inner_y, axis=0)
    middle_columns = lax.slice_in_dim(padded, 1, 1 + inner_x, axis=1)
    return (
        lax.slice_in_dim(middle_columns, 0, inner_y, axis=0)
        + lax.slice_in_dim(middle_columns, 2, 2 + inner_y, axis=0)
        + lax.slice_in_dim(middle_rows, 0, inner_x, axis=1)
        + lax.slice_in_dim(middle_rows, 2, 2 + inner_x, axis=1)
    )


def relax_once(padded, values, load, mass_here):
    return values + 0.8 * (load + around_sum(padded) - (4.0 + mass_here) * values) / (
        4.0 + mass_here
    )


def block_means(values):
    cut = values.reshape(
        values.shape[0] // RATIO, RATIO, values.shape[1] // RATIO, RATIO, values.shape[2]
    )
    return jnp.mean(cut, axis=(1, 3))


def spread_blocks(values):
    return jnp.repeat(jnp.repeat(values, RATIO, axis=0), RATIO, axis=1)


def inner_part(values):
    return lax.slice_in_dim(
        lax.slice_in_dim(values, 1, values.shape[0] - 1, axis=0), 1, values.shape[1] - 1, axis=1
    )


def per_device(load_terms, start_values, reaction_rate):
    values = start_values
    for sweep in range(BEFORE):
        values = relax_once(
            extended(values, (("py", 0), ("px", 1)), 1), values, load_terms, reaction_rate
        )
    defect = (
        load_terms
        + around_sum(extended(values, (("py", 0), ("px", 1)), 1))
        - (4.0 + reaction_rate) * values
    )
    coarse_load, coarse_mass = (block_means(defect) * RATIO, block_means(reaction_rate) * RATIO)
    coarse_values = 0.8 * coarse_load / (4.0 + coarse_mass)
    load_mass = extended_2(
        jnp.concatenate([coarse_load, coarse_mass], axis=2), (("py", 0), ("px", 1)), 2
    )
    wide_load, wide_mass = jnp.split(load_mass, 2, axis=2)
    for group in range((INNER - 1) // 2):
        wide_values = extended_2(coarse_values, (("py", 0), ("px", 1)), 2)
        once = relax_once(
            wide_values, inner_part(wide_values), inner_part(wide_load), inner_part(wide_mass)
        )
        middle = inner_part(once)
        coarse_values = relax_once(once, middle, coarse_load, coarse_mass)
    values = values + spread_blocks(coarse_values)
    for sweep in range(AFTER):
        values = relax_once(
            extended(values, (("py", 0), ("px", 1)), 1), values, load_terms, reaction_rate
        )
    return values


def solution(mesh):
    return jax.shard_map(
        per_device,
        mesh=mesh,
        in_specs=(P("py", "px", None), P("py", "px", None), P("py", "px", None)),
        out_specs=P("py", "px", None),
        check_vma=False,
    )
```

profile of v0, /device:TPU:0, one launch (start us, length us, event | category | flops | bytes accessed | tf_op | source)
XLA Modules:
  0.0 184.6 jit_solution(662882571440002466)
XLA Ops:
  0.0 0.9 fusion.91
  0.9 0.1 collective-permute-start
  1.0 5.3 %collective-permute-start.1 = (f32[1,64,256]{2,1,0:T(8,128)S(1)}, f32[1,64,256]{2,1,0:T(8,128)S(1)}, u32[]{:S(2)}, u32[]{:S(2)}) collective-permute-start(f32[1,64,256]{2,1,0:T(8,128)S(1)} %get-tuple-element.23), channel_id=1, source_target_pairs={{8,0},{16,8},{24,16},{32,24},{40,32},{48,40},{56,48},{64,56},{72,6... | collective-permute-start | bytes 196616 | tf_op jit(solution)/shard_map/ppermute | solution.py:21
  6.3 1.3 fusion.90
  7.6 1.7 collective-permute-start.2
  9.3 3.6 %collective-permute-start.3 = (f32[64,1,256]{2,1,0:T(1,128)S(1)}, f32[64,1,256]{2,1,0:T(1,128)S(1)}, u32[]{:S(2)}, u32[]{:S(2)}) collective-permute-start(f32[64,1,256]{2,1,0:T(1,128)S(1)} %get-tuple-element.22), channel_id=1, source_target_pairs={{1,0},{2,1},{3,2},{4,3},{5,4},{6,5},{7,6},{0,7},{9,8},{10,9},{11,1... | collective-permute-start | bytes 196616 | tf_op jit(solution)/shard_map/ppermute | solution.py:21
  12.9 3.1 %constant_dynamic-update-slice_fusion.1 = f32[66,64,256]{2,1,0:T(8,128)S(1)} fusion(f32[66,64,256]{2,1,0:T(8,128)S(1)} %constant_dynamic-update-slice_fusion.2, f32[64,64,256]{2,1,0:T(8,128)} %param.4), kind=kLoop, calls=%fused_computation.180 | loop fusion | bytes 8388608
  16.0 0.3 copy-done
  16.3 1.3 copy-done.2
  17.6 6.5 %fusion.42 = f32[64,64,256]{2,1,0:T(8,128)S(1)} fusion(f32[64,64,256]{2,1,0:T(8,128)} %param.4, f32[64,64,256]{2,1,0:T(8,128)S(1)} %copy-done.2, f32[66,64,256]{2,1,0:T(8,128)S(1)} %constant_dynamic-update-slice_fusion, f32[64,1,256]{2,1,0:T(1,128)S(1)} %collective-permute-done.3, f32[64,1,256]{2,1,0:T(1,128)S(1)} %collective-permute-done.2, ...), kind=kLoop, calls=%fused_computation.75 | loop fusion | flops 20971520 | bytes 21364736 | tf_op jit(solution)/shard_map/add | solution.py:58
  24.1 0.1 fusion.88
  24.3 5.3 %collective-permute-start.5 = (f32[1,64,256]{2,1,0:T(8,128)S(1)}, f32[1,64,256]{2,1,0:T(8,128)S(1)}, u32[]{:S(2)}, u32[]{:S(2)}) collective-permute-start(f32[1,64,256]{2,1,0:T(8,128)S(1)} %get-tuple-element.20), channel_id=1, source_target_pairs={{8,0},{16,8},{24,16},{32,24},{40,32},{48,40},{56,48},{64,56},{72,6... | collective-permute-start | bytes 196616 | tf_op jit(solution)/shard_map/ppermute | solution.py:21
  29.6 4.1 %collective-permute-start.7 = (f32[64,1,256]{2,1,0:T(1,128)S(1)}, f32[64,1,256]{2,1,0:T(1,128)S(1)}, u32[]{:S(2)}, u32[]{:S(2)}) collective-permute-start(f32[64,1,256]{2,1,0:T(1,128)S(1)} %get-tuple-element.18), channel_id=1, source_target_pairs={{1,0},{2,1},{3,2},{4,3},{5,4},{6,5},{7,6},{0,7},{9,8},{10,9},{11,1... | collective-permute-start | bytes 196616 | tf_op jit(solution)/shard_map/ppermute | solution.py:21
  33.8 2.2 %collective-permute-done.6 = f32[64,1,256]{2,1,0:T(1,128)S(1)} collective-permute-done((f32[64,1,256]{2,1,0:T(1,128)S(1)}, f32[64,1,256]{2,1,0:T(1,128)S(1)}, u32[]{:S(2)}, u32[]{:S(2)}) %collective-permute-start.6) | collective-permute-done | bytes 65568 | tf_op jit(solution)/shard_map/ppermute | solution.py:20
  36.0 5.7 %fusion.33 = f32[64,64,256]{2,1,0:T(8,128)S(1)} fusion(f32[64,64,256]{2,1,0:T(8,128)S(1)} %fusion.42, f32[64,64,256]{2,1,0:T(8,128)S(1)} %copy-done.2, f32[64,1,256]{2,1,0:T(1,128)S(1)} %collective-permute-done.7, f32[1,64,256]{2,1,0:T(8,128)S(1)} %collective-permute-done.5, f32[1,64,256]{2,1,0:T(8,128)S(1)} %collective-permute-done.4, ...), kind=kLoop, calls=%fused_computation.58 | loop fusion | flops 25165824 | bytes 17039360 | tf_op jit(solution)/shard_map/add | solution.py:58
  41.7 0.1 fusion.86
  41.8 1.9 %copy-done.4 = f32[64,64,256]{2,1,0:T(8,128)} copy-done((f32[64,64,256]{2,1,0:T(8,128)}, f32[64,64,256]{2,1,0:T(8,128)S(1)}, u32[]{:S(2)}) %copy-start.4) | copy-done | bytes 4194328
  43.7 0.1 collective-permute-start.10
  43.9 4.2 %collective-permute-start.11 = (f32[64,1,256]{2,1,0:T(1,128)S(1)}, f32[64,1,256]{2,1,0:T(1,128)S(1)}, u32[]{:S(2)}, u32[]{:S(2)}) collective-permute-start(f32[64,1,256]{2,1,0:T(1,128)S(1)} %get-tuple-element.14), channel_id=1, source_target_pairs={{1,0},{2,1},{3,2},{4,3},{5,4},{6,5},{7,6},{0,7},{9,8},{10,9},{11,1... | collective-permute-start | bytes 196616 | tf_op jit(solution)/shard_map/ppermute | solution.py:21
  48.0 5.4 %collective-permute-start.9 = (f32[1,64,256]{2,1,0:T(8,128)S(1)}, f32[1,64,256]{2,1,0:T(8,128)S(1)}, u32[]{:S(2)}, u32[]{:S(2)}) collective-permute-start(f32[1,64,256]{2,1,0:T(8,128)S(1)} %get-tuple-element.16), channel_id=1, source_target_pairs={{8,0},{16,8},{24,16},{32,24},{40,32},{48,40},{56,48},{64,56},{72,6... | collective-permute-start | bytes 196616 | tf_op jit(solution)/shard_map/ppermute | solution.py:21
  53.4 5.2 %reshape.13 = f32[16,4,16,4,256]{4,3,2,1,0:T(4,128)} reshape(f32[64,64,256]{2,1,0:T(8,128)} %param.5) | data formatting | bytes 8388608 | tf_op jit(solution)/shard_map/reshape | solution.py:64
  58.6 3.5 %reduce_sum.19 = f32[16,16,256]{2,1,0:T(8,128)S(1)} reduce(f32[16,4,16,4,256]{4,3,2,1,0:T(4,128)} %reshape.13, f32[]{:T(128)} %constant.6.clone.1), dimensions={1,3}, to_apply=%region_1.2 | reduce | flops 983040 | bytes 4456452 | tf_op jit(solution)/shard_map/reduce_sum | solution.py:67
  62.2 13.5 %fusion.23 = f32[64,64,256]{2,1,0:T(8,128)} fusion(f32[64,64,256]{2,1,0:T(8,128)} %param.3, f32[64,1,256]{2,1,0:T(1,128)S(1)} %collective-permute-done.11, f32[1,64,256]{2,1,0:T(8,128)S(1)} %collective-permute-done.9, f32[64,64,256]{2,1,0:T(8,128)} %copy-done.4, f32[1,64,256]{2,1,0:T(8,128)S(1)} %collective-permute-done.8, ...), kind=kLoop, calls=%fused_computation.40 | loop fusion | flops 22020096 | bytes 17039360 | tf_op jit(solution)/shard_map/sub | solution.py:87
  75.6 5.2 %reshape.12 = f32[16,4,16,4,256]{4,3,2,1,0:T(4,128)} reshape(f32[64,64,256]{2,1,0:T(8,128)} %fusion.23) | data formatting | bytes 8388608 | tf_op jit(solution)/shard_map/reshape | solution.py:64
  80.9 3.5 %reduce_sum.18 = f32[16,16,256]{2,1,0:T(8,128)S(1)} reduce(f32[16,4,16,4,256]{4,3,2,1,0:T(4,128)} %reshape.12, f32[]{:T(128)} %constant.6.clone.1), dimensions={1,3}, to_apply=%region_0.1 | reduce | flops 983040 | bytes 4456452 | tf_op jit(solution)/shard_map/reduce_sum | solution.py:67
  84.4 0.1 broadcast_multiply_fusion
  84.5 0.1 collective-permute-start.12
  84.6 5.3 %collective-permute-start.13 = (f32[2,16,256]{2,1,0:T(8,128)S(1)}, f32[2,16,256]{2,1,0:T(8,128)S(1)}, u32[]{:S(2)}, u32[]{:S(2)}) collective-permute-start(f32[2,16,256]{2,1,0:T(8,128)S(1)} %get-tuple-element.43), channel_id=1, source_target_pairs={{8,0},{16,8},{24,16},{32,24},{40,32},{48,40},{56,48},{64,56},{72,6... | collective-permute-start | bytes 98312 | tf_op jit(solution)/shard_map/ppermute | solution.py:40
  90.0 0.1 collective-permute-start.16
  90.1 5.3 %collective-permute-start.17 = (f32[2,16,512]{2,1,0:T(8,128)S(1)}, f32[2,16,512]{2,1,0:T(8,128)S(1)}, u32[]{:S(2)}, u32[]{:S(2)}) collective-permute-start(f32[2,16,512]{2,1,0:T(8,128)S(1)} %get-tuple-element.28), channel_id=1, source_target_pairs={{8,0},{16,8},{24,16},{32,24},{40,32},{48,40},{56,48},{64,56},{72,6... | collective-permute-start | bytes 196616 | tf_op jit(solution)/shard_map/ppermute | solution.py:40
  95.5 0.1 collective-permute-start.14
  95.5 4.1 %collective-permute-start.15 = (f32[20,2,256]{2,1,0:T(2,128)S(1)}, f32[20,2,256]{2,1,0:T(2,128)S(1)}, u32[]{:S(2)}, u32[]{:S(2)}) collective-permute-start(f32[20,2,256]{2,1,0:T(2,128)S(1)} %get-tuple-element.34), channel_id=1, source_target_pairs={{1,0},{2,1},{3,2},{4,3},{5,4},{6,5},{7,6},{0,7},{9,8},{10,9},{11,1... | collective-permute-start | bytes 122888 | tf_op jit(solution)/shard_map/ppermute | solution.py:40
  99.7 0.1 collective-permute-start.18
  99.8 4.1 %collective-permute-start.19 = (f32[20,2,512]{2,1,0:T(2,128)S(1)}, f32[20,2,512]{2,1,0:T(2,128)S(1)}, u32[]{:S(2)}, u32[]{:S(2)}) collective-permute-start(f32[20,2,512]{2,1,0:T(2,128)S(1)} %get-tuple-element.26), channel_id=1, source_target_pairs={{1,0},{2,1},{3,2},{4,3},{5,4},{6,5},{7,6},{0,7},{9,8},{10,9},{11,1... | collective-permute-start | bytes 245768 | tf_op jit(solution)/shard_map/ppermute | solution.py:40
  104.0 2.4 %collective-permute-done.18 = f32[20,2,512]{2,1,0:T(2,128)S(1)} collective-permute-done((f32[20,2,512]{2,1,0:T(2,128)S(1)}, f32[20,2,512]{2,1,0:T(2,128)S(1)}, u32[]{:S(2)}, u32[]{:S(2)}) %collective-permute-start.18) | collective-permute-done | bytes 81952 | tf_op jit(solution)/shard_map/ppermute | solution.py:39
  106.4 0.4 fusion.65
  106.8 0.2 fusion.81
  107.0 0.1 collective-permute-start.20
  107.1 5.3 %collective-permute-start.21 = (f32[2,16,256]{2,1,0:T(8,128)S(1)}, f32[2,16,256]{2,1,0:T(8,128)S(1)}, u32[]{:S(2)}, u32[]{:S(2)}) collective-permute-start(f32[2,16,256]{2,1,0:T(8,128)S(1)} %get-tuple-element.38), channel_id=1, source_target_pairs={{8,0},{16,8},{24,16},{32,24},{40,32},{48,40},{56,48},{64,56},{72,6... | collective-permute-start | bytes 98312 | tf_op jit(solution)/shard_map/ppermute | solution.py:40
  112.4 1.6 collective-permute-done.20
  114.2 4.1 %collective-permute-start.23 = (f32[20,2,256]{2,1,0:T(2,128)S(1)}, f32[20,2,256]{2,1,0:T(2,128)S(1)}, u32[]{:S(2)}, u32[]{:S(2)}) collective-permute-start(f32[20,2,256]{2,1,0:T(2,128)S(1)} %get-tuple-element.32), channel_id=1, source_target_pairs={{1,0},{2,1},{3,2},{4,3},{5,4},{6,5},{7,6},{0,7},{9,8},{10,9},{11,1... | collective-permute-start | bytes 122888 | tf_op jit(solution)/shard_map/ppermute | solution.py:40
  118.3 2.1 %collective-permute-done.22 = f32[20,2,256]{2,1,0:T(2,128)S(1)} collective-permute-done((f32[20,2,256]{2,1,0:T(2,128)S(1)}, f32[20,2,256]{2,1,0:T(2,128)S(1)}, u32[]{:S(2)}, u32[]{:S(2)}) %collective-permute-start.22) | collective-permute-done | bytes 40992 | tf_op jit(solution)/shard_map/ppermute | solution.py:39
  120.5 0.4 fusion.57
  120.8 0.2 fusion.76
  121.1 5.3 %collective-permute-start.25 = (f32[2,16,256]{2,1,0:T(8,128)S(1)}, f32[2,16,256]{2,1,0:T(8,128)S(1)}, u32[]{:S(2)}, u32[]{:S(2)}) collective-permute-start(f32[2,16,256]{2,1,0:T(8,128)S(1)} %get-tuple-element.36), channel_id=1, source_target_pairs={{8,0},{16,8},{24,16},{32,24},{40,32},{48,40},{56,48},{64,56},{72,6... | collective-permute-start | bytes 98312 | tf_op jit(solution)/shard_map/ppermute | solution.py:40
  126.5 1.7 collective-permute-done.24
  128.3 4.1 %collective-permute-start.27 = (f32[20,2,256]{2,1,0:T(2,128)S(1)}, f32[20,2,256]{2,1,0:T(2,128)S(1)}, u32[]{:S(2)}, u32[]{:S(2)}) collective-permute-start(f32[20,2,256]{2,1,0:T(2,128)S(1)} %get-tuple-element.30), channel_id=1, source_target_pairs={{1,0},{2,1},{3,2},{4,3},{5,4},{6,5},{7,6},{0,7},{9,8},{10,9},{11,1... | collective-permute-start | bytes 122888 | tf_op jit(solution)/shard_map/ppermute | solution.py:40
  132.4 2.0 %collective-permute-done.26 = f32[20,2,256]{2,1,0:T(2,128)S(1)} collective-permute-done((f32[20,2,256]{2,1,0:T(2,128)S(1)}, f32[20,2,256]{2,1,0:T(2,128)S(1)}, u32[]{:S(2)}, u32[]{:S(2)}) %collective-permute-start.26) | collective-permute-done | bytes 40992 | tf_op jit(solution)/shard_map/ppermute | solution.py:39
  134.5 0.4 fusion.50
  134.9 0.2 fusion.71
  135.0 0.1 broadcast_in_dim.6
  135.2 2.8 %broadcast_in_dim.7 = f32[64,16,4,256]{3,2,1,0:T(4,128)} broadcast(f32[64,16,256]{2,1,0:T(8,128)S(1)} %bitcast.1), dimensions={0,1,3} | broadcast | bytes 5242880 | tf_op jit(solution)/shard_map/broadcast_in_dim | solution.py:71
  137.9 5.3 %reshape.15 = f32[64,64,256]{2,1,0:T(8,128)} reshape(f32[64,16,4,256]{3,2,1,0:T(4,128)} %broadcast_in_dim.7) | data formatting | bytes 8388608 | tf_op jit(solution)/shard_map/reshape | solution.py:71
  143.3 4.4 %add.260 = f32[64,64,256]{2,1,0:T(8,128)S(1)} add(f32[64,64,256]{2,1,0:T(8,128)} %copy-done.4, f32[64,64,256]{2,1,0:T(8,128)} %reshape.15) | non-fusion elementwise | flops 1048576 | bytes 12582912 | tf_op jit(solution)/shard_map/add | solution.py:104
  147.7 0.1 fusion.84
  147.9 5.3 %collective-permute-start.29 = (f32[1,64,256]{2,1,0:T(8,128)S(1)}, f32[1,64,256]{2,1,0:T(8,128)S(1)}, u32[]{:S(2)}, u32[]{:S(2)}) collective-permute-start(f32[1,64,256]{2,1,0:T(8,128)S(1)} %get-tuple-element.12), channel_id=1, source_target_pairs={{8,0},{16,8},{24,16},{32,24},{40,32},{48,40},{56,48},{64,56},{72,6... | collective-permute-start | bytes 196616 | tf_op jit(solution)/shard_map/ppermute | solution.py:21
  153.2 4.1 %collective-permute-start.31 = (f32[64,1,256]{2,1,0:T(1,128)S(1)}, f32[64,1,256]{2,1,0:T(1,128)S(1)}, u32[]{:S(2)}, u32[]{:S(2)}) collective-permute-start(f32[64,1,256]{2,1,0:T(1,128)S(1)} %get-tuple-element.10), channel_id=1, source_target_pairs={{1,0},{2,1},{3,2},{4,3},{5,4},{6,5},{7,6},{0,7},{9,8},{10,9},{11,1... | collective-permute-start | bytes 196616 | tf_op jit(solution)/shard_map/ppermute | solution.py:21
  157.4 2.9 %collective-permute-done.30 = f32[64,1,256]{2,1,0:T(1,128)S(1)} collective-permute-done((f32[64,1,256]{2,1,0:T(1,128)S(1)}, f32[64,1,256]{2,1,0:T(1,128)S(1)}, u32[]{:S(2)}, u32[]{:S(2)}) %collective-permute-start.30) | collective-permute-done | bytes 65568 | tf_op jit(solution)/shard_map/ppermute | solution.py:20
  160.3 5.7 %fusion.16 = f32[64,64,256]{2,1,0:T(8,128)S(1)} fusion(f32[64,64,256]{2,1,0:T(8,128)S(1)} %add.260, f32[64,64,256]{2,1,0:T(8,128)S(1)} %copy-done.3, f32[64,1,256]{2,1,0:T(1,128)S(1)} %collective-permute-done.31, f32[1,64,256]{2,1,0:T(8,128)S(1)} %collective-permute-done.29, f32[1,64,256]{2,1,0:T(8,128)S(1)} %collective-permute-done.28, ...), kind=kLoop, calls=%fused_computation.25 | loop fusion | flops 25165824 | bytes 17039360 | tf_op jit(solution)/shard_map/add | solution.py:58
  166.1 0.1 fusion.82
  166.3 5.3 %collective-permute-start.33 = (f32[1,64,256]{2,1,0:T(8,128)S(1)}, f32[1,64,256]{2,1,0:T(8,128)S(1)}, u32[]{:S(2)}, u32[]{:S(2)}) collective-permute-start(f32[1,64,256]{2,1,0:T(8,128)S(1)} %get-tuple-element.8), channel_id=1, source_target_pairs={{8,0},{16,8},{24,16},{32,24},{40,32},{48,40},{56,48},{64,56},{72,6... | collective-permute-start | bytes 196616 | tf_op jit(solution)/shard_map/ppermute | solution.py:21
  171.6 4.1 %collective-permute-start.35 = (f32[64,1,256]{2,1,0:T(1,128)S(1)}, f32[64,1,256]{2,1,0:T(1,128)S(1)}, u32[]{:S(2)}, u32[]{:S(2)}) collective-permute-start(f32[64,1,256]{2,1,0:T(1,128)S(1)} %get-tuple-element.6), channel_id=1, source_target_pairs={{1,0},{2,1},{3,2},{4,3},{5,4},{6,5},{7,6},{0,7},{9,8},{10,9},{11,1... | collective-permute-start | bytes 196616 | tf_op jit(solution)/shard_map/ppermute | solution.py:21
  175.8 2.2 %collective-permute-done.34 = f32[64,1,256]{2,1,0:T(1,128)S(1)} collective-permute-done((f32[64,1,256]{2,1,0:T(1,128)S(1)}, f32[64,1,256]{2,1,0:T(1,128)S(1)}, u32[]{:S(2)}, u32[]{:S(2)}) %collective-permute-start.34) | collective-permute-done | bytes 65568 | tf_op jit(solution)/shard_map/ppermute | solution.py:20
  178.0 6.7 %fusion.6 = f32[64,64,256]{2,1,0:T(8,128)} fusion(f32[64,64,256]{2,1,0:T(8,128)S(1)} %fusion.16, f32[64,64,256]{2,1,0:T(8,128)S(1)} %copy-done.3, f32[64,1,256]{2,1,0:T(1,128)S(1)} %collective-permute-done.35, f32[1,64,256]{2,1,0:T(8,128)S(1)} %collective-permute-done.33, f32[1,64,256]{2,1,0:T(8,128)S(1)} %collective-permute-done.32, ...), kind=kLoop, calls=%fused_computation.7 | loop fusion | flops 25165824 | bytes 17039360 | tf_op jit(solution)/shard_map/add | solution.py:58
  (62 shorter events, 1.0 us)
Async XLA Ops:
  0.9 12.0 %collective-permute-start = (f32[1,64,256]{2,1,0:T(8,128)S(1)}, f32[1,64,256]{2,1,0:T(8,128)S(1)}, u32[]{:S(2)}, u32[]{:S(2)}) collective-permute-start(f32[1,64,256]{2,1,0:T(8,128)S(1)} %get-tuple-element.24), channel_id=1, source_target_pairs={{0,8},{8,16},{16,24},{24,32},{32,40},{40,48},{48,56},{56,64},{64,7... | collective-permute-start | bytes 196616 | tf_op jit(solution)/shard_map/ppermute | solution.py:20
  1.0 15.0 %collective-permute-start.1 = (f32[1,64,256]{2,1,0:T(8,128)S(1)}, f32[1,64,256]{2,1,0:T(8,128)S(1)}, u32[]{:S(2)}, u32[]{:S(2)}) collective-permute-start(f32[1,64,256]{2,1,0:T(8,128)S(1)} %get-tuple-element.23), channel_id=1, source_target_pairs={{8,0},{16,8},{24,16},{32,24},{40,32},{48,40},{56,48},{64,56},{72,6... | collective-permute-start | bytes 196616 | tf_op jit(solution)/shard_map/ppermute | solution.py:21
  7.6 8.4 %collective-permute-start.2 = (f32[64,1,256]{2,1,0:T(1,128)S(1)}, f32[64,1,256]{2,1,0:T(1,128)S(1)}, u32[]{:S(2)}, u32[]{:S(2)}) collective-permute-start(f32[64,1,256]{2,1,0:T(1,128)S(1)} %get-tuple-element.21), channel_id=1, source_target_pairs={{0,1},{1,2},{2,3},{3,4},{4,5},{5,6},{6,7},{7,0},{8,9},{9,10},{10,1... | collective-permute-start | bytes 196616 | tf_op jit(solution)/shard_map/ppermute | solution.py:20
  9.3 6.8 %collective-permute-start.3 = (f32[64,1,256]{2,1,0:T(1,128)S(1)}, f32[64,1,256]{2,1,0:T(1,128)S(1)}, u32[]{:S(2)}, u32[]{:S(2)}) collective-permute-start(f32[64,1,256]{2,1,0:T(1,128)S(1)} %get-tuple-element.22), channel_id=1, source_target_pairs={{1,0},{2,1},{3,2},{4,3},{5,4},{6,5},{7,6},{0,7},{9,8},{10,9},{11,1... | collective-permute-start | bytes 196616 | tf_op jit(solution)/shard_map/ppermute | solution.py:21
  12.8 3.5 %copy-start = (f32[64,64,256]{2,1,0:T(8,128)S(1)}, f32[64,64,256]{2,1,0:T(8,128)}, u32[]{:S(2)}) copy-start(f32[64,64,256]{2,1,0:T(8,128)} %param.5) | copy-start | bytes 12582916
  12.9 4.7 %copy-start.2 = (f32[64,64,256]{2,1,0:T(8,128)S(1)}, f32[64,64,256]{2,1,0:T(8,128)}, u32[]{:S(2)}) copy-start(f32[64,64,256]{2,1,0:T(8,128)} %param.3) | copy-start | bytes 12582916
  24.2 9.6 %collective-permute-start.4 = (f32[1,64,256]{2,1,0:T(8,128)S(1)}, f32[1,64,256]{2,1,0:T(8,128)S(1)}, u32[]{:S(2)}, u32[]{:S(2)}) collective-permute-start(f32[1,64,256]{2,1,0:T(8,128)S(1)} %get-tuple-element.19), channel_id=1, source_target_pairs={{0,8},{8,16},{16,24},{24,32},{32,40},{40,48},{48,56},{56,64},{64,7... | collective-permute-start | bytes 196616 | tf_op jit(solution)/shard_map/ppermute | solution.py:20
  24.3 9.5 %collective-permute-start.5 = (f32[1,64,256]{2,1,0:T(8,128)S(1)}, f32[1,64,256]{2,1,0:T(8,128)S(1)}, u32[]{:S(2)}, u32[]{:S(2)}) collective-permute-start(f32[1,64,256]{2,1,0:T(8,128)S(1)} %get-tuple-element.20), channel_id=1, source_target_pairs={{8,0},{16,8},{24,16},{32,24},{40,32},{48,40},{56,48},{64,56},{72,6... | collective-permute-start | bytes 196616 | tf_op jit(solution)/shard_map/ppermute | solution.py:21
  29.6 6.4 %collective-permute-start.6 = (f32[64,1,256]{2,1,0:T(1,128)S(1)}, f32[64,1,256]{2,1,0:T(1,128)S(1)}, u32[]{:S(2)}, u32[]{:S(2)}) collective-permute-start(f32[64,1,256]{2,1,0:T(1,128)S(1)} %get-tuple-element.17), channel_id=1, source_target_pairs={{0,1},{1,2},{2,3},{3,4},{4,5},{5,6},{6,7},{7,0},{8,9},{9,10},{10,1... | collective-permute-start | bytes 196616 | tf_op jit(solution)/shard_map/ppermute | solution.py:20
  29.6 6.4 %collective-permute-start.7 = (f32[64,1,256]{2,1,0:T(1,128)S(1)}, f32[64,1,256]{2,1,0:T(1,128)S(1)}, u32[]{:S(2)}, u32[]{:S(2)}) collective-permute-start(f32[64,1,256]{2,1,0:T(1,128)S(1)} %get-tuple-element.18), channel_id=1, source_target_pairs={{1,0},{2,1},{3,2},{4,3},{5,4},{6,5},{7,6},{0,7},{9,8},{10,9},{11,1... | collective-permute-start | bytes 196616 | tf_op jit(solution)/shard_map/ppermute | solution.py:21
  41.7 2.0 %copy-start.4 = (f32[64,64,256]{2,1,0:T(8,128)}, f32[64,64,256]{2,1,0:T(8,128)S(1)}, u32[]{:S(2)}) copy-start(f32[64,64,256]{2,1,0:T(8,128)S(1)} %fusion.33) | copy-start | bytes 12582916
  43.7 18.4 %collective-permute-start.10 = (f32[64,1,256]{2,1,0:T(1,128)S(1)}, f32[64,1,256]{2,1,0:T(1,128)S(1)}, u32[]{:S(2)}, u32[]{:S(2)}) collective-permute-start(f32[64,1,256]{2,1,0:T(1,128)S(1)} %get-tuple-element.13), channel_id=1, source_target_pairs={{0,1},{1,2},{2,3},{3,4},{4,5},{5,6},{6,7},{7,0},{8,9},{9,10},{10,1... | collective-permute-start | bytes 196616 | tf_op jit(solution)/shard_map/ppermute | solution.py:20
  43.9 18.3 %collective-permute-start.11 = (f32[64,1,256]{2,1,0:T(1,128)S(1)}, f32[64,1,256]{2,1,0:T(1,128)S(1)}, u32[]{:S(2)}, u32[]{:S(2)}) collective-permute-start(f32[64,1,256]{2,1,0:T(1,128)S(1)} %get-tuple-element.14), channel_id=1, source_target_pairs={{1,0},{2,1},{3,2},{4,3},{5,4},{6,5},{7,6},{0,7},{9,8},{10,9},{11,1... | collective-permute-start | bytes 196616 | tf_op jit(solution)/shard_map/ppermute | solution.py:21
  48.0 14.1 %collective-permute-start.8 = (f32[1,64,256]{2,1,0:T(8,128)S(1)}, f32[1,64,256]{2,1,0:T(8,128)S(1)}, u32[]{:S(2)}, u32[]{:S(2)}) collective-permute-start(f32[1,64,256]{2,1,0:T(8,128)S(1)} %get-tuple-element.15), channel_id=1, source_target_pairs={{0,8},{8,16},{16,24},{24,32},{32,40},{40,48},{48,56},{56,64},{64,7... | collective-permute-start | bytes 196616 | tf_op jit(solution)/shard_map/ppermute | solution.py:20
  48.0 14.1 %collective-permute-start.9 = (f32[1,64,256]{2,1,0:T(8,128)S(1)}, f32[1,64,256]{2,1,0:T(8,128)S(1)}, u32[]{:S(2)}, u32[]{:S(2)}) collective-permute-start(f32[1,64,256]{2,1,0:T(8,128)S(1)} %get-tuple-element.16), channel_id=1, source_target_pairs={{8,0},{16,8},{24,16},{32,24},{40,32},{48,40},{56,48},{64,56},{72,6... | collective-permute-start | bytes 196616 | tf_op jit(solution)/shard_map/ppermute | solution.py:21
  84.5 10.9 %collective-permute-start.12 = (f32[2,16,256]{2,1,0:T(8,128)S(1)}, f32[2,16,256]{2,1,0:T(8,128)S(1)}, u32[]{:S(2)}, u32[]{:S(2)}) collective-permute-start(f32[2,16,256]{2,1,0:T(8,128)S(1)} %get-tuple-element.42), channel_id=1, source_target_pairs={{0,8},{8,16},{16,24},{24,32},{32,40},{40,48},{48,56},{56,64},{64,7... | collective-permute-start | bytes 98312 | tf_op jit(solution)/shard_map/ppermute | solution.py:39
  84.6 10.8 %collective-permute-start.13 = (f32[2,16,256]{2,1,0:T(8,128)S(1)}, f32[2,16,256]{2,1,0:T(8,128)S(1)}, u32[]{:S(2)}, u32[]{:S(2)}) collective-permute-start(f32[2,16,256]{2,1,0:T(8,128)S(1)} %get-tuple-element.43), channel_id=1, source_target_pairs={{8,0},{16,8},{24,16},{32,24},{40,32},{48,40},{56,48},{64,56},{72,6... | collective-permute-start | bytes 98312 | tf_op jit(solution)/shard_map/ppermute | solution.py:40
  90.0 9.7 %collective-permute-start.16 = (f32[2,16,512]{2,1,0:T(8,128)S(1)}, f32[2,16,512]{2,1,0:T(8,128)S(1)}, u32[]{:S(2)}, u32[]{:S(2)}) collective-permute-start(f32[2,16,512]{2,1,0:T(8,128)S(1)} %get-tuple-element.27), channel_id=1, source_target_pairs={{0,8},{8,16},{16,24},{24,32},{32,40},{40,48},{48,56},{56,64},{64,7... | collective-permute-start | bytes 196616 | tf_op jit(solution)/shard_map/ppermute | solution.py:39
  90.1 9.6 %collective-permute-start.17 = (f32[2,16,512]{2,1,0:T(8,128)S(1)}, f32[2,16,512]{2,1,0:T(8,128)S(1)}, u32[]{:S(2)}, u32[]{:S(2)}) collective-permute-start(f32[2,16,512]{2,1,0:T(8,128)S(1)} %get-tuple-element.28), channel_id=1, source_target_pairs={{8,0},{16,8},{24,16},{32,24},{40,32},{48,40},{56,48},{64,56},{72,6... | collective-permute-start | bytes 196616 | tf_op jit(solution)/shard_map/ppermute | solution.py:40
  95.5 8.5 %collective-permute-start.14 = (f32[20,2,256]{2,1,0:T(2,128)S(1)}, f32[20,2,256]{2,1,0:T(2,128)S(1)}, u32[]{:S(2)}, u32[]{:S(2)}) collective-permute-start(f32[20,2,256]{2,1,0:T(2,128)S(1)} %get-tuple-element.33), channel_id=1, source_target_pairs={{0,1},{1,2},{2,3},{3,4},{4,5},{5,6},{6,7},{7,0},{8,9},{9,10},{10,1... | collective-permute-start | bytes 122888 | tf_op jit(solution)/shard_map/ppermute | solution.py:39
  95.5 8.4 %collective-permute-start.15 = (f32[20,2,256]{2,1,0:T(2,128)S(1)}, f32[20,2,256]{2,1,0:T(2,128)S(1)}, u32[]{:S(2)}, u32[]{:S(2)}) collective-permute-start(f32[20,2,256]{2,1,0:T(2,128)S(1)} %get-tuple-element.34), channel_id=1, source_target_pairs={{1,0},{2,1},{3,2},{4,3},{5,4},{6,5},{7,6},{0,7},{9,8},{10,9},{11,1... | collective-permute-start | bytes 122888 | tf_op jit(solution)/shard_map/ppermute | solution.py:40
  99.7 6.7 %collective-permute-start.18 = (f32[20,2,512]{2,1,0:T(2,128)S(1)}, f32[20,2,512]{2,1,0:T(2,128)S(1)}, u32[]{:S(2)}, u32[]{:S(2)}) collective-permute-start(f32[20,2,512]{2,1,0:T(2,128)S(1)} %get-tuple-element.25), channel_id=1, source_target_pairs={{0,1},{1,2},{2,3},{3,4},{4,5},{5,6},{6,7},{7,0},{8,9},{9,10},{10,1... | collective-permute-start | bytes 245768 | tf_op jit(solution)/shard_map/ppermute | solution.py:39
  99.8 6.6 %collective-permute-start.19 = (f32[20,2,512]{2,1,0:T(2,128)S(1)}, f32[20,2,512]{2,1,0:T(2,128)S(1)}, u32[]{:S(2)}, u32[]{:S(2)}) collective-permute-start(f32[20,2,512]{2,1,0:T(2,128)S(1)} %get-tuple-element.26), channel_id=1, source_target_pairs={{1,0},{2,1},{3,2},{4,3},{5,4},{6,5},{7,6},{0,7},{9,8},{10,9},{11,1... | collective-permute-start | bytes 245768 | tf_op jit(solution)/shard_map/ppermute | solution.py:40
  107.0 7.0 %collective-permute-start.20 = (f32[2,16,256]{2,1,0:T(8,128)S(1)}, f32[2,16,256]{2,1,0:T(8,128)S(1)}, u32[]{:S(2)}, u32[]{:S(2)}) collective-permute-start(f32[2,16,256]{2,1,0:T(8,128)S(1)} %get-tuple-element.37), channel_id=1, source_target_pairs={{0,8},{8,16},{16,24},{24,32},{32,40},{40,48},{48,56},{56,64},{64,7... | collective-permute-start | bytes 98312 | tf_op jit(solution)/shard_map/ppermute | solution.py:39
  107.1 6.9 %collective-permute-start.21 = (f32[2,16,256]{2,1,0:T(8,128)S(1)}, f32[2,16,256]{2,1,0:T(8,128)S(1)}, u32[]{:S(2)}, u32[]{:S(2)}) collective-permute-start(f32[2,16,256]{2,1,0:T(8,128)S(1)} %get-tuple-element.38), channel_id=1, source_target_pairs={{8,0},{16,8},{24,16},{32,24},{40,32},{48,40},{56,48},{64,56},{72,6... | collective-permute-start | bytes 98312 | tf_op jit(solution)/shard_map/ppermute | solution.py:40
  114.1 6.3 %collective-permute-start.22 = (f32[20,2,256]{2,1,0:T(2,128)S(1)}, f32[20,2,256]{2,1,0:T(2,128)S(1)}, u32[]{:S(2)}, u32[]{:S(2)}) collective-permute-start(f32[20,2,256]{2,1,0:T(2,128)S(1)} %get-tuple-element.31), channel_id=1, source_target_pairs={{0,1},{1,2},{2,3},{3,4},{4,5},{5,6},{6,7},{7,0},{8,9},{9,10},{10,1... | collective-permute-start | bytes 122888 | tf_op jit(solution)/shard_map/ppermute | solution.py:39
  114.2 6.2 %collective-permute-start.23 = (f32[20,2,256]{2,1,0:T(2,128)S(1)}, f32[20,2,256]{2,1,0:T(2,128)S(1)}, u32[]{:S(2)}, u32[]{:S(2)}) collective-permute-start(f32[20,2,256]{2,1,0:T(2,128)S(1)} %get-tuple-element.32), channel_id=1, source_target_pairs={{1,0},{2,1},{3,2},{4,3},{5,4},{6,5},{7,6},{0,7},{9,8},{10,9},{11,1... | collective-permute-start | bytes 122888 | tf_op jit(solution)/shard_map/ppermute | solution.py:40
  121.0 7.2 %collective-permute-start.24 = (f32[2,16,256]{2,1,0:T(8,128)S(1)}, f32[2,16,256]{2,1,0:T(8,128)S(1)}, u32[]{:S(2)}, u32[]{:S(2)}) collective-permute-start(f32[2,16,256]{2,1,0:T(8,128)S(1)} %get-tuple-element.35), channel_id=1, source_target_pairs={{0,8},{8,16},{16,24},{24,32},{32,40},{40,48},{48,56},{56,64},{64,7... | collective-permute-start | bytes 98312 | tf_op jit(solution)/shard_map/ppermute | solution.py:39
  121.1 7.1 %collective-permute-start.25 = (f32[2,16,256]{2,1,0:T(8,128)S(1)}, f32[2,16,256]{2,1,0:T(8,128)S(1)}, u32[]{:S(2)}, u32[]{:S(2)}) collective-permute-start(f32[2,16,256]{2,1,0:T(8,128)S(1)} %get-tuple-element.36), channel_id=1, source_target_pairs={{8,0},{16,8},{24,16},{32,24},{40,32},{48,40},{56,48},{64,56},{72,6... | collective-permute-start | bytes 98312 | tf_op jit(solution)/shard_map/ppermute | solution.py:40
  128.2 6.2 %collective-permute-start.26 = (f32[20,2,256]{2,1,0:T(2,128)S(1)}, f32[20,2,256]{2,1,0:T(2,128)S(1)}, u32[]{:S(2)}, u32[]{:S(2)}) collective-permute-start(f32[20,2,256]{2,1,0:T(2,128)S(1)} %get-tuple-element.29), channel_id=1, source_target_pairs={{0,1},{1,2},{2,3},{3,4},{4,5},{5,6},{6,7},{7,0},{8,9},{9,10},{10,1... | collective-permute-start | bytes 122888 | tf_op jit(solution)/shard_map/ppermute | solution.py:39
  128.3 6.1 %collective-permute-start.27 = (f32[20,2,256]{2,1,0:T(2,128)S(1)}, f32[20,2,256]{2,1,0:T(2,128)S(1)}, u32[]{:S(2)}, u32[]{:S(2)}) collective-permute-start(f32[20,2,256]{2,1,0:T(2,128)S(1)} %get-tuple-element.30), channel_id=1, source_target_pairs={{1,0},{2,1},{3,2},{4,3},{5,4},{6,5},{7,6},{0,7},{9,8},{10,9},{11,1... | collective-permute-start | bytes 122888 | tf_op jit(solution)/shard_map/ppermute | solution.py:40
  143.3 17.0 %copy-start.1 = (f32[64,64,256]{2,1,0:T(8,128)S(1)}, f32[64,64,256]{2,1,0:T(8,128)}, u32[]{:S(2)}) copy-start(f32[64,64,256]{2,1,0:T(8,128)} %param.5) | copy-start | bytes 12582916
  143.3 17.0 %copy-start.3 = (f32[64,64,256]{2,1,0:T(8,128)S(1)}, f32[64,64,256]{2,1,0:T(8,128)}, u32[]{:S(2)}) copy-start(f32[64,64,256]{2,1,0:T(8,128)} %param.3) | copy-start | bytes 12582916
  147.8 9.6 %collective-permute-start.28 = (f32[1,64,256]{2,1,0:T(8,128)S(1)}, f32[1,64,256]{2,1,0:T(8,128)S(1)}, u32[]{:S(2)}, u32[]{:S(2)}) collective-permute-start(f32[1,64,256]{2,1,0:T(8,128)S(1)} %get-tuple-element.11), channel_id=1, source_target_pairs={{0,8},{8,16},{16,24},{24,32},{32,40},{40,48},{48,56},{56,64},{64,7... | collective-permute-start | bytes 196616 | tf_op jit(solution)/shard_map/ppermute | solution.py:20
  147.9 9.5 %collective-permute-start.29 = (f32[1,64,256]{2,1,0:T(8,128)S(1)}, f32[1,64,256]{2,1,0:T(8,128)S(1)}, u32[]{:S(2)}, u32[]{:S(2)}) collective-permute-start(f32[1,64,256]{2,1,0:T(8,128)S(1)} %get-tuple-element.12), channel_id=1, source_target_pairs={{8,0},{16,8},{24,16},{32,24},{40,32},{48,40},{56,48},{64,56},{72,6... | collective-permute-start | bytes 196616 | tf_op jit(solution)/shard_map/ppermute | solution.py:21
  153.2 7.1 %collective-permute-start.30 = (f32[64,1,256]{2,1,0:T(1,128)S(1)}, f32[64,1,256]{2,1,0:T(1,128)S(1)}, u32[]{:S(2)}, u32[]{:S(2)}) collective-permute-start(f32[64,1,256]{2,1,0:T(1,128)S(1)} %get-tuple-element.9), channel_id=1, source_target_pairs={{0,1},{1,2},{2,3},{3,4},{4,5},{5,6},{6,7},{7,0},{8,9},{9,10},{10,1... | collective-permute-start | bytes 196616 | tf_op jit(solution)/shard_map/ppermute | solution.py:20
  153.2 7.1 %collective-permute-start.31 = (f32[64,1,256]{2,1,0:T(1,128)S(1)}, f32[64,1,256]{2,1,0:T(1,128)S(1)}, u32[]{:S(2)}, u32[]{:S(2)}) collective-permute-start(f32[64,1,256]{2,1,0:T(1,128)S(1)} %get-tuple-element.10), channel_id=1, source_target_pairs={{1,0},{2,1},{3,2},{4,3},{5,4},{6,5},{7,6},{0,7},{9,8},{10,9},{11,1... | collective-permute-start | bytes 196616 | tf_op jit(solution)/shard_map/ppermute | solution.py:21
  166.2 9.6 %collective-permute-start.32 = (f32[1,64,256]{2,1,0:T(8,128)S(1)}, f32[1,64,256]{2,1,0:T(8,128)S(1)}, u32[]{:S(2)}, u32[]{:S(2)}) collective-permute-start(f32[1,64,256]{2,1,0:T(8,128)S(1)} %get-tuple-element.7), channel_id=1, source_target_pairs={{0,8},{8,16},{16,24},{24,32},{32,40},{40,48},{48,56},{56,64},{64,7... | collective-permute-start | bytes 196616 | tf_op jit(solution)/shard_map/ppermute | solution.py:20
  166.3 9.5 %collective-permute-start.33 = (f32[1,64,256]{2,1,0:T(8,128)S(1)}, f32[1,64,256]{2,1,0:T(8,128)S(1)}, u32[]{:S(2)}, u32[]{:S(2)}) collective-permute-start(f32[1,64,256]{2,1,0:T(8,128)S(1)} %get-tuple-element.8), channel_id=1, source_target_pairs={{8,0},{16,8},{24,16},{32,24},{40,32},{48,40},{56,48},{64,56},{72,6... | collective-permute-start | bytes 196616 | tf_op jit(solution)/shard_map/ppermute | solution.py:21
  171.6 6.4 %collective-permute-start.34 = (f32[64,1,256]{2,1,0:T(1,128)S(1)}, f32[64,1,256]{2,1,0:T(1,128)S(1)}, u32[]{:S(2)}, u32[]{:S(2)}) collective-permute-start(f32[64,1,256]{2,1,0:T(1,128)S(1)} %get-tuple-element.5), channel_id=1, source_target_pairs={{0,1},{1,2},{2,3},{3,4},{4,5},{5,6},{6,7},{7,0},{8,9},{9,10},{10,1... | collective-permute-start | bytes 196616 | tf_op jit(solution)/shard_map/ppermute | solution.py:20
  171.6 6.4 %collective-permute-start.35 = (f32[64,1,256]{2,1,0:T(1,128)S(1)}, f32[64,1,256]{2,1,0:T(1,128)S(1)}, u32[]{:S(2)}, u32[]{:S(2)}) collective-permute-start(f32[64,1,256]{2,1,0:T(1,128)S(1)} %get-tuple-element.6), channel_id=1, source_target_pairs={{1,0},{2,1},{3,2},{4,3},{5,4},{6,5},{7,6},{0,7},{9,8},{10,9},{11,1... | collective-permute-start | bytes 196616 | tf_op jit(solution)/shard_map/ppermute | solution.py:21
where the time goes:
time: 185 us
  starting transfers between devices  87.4 us (47%)
  other arithmetic  51.7 us (28%)
  local copies, waits for them, and re-layouts  27.8 us (15%)
  waiting for transfers between devices  17.3 us (9%)
    ppermute x10, starting transfers between devices, extended(): lax.ppermute(leading, axis, [(b, a) for a, b in up])  46.9 us
    ppermute x8, starting transfers between devices, extended_2(): after = lax.ppermute(leading, axis, down)  37.9 us
    add x10, other arithmetic, relax_once(): values + 0.8 * (load + around_sum(padded) - (4.0 + mass_here) * values) /...  26.2 us
    sub x1, other arithmetic, per_device(): load_terms + around_sum(extended(values, (('py', 0), ('px', 1)), 1))  13.5 us
    reshape x2, local copies, waits for them, and re-layouts, block_means(): values.reshape(values.shape[0] // RATIO, RATIO, values.shape[1] // RATIO,...  10.4 us
    ppermute x8, waiting for transfers between devices, extended_2(): before = lax.ppermute(last, axis, up)  9.83 us
    ppermute x10, waiting for transfers between devices, extended(): lax.ppermute(last, axis, up)  7.41 us
    reduce_sum x2, other arithmetic, block_means(): return jnp.mean(cut, axis=(1, 3))  7.09 us
  transfers between devices with their start and end apart: 36, of which 8 were waited for; matrix products, arithmetic and copies ran while one was open for 7% of the time, Pallas kernels for 0%

commit v1 on v0

v1 whole, which is shorter than its diff:
```python
import jax
import jax.numpy as jnp
from jax import lax
from jax.experimental import pallas as pl
from jax.experimental.pallas import tpu as pltpu
from jax.sharding import PartitionSpec as P

F = jnp.float32
T = 64
R = 4
NB = T // R
INNER = 7
DEPTH = INNER
LANES = 128
HALVES = 2
PR, PC = T + 2, T + 16
PLANE = PR * PC
CW = 32
CR = NB + 2 * DEPTH
QX = 2 * DEPTH * NB + 2 * T + 16
QY = 2 * DEPTH * CW + CW + 2 * T + 8
QX_U2, QX_D, QX_S = 2 * DEPTH * NB, 2 * DEPTH * NB + T, 2 * DEPTH * NB + 2 * T
QY_M, QY_S = DEPTH * CW, 2 * DEPTH * CW
QY_U2, QY_D, QY_DIAG = QY_S + CW, QY_S + CW + T, QY_S + CW + 2 * T
MIB = 2**20


def at(refs, *names):
    return [refs[n] for n in names]


def rows(start, size, stride=1):
    return pl.ds(start, size, stride=stride)


def mid():
    return pl.ds(8, T)


def left():
    return pl.ds(7, T)


def right():
    return pl.ds(9, T)


def around(ref, h, y):
    return (ref[h, y, mid(), :] + ref[h, y + 2, mid(), :]) + (
        ref[h, y + 1, left(), :] + ref[h, y + 1, right(), :]
    )


def each_row(body, n=T, unroll=2):
    for h in range(HALVES):
        lax.fori_loop(0, n, lambda y, c, h=h: (body(h, y), c)[1], 0, unroll=unroll)


def clear_border(ref):
    for h in range(HALVES):
        ref[h, 0] = jnp.zeros((PC, LANES), F)
        ref[h, PR - 1] = jnp.zeros((PC, LANES), F)
        for x in (0, PC - 8):
            ref[h, pl.ds(1, T), pl.ds(x, 8), :] = jnp.zeros((T, 8, LANES), F)


def column(ref2, h, x):
    return rows(h * PLANE + PC + 8 + x, T, PC)


def block_sums(part, out):
    n = HALVES * NB * NB

    def body(j, c):
        total = part[rows(j * 4 * T, T, R), :]
        for k in range(1, R):
            total = total + part[rows(j * 4 * T + k, T, R), :]
        out[pl.ds(j * T, T), :] = total * (1.0 / R)
        return c

    lax.fori_loop(0, n // T, body, 0)


def first_kernel(load_h, u_h, m_h, pxl, pxh, pyl, pyh, u1p, b, ld, m, mo, up, part, sems):
    copies = []
    for h in range(HALVES):
        lanes = pl.ds(h * LANES, LANES)
        copies.append(pltpu.make_async_copy(m_h.at[:, :, lanes], m.at[h], sems.at[0, h]))
        copies.append(
            pltpu.make_async_copy(u_h.at[:, :, lanes], up.at[h, pl.ds(1, T), pl.ds(8, T), :], sems.at[1, h])
        )
        copies.append(pltpu.make_async_copy(load_h.at[:, :, lanes], ld.at[h], sems.at[2, h]))
    for c in copies:
        c.start()
    clear_border(up)
    for c in copies:
        c.wait()

    def sweep(h, y):
        bb = 0.8 / (4.0 + m[h, y])
        b[h, y] = bb
        u1p[h, y + 1, mid(), :] = 0.2 * up[h, y + 1, mid(), :] + bb * (ld[h, y] + around(up, h, y))

    each_row(sweep)

    def sums(h, y):
        part[pl.ds(pl.multiple_of((h * NB + y) * T, T), T), :] = (m[h, R * y] + m[h, R * y + 1]) + (
            m[h, R * y + 2] + m[h, R * y + 3]
        )

    each_row(sums, NB)
    block_sums(part, mo)

    up2, u1p2, b2 = up.reshape(HALVES * PLANE, LANES), u1p.reshape(HALVES * PLANE, LANES), b.reshape(
        HALVES * T * T, LANES
    )
    for h in range(HALVES):
        for x, p in ((0, pxl), (T - 1, pxh)):
            p[h, pl.ds(0, T), :] = up2[column(up2, h, x), :]
            p[h, pl.ds(T, T), :] = u1p2[column(u1p2, h, x), :]
            p[h, pl.ds(2 * T, T), :] = b2[rows(h * T * T + x, T, T), :]
        for y, p in ((0, pyl), (T - 1, pyh)):
            p[h, pl.ds(0, T), :] = up[h, y + 1, mid(), :]
            p[h, pl.ds(T, T), :] = u1p[h, y + 1, mid(), :]
            p[h, pl.ds(2 * T, T), :] = b[h, y]


def second_kernel(u1p_in, b, ld, m, mo, pxl, pxh, pyl, pyh, hxl, hxh, hyl, hyh, u1p, u2p, lp, qxl, qxh, part):
    del u1p_in
    u1p2 = u1p.reshape(HALVES * PLANE, LANES)
    U, A, B = pl.ds(0, T), pl.ds(T, T), pl.ds(2 * T, T)
    clear_border(u2p)
    for h in range(HALVES):
        for x, p, g in ((0, pxl, hxl), (T - 1, pxh, hxh)):
            inner = column(u1p2, h, x)
            outer = column(u1p2, h, -1 if x == 0 else T)
            u1p2[inner, :] = u1p2[inner, :] + p[h, B, :] * g[h, U, :]
            u1p2[outer, :] = g[h, A, :] + g[h, B, :] * p[h, U, :]
        for y, p, g in ((0, pyl, hyl), (T - 1, pyh, hyh)):
            u1p[h, y + 1, mid(), :] = u1p[h, y + 1, mid(), :] + p[h, B, :] * g[h, U, :]
            u1p[h, 0 if y == 0 else T + 1, mid(), :] = g[h, A, :] + g[h, B, :] * p[h, U, :]

    def sweep(h, y):
        u2p[h, y + 1, mid(), :] = 0.2 * u1p[h, y + 1, mid(), :] + b[h, y] * (ld[h, y] + around(u1p, h, y))

    each_row(sweep)

    def sums(h, y):
        total = None
        for k in range(R):
            c = R * y + k
            d = (ld[h, c] + around(u2p, h, c)) - (4.0 + m[h, c]) * u2p[h, c + 1, mid(), :]
            total = d if total is None else total + d
        part[pl.ds(pl.multiple_of((h * NB + y) * T, T), T), :] = total

    each_row(sums, NB, unroll=1)
    block_sums(part, lp)

    u2p2, ld2 = u2p.reshape(HALVES * PLANE, LANES), ld.reshape(HALVES * T * T, LANES)
    for h in range(HALVES):
        for x, first, s, q in ((0, 0, 0, qxl), (T - 1, NB - DEPTH, 8, qxh)):
            for k in range(DEPTH):
                q[h, pl.ds(k * NB, NB), :] = lp[rows(h * NB * NB + first + k, NB, NB), :]
                q[h, pl.ds((DEPTH + k) * NB, NB), :] = mo[rows(h * NB * NB + first + k, NB, NB), :]
            q[h, pl.ds(QX_U2, T), :] = u2p2[column(u2p2, h, x), :]
            q[h, pl.ds(QX_D, T), :] = (
                ld2[rows(h * T * T + x, T, T), :] + u2p2[column(u2p2, h, 1 if x == 0 else T - 2), :]
            )
            for i, y in enumerate((0, T - 1)):
                total = None
                for k in range(R):
                    v = u2p2[rows(h * PLANE + (y + 1) * PC + 8 + R * s + k, 8, R), :]
                    total = v if total is None else total + v
                q[h, pl.ds(QX_S + 8 * i, 8), :] = total


def third_kernel(lp, mo, u2p, ld, qxl, qxh, gxl, gxh, hxl, hxh, lx, mx, s0, s1, qyl, qyh):
    lx2, mx2 = lx.reshape(HALVES * NB * CW, LANES), mx.reshape(HALVES * NB * CW, LANES)
    flat = lambda r: r.reshape(HALVES * QX, LANES)
    qxl2, qxh2, gxl2, gxh2 = flat(qxl), flat(qxh), flat(gxl), flat(gxh)

    def quarter(ref, h):
        total = ref[rows(h * QX + QX_U2, NB, R), :]
        for k in range(1, R):
            total = total + ref[rows(h * QX + QX_U2 + k, NB, R), :]
        return total * (1.0 / R)

    for h in range(HALVES):
        col = lambda c: rows(h * NB * CW + c, NB, CW)
        for y in range(NB):
            lx[h, y, pl.ds(8, NB), :] = lp[pl.ds(h * NB * NB + y * NB, NB), :]
            mx[h, y, pl.ds(8, NB), :] = mo[pl.ds(h * NB * NB + y * NB, NB), :]
        for c in (0, CW - 1):
            lx2[col(c), :] = jnp.zeros((NB, LANES), F)
            mx2[col(c), :] = jnp.zeros((NB, LANES), F)
        for c, g in ((1, gxl), (8 + NB, gxh)):
            for k in range(DEPTH):
                lx2[col(c + k), :] = g[h, pl.ds(k * NB, NB), :]
                mx2[col(c + k), :] = g[h, pl.ds((DEPTH + k) * NB, NB), :]
        for c, ref in ((8, gxl2), (7, qxl2), (7 + NB, gxh2), (8 + NB, qxh2)):
            lx2[col(c), :] = lx2[col(c), :] + quarter(ref, h)
        for i, s in enumerate((s0, s1)):
            for c, ref in ((0, gxl), (8, qxl), (16, qxh), (24, gxh)):
                s[h, pl.ds(c, 8), :] = ref[h, pl.ds(QX_S + 8 * i, 8), :]
        for y, first, inside, s, q in ((0, 0, 1, s0, qyl), (T - 1, NB - DEPTH, T - 2, s1, qyh)):
            for k in range(DEPTH):
                q[h, pl.ds(k * CW, CW), :] = lx[h, first + k]
                q[h, pl.ds(QY_M + k * CW, CW), :] = mx[h, first + k]
            q[h, pl.ds(QY_S, CW), :] = s[h]
            q[h, pl.ds(QY_U2, T), :] = u2p[h, y + 1, mid(), :]
            q[h, pl.ds(QY_D, T), :] = ld[h, y] + u2p[h, inside + 1, mid(), :]
            for j, (g1, g2) in enumerate(((hxl, gxl), (hxh, gxh))):
                q[h, pl.ds(QY_DIAG + 3 * j, 1), :] = g1[h, pl.ds(y, 1), :]
                q[h, pl.ds(QY_DIAG + 3 * j + 1, 1), :] = g1[h, pl.ds(2 * T + y, 1), :]
                q[h, pl.ds(QY_DIAG + 3 * j + 2, 1), :] = g2[h, pl.ds(QX_U2 + y, 1), :]
            q[h, pl.ds(QY_DIAG + 6, 2), :] = jnp.zeros((2, LANES), F)


def last_kernel(
    lx, mx, s0, s1, gyl, gyh, gxl, gxh, hxl, hxh, hyl, hyh, pxl, pxh, u2p, b, ld,
    out, lg, bc, ca, cb, sp, w0, w1, wh, sh, sems,
):
    one = lambda r: pl.ds(r, 1)
    for h in range(HALVES):
        for k in range(DEPTH):
            for base, g in ((0, gyl), (DEPTH + NB, gyh)):
                lg[h, base + k] = g[h, pl.ds(k * CW, CW), :]
                bc[h, base + k] = 0.8 / (4.0 + g[h, pl.ds(QY_M + k * CW, CW), :])
        for y in range(NB):
            lg[h, DEPTH + y] = lx[h, y]
            bc[h, DEPTH + y] = 0.8 / (4.0 + mx[h, y])
        quarter = 1.0 / R
        for r, v in (
            (DEPTH - 1, s0[h]),
            (DEPTH, gyl[h, pl.ds(QY_S, CW), :]),
            (DEPTH + NB - 1, gyh[h, pl.ds(QY_S, CW), :]),
            (DEPTH + NB, s1[h]),
        ):
            lg[h, r] = lg[h, r] + quarter * v

    bumps = {}
    for h in range(HALVES):
        for j, (px, hx) in enumerate(((pxl, hxl), (pxh, hxh))):
            for i, (hy, gy) in enumerate(((hyl, gyl), (hyh, gyh))):
                y, x = (0, T - 1)[i], (0, T - 1)[j]
                ua, ba = px[h, one(y), :], px[h, one(2 * T + y), :]
                ux, bx = hx[h, one(y), :], hx[h, one(2 * T + y), :]
                uy, by = hy[h, one(x), :], hy[h, one(2 * T + x), :]
                ud, bd = gy[h, one(QY_DIAG + 3 * j), :], gy[h, one(QY_DIAG + 3 * j + 1), :]
                ea, ed = ba * (bx + by) * ud, bd * (bx + by) * ua
                ex, ey = bx * (ba + bd) * uy, by * (ba + bd) * ux
                ya, yo = (DEPTH, DEPTH - 1) if i == 0 else (DEPTH + NB - 1, DEPTH + NB)
                xa, xo = (8, 7) if j == 0 else (7 + NB, 8 + NB)
                for yy, xx, e, bb, e1, e2 in (
                    (ya, xa, ea, ba, ex, ey),
                    (ya, xo, ex, bx, ea, ed),
                    (yo, xa, ey, by, ea, ed),
                    (yo, xo, ed, bd, ex, ey),
                ):
                    lg[h, yy, one(xx), :] = lg[h, yy, one(xx), :] + quarter * (
                        (2.0 - 0.8 / bb) * e + (e1 + e2)
                    )
                bumps[h, i, j] = (ea, ex, ey, ed + gy[h, one(QY_DIAG + 3 * j + 2), :])

    def start(h, y):
        v = bc[h, y] * lg[h, y]
        lg[h, y] = v
        ca[h, y] = v

    each_row(start, CR)
    old, new = ca, cb
    for s in range(1, INNER):

        def inner(h, i, old=old, new=new, s=s):
            y = i + s
            c = old[h, y]
            around_c = (old[h, y - 1] + old[h, y + 1]) + (pltpu.roll(c, 1, 0) + pltpu.roll(c, CW - 1, 0))
            new[h, y] = (0.2 * c + lg[h, y]) + bc[h, y] * around_c

        each_row(inner, CR - 2 * s)
        old, new = new, old
    cv = old
    cv2 = cv.reshape(HALVES * CR * CW, LANES)

    def correct(h, y):
        base = pl.multiple_of((h * NB + y) * T, T)
        c = cv[h, y + DEPTH, pl.ds(8, NB), :]
        for k in range(R):
            sp[rows(base + k, NB, R), :] = c
        add = sp[pl.ds(base, T), :]
        for k in range(R):
            w0[h, R * y + k + 1, mid(), :] = u2p[h, R * y + k + 1, mid(), :] + add

    each_row(correct, NB)

    w02, w12 = w0.reshape(HALVES * PLANE, LANES), w1.reshape(HALVES * PLANE, LANES)
    for h in range(HALVES):
        for i in range(2):
            for j in range(2):
                r, x = (1, T)[i], (8, T + 7)[j]
                w0[h, r, one(x), :] = w0[h, r, one(x), :] + bumps[h, i, j][0]
    U2X, DX, U2Y, DY, BH = pl.ds(QX_U2, T), pl.ds(QX_D, T), pl.ds(QY_U2, T), pl.ds(QY_D, T), pl.ds(2 * T, T)
    n = 0
    for h in range(HALVES):
        diag = {}
        for i in range(2):
            for j in range(2):
                diag[i, j] = (
                    bumps[h, i, j][3] + cv[h, (DEPTH - 1, DEPTH + NB)[i], one((7, 8 + NB)[j]), :]
                )
        for j, (g, hx) in enumerate(((gxl, hxl), (gxh, hxh))):
            c = cv2[rows(h * CR * CW + DEPTH * CW + (7, 8 + NB)[j], NB, CW), :]
            for k in range(R):
                sh[n, rows(k, NB, R), :] = c
            add = sh[n]
            wh[n, mid(), :] = g[h, U2X, :] + add
            wh[n, one(7), :], wh[n, one(8 + T), :] = diag[0, j], diag[1, j]
            wh[n, one(8), :] = wh[n, one(8), :] + bumps[h, 0, j][1]
            wh[n, one(7 + T), :] = wh[n, one(7 + T), :] + bumps[h, 1, j][1]
            v = wh[n, mid(), :]
            x = (-1, T)[j]
            w02[column(w02, h, x), :] = v
            w12[column(w12, h, x), :] = 0.2 * v + hx[h, BH, :] * (
                (g[h, DX, :] + add)
                + (wh[n, left(), :] + wh[n, right(), :])
                + w02[column(w02, h, (0, T - 1)[j]), :]
            )
            n += 1
        for i, (g, hy) in enumerate(((gyl, hyl), (gyh, hyh))):
            c = cv[h, (DEPTH - 1, DEPTH + NB)[i], pl.ds(8, NB), :]
            for k in range(R):
                sh[n, rows(k, NB, R), :] = c
            add = sh[n]
            wh[n, mid(), :] = g[h, U2Y, :] + add
            wh[n, one(7), :], wh[n, one(8 + T), :] = diag[i, 0], diag[i, 1]
            wh[n, one(8), :] = wh[n, one(8), :] + bumps[h, i, 0][2]
            wh[n, one(7 + T), :] = wh[n, one(7 + T), :] + bumps[h, i, 1][2]
            v = wh[n, mid(), :]
            r = (0, T + 1)[i]
            w0[h, r, mid(), :] = v
            w1[h, r, mid(), :] = 0.2 * v + hy[h, BH, :] * (
                (g[h, DY, :] + add)
                + (wh[n, left(), :] + wh[n, right(), :])
                + w0[h, (1, T)[i], mid(), :]
            )
            n += 1

    copies = []
    for h in range(HALVES):

        def one_more(y, c, h=h):
            w1[h, y + 1, mid(), :] = 0.2 * w0[h, y + 1, mid(), :] + b[h, y] * (ld[h, y] + around(w0, h, y))
            return c

        def last(y, c, h=h):
            w0[h, y + 1, mid(), :] = 0.2 * w1[h, y + 1, mid(), :] + b[h, y] * (ld[h, y] + around(w1, h, y))
            return c

        lax.fori_loop(0, T, one_more, 0, unroll=2)
        step = T // 4
        for q in range(4):
            lax.fori_loop(q * step, (q + 1) * step, last, 0, unroll=2)
            copies.append(
                pltpu.make_async_copy(
                    w0.at[h, pl.ds(1 + q * step, step), mid(), :],
                    out.at[pl.ds(q * step, step), :, pl.ds(h * LANES, LANES)],
                    sems.at[h, q],
                )
            )
            copies[-1].start()
    for c in copies:
        c.wait()


def vmem(*shape):
    return pltpu.VMEM(shape, F)


V = pl.BlockSpec(memory_space=pltpu.VMEM)
H = pl.BlockSpec(memory_space=pltpu.HBM)


def shifted(value, axis, step):
    size = lax.axis_size(axis)
    return lax.ppermute(value, axis, [(i, (i + step) % size) for i in range(size)])


def per_device(load_terms, start_values, reaction_rate):
    tile, padded = (HALVES, T, T, LANES), (HALVES, PR, PC, LANES)
    coarse = (HALVES * NB * NB, LANES)
    edge = (HALVES, 3 * T, LANES)
    part = vmem(HALVES * NB * T, LANES)
    pxl, pxh, pyl, pyh, u1p, b, ld, m, mo = pl.pallas_call(
        first_kernel,
        in_specs=[H] * 3,
        out_specs=[V] * 9,
        out_shape=[vmem(*edge)] * 4 + [vmem(*padded)] + [vmem(*tile)] * 3 + [vmem(*coarse)],
        scratch_shapes=[vmem(*padded), part, pltpu.SemaphoreType.DMA((3, HALVES))],
        compiler_params=pltpu.CompilerParams(vmem_limit_bytes=12 * MIB),
        name="first",
    )(*(pltpu.with_memory_space_constraint(v, pltpu.HBM) for v in (load_terms, start_values, reaction_rate)))
    hyl, hyh = shifted(pyh, "py", 1), shifted(pyl, "py", -1)
    hxl, hxh = shifted(pxh, "px", 1), shifted(pxl, "px", -1)
    _, u2p, lp, qxl, qxh = pl.pallas_call(
        second_kernel,
        in_specs=[V] * 13,
        out_specs=[V] * 5,
        out_shape=[vmem(*padded)] * 2 + [vmem(*coarse)] + [vmem(HALVES, QX, LANES)] * 2,
        scratch_shapes=[part],
        input_output_aliases={0: 0},
        compiler_params=pltpu.CompilerParams(vmem_limit_bytes=8 * MIB),
        name="second",
    )(u1p, b, ld, m, mo, pxl, pxh, pyl, pyh, hxl, hxh, hyl, hyh)
    gxl, gxh = shifted(qxh, "px", 1), shifted(qxl, "px", -1)
    lx, mx, s0, s1, qyl, qyh = pl.pallas_call(
        third_kernel,
        in_specs=[V] * 10,
        out_specs=[V] * 6,
        out_shape=[vmem(HALVES, NB, CW, LANES)] * 2
        + [vmem(HALVES, CW, LANES)] * 2
        + [vmem(HALVES, QY, LANES)] * 2,
        compiler_params=pltpu.CompilerParams(vmem_limit_bytes=8 * MIB),
        name="third",
    )(lp, mo, u2p, ld, qxl, qxh, gxl, gxh, hxl, hxh)
    gyl, gyh = shifted(qyh, "py", 1), shifted(qyl, "py", -1)
    grid = vmem(HALVES, CR, CW, LANES)
    return pl.pallas_call(
        last_kernel,
        in_specs=[V] * 17,
        out_specs=H,
        out_shape=jax.ShapeDtypeStruct(load_terms.shape, F),
        scratch_shapes=[grid] * 4
        + [part, vmem(*padded), vmem(*padded)]
        + [vmem(8, PC, LANES), vmem(8, T, LANES), pltpu.SemaphoreType.DMA((HALVES, 4))],
        compiler_params=pltpu.CompilerParams(vmem_limit_bytes=20 * MIB),
        name="last",
    )(lx, mx, s0, s1, gyl, gyh, gxl, gxh, hxl, hxh, hyl, hyh, pxl, pxh, u2p, b, ld)


def solution(mesh):
    return jax.shard_map(
        per_device,
        mesh=mesh,
        in_specs=(P("py", "px", None), P("py", "px", None), P("py", "px", None)),
        out_specs=P("py", "px", None),
        check_vma=False,
    )
```

time: 185 us -> 77.4 us (0.42)
  starting transfers between devices: 87.4 us -> 16.7 us
  other arithmetic: 51.7 us -> 0 us
  local copies, waits for them, and re-layouts: 27.8 us -> 0 us
  waiting for transfers between devices: 17.3 us -> 41.6 us
  Pallas kernels: 0 us -> 19 us
    ppermute x36 -> x8, starting transfers between devices: 87.4 us -> 16.7 us  [shifted(): lax.ppermute(value, axis, [(i, (i + step) % size) for i in range(size)])]
    add x11 -> x0, other arithmetic: 30.6 us -> none  [the longest x10 26.2 us: relax_once(): values + 0.8 * (load + around_sum(padded) - (4.0 + mass_here) * values) /...]
    ppermute x36 -> x8, waiting for transfers between devices: 17.3 us -> 41.6 us  [shifted(): lax.ppermute(value, axis, [(i, (i + step) % size) for i in range(size)])]
    pallas_call x0 -> x4, Pallas kernels: none -> 19 us  [the longest x1 7.61 us: per_device(): pl.pallas_call(last_kernel, in_specs=[V] * 17, out_specs=H, out_shape=jax...]
    reshape x3 -> x0, local copies, waits for them, and re-layouts: 15.8 us -> none  [the longest x2 10.4 us: block_means(): values.reshape(values.shape[0] // RATIO, RATIO, values.shape[1] // RATIO,...]
    sub x1 -> x0, other arithmetic: 13.5 us -> none  [per_device(): load_terms + around_sum(extended(values, (('py', 0), ('px', 1)), 1))]
    reduce_sum x2 -> x0, other arithmetic: 7.09 us -> none  [block_means(): return jnp.mean(cut, axis=(1, 3))]
    unnamed x12 -> x0, local copies, waits for them, and re-layouts: 6.58 us -> none
  transfers between devices with their start and end apart: 36 -> 8, of which waited for: 8 -> 6; matrix products, arithmetic and copies ran while one was open for 7% -> 0% of each run, Pallas kernels for 0% -> 0%
where the time goes in v1:
time: 77.4 us; the launch traced here: 77.3 us
  waiting for transfers between devices  41.6 us (54%)
  Pallas kernels  19 us (25%)
  starting transfers between devices  16.7 us (22%)
    ppermute x8, waiting for transfers between devices, shifted(): lax.ppermute(value, axis, [(i, (i + step) % size) for i in range(size)])  41.6 us
    ppermute x8, starting transfers between devices, shifted(): lax.ppermute(value, axis, [(i, (i + step) % size) for i in range(size)])  16.7 us
    pallas_call x1, Pallas kernels, per_device(): pl.pallas_call(last_kernel, in_specs=[V] * 17, out_specs=H, out_shape=jax...  7.61 us
    pallas_call x1, Pallas kernels, per_device(): pl.pallas_call(first_kernel, in_specs=[H] * 3, out_specs=[V] * 9, out_sha...  7.1 us
    pallas_call x1, Pallas kernels, per_device(): pl.pallas_call(second_kernel, in_specs=[V] * 13, out_specs=[V] * 5, out_s...  3.57 us
  transfers between devices with their start and end apart: 8, of which 6 were waited for; matrix products, arithmetic and copies ran while one was open for 0% of the time, Pallas kernels for 0%

profile of v1, /device:TPU:0, one launch (start us, length us, event | category | flops | bytes accessed | tf_op | source)
XLA Modules:
  0.0 77.3 jit_solution(10710401826998250976)
XLA Ops:
  0.0 7.1 %first.1 = (f32[2,192,128]{2,1,0:T(8,128)S(1)}, f32[2,192,128]{2,1,0:T(8,128)S(1)}, f32[2,192,128]{2,1,0:T(8,128)S(1)}, f32[2,192,128]{2,1,0:T(8,128)S(1)}, f32[...) custom-call(f32[64,64,256]{2,1,0:T(8,128)} %load_h.1, ...), custom_call_target="tpu_custom_call" | custom-call | tf_op jit(solution)/shard_map/first/pallas_call | solution.py:393
  7.1 5.1 %collective-permute-start.3 = (f32[2,192,128]{2,1,0:T(8,128)S(1)}, f32[2,192,128]{2,1,0:T(8,128)S(1)}, u32[]{:S(2)}, u32[]{:S(2)}) collective-permute-start(f32[2,192,128]{2,1,0:T(8,128)S(1)} %get-tuple-element.31.pyl), channel_id=1, source_target_pairs={{0,120},{8,0},{16,8},{24,16},{32,24},{40,32},{48,40},{56,48},{64,5... | collective-permute-start | bytes 589832 | tf_op jit(solution)/shard_map/ppermute | solution.py:385
  12.2 0.0 collective-permute-start.2
  12.2 4.1 %collective-permute-start.1 = (f32[2,192,128]{2,1,0:T(8,128)S(1)}, f32[2,192,128]{2,1,0:T(8,128)S(1)}, u32[]{:S(2)}, u32[]{:S(2)}) collective-permute-start(f32[2,192,128]{2,1,0:T(8,128)S(1)} %get-tuple-element.29.pxl), channel_id=1, source_target_pairs={{0,7},{1,0},{2,1},{3,2},{4,3},{5,4},{6,5},{7,6},{8,15},{9,8},{10,9... | collective-permute-start | bytes 589832 | tf_op jit(solution)/shard_map/ppermute | solution.py:385
  16.3 0.0 collective-permute-start
  16.3 0.0 collective-permute-done.3.hyh
  16.3 5.7 %collective-permute-done.2.hyl = f32[2,192,128]{2,1,0:T(8,128)S(1)} collective-permute-done((f32[2,192,128]{2,1,0:T(8,128)S(1)}, f32[2,192,128]{2,1,0:T(8,128)S(1)}, u32[]{:S(2)}, u32[]{:S(2)}) %collective-permute-start.2) | collective-permute-done | bytes 196640 | tf_op jit(solution)/shard_map/ppermute | solution.py:385
  22.0 0.8 collective-permute-done.1.hxh
  22.8 6.1 %collective-permute-done.hxl = f32[2,192,128]{2,1,0:T(8,128)S(1)} collective-permute-done((f32[2,192,128]{2,1,0:T(8,128)S(1)}, f32[2,192,128]{2,1,0:T(8,128)S(1)}, u32[]{:S(2)}, u32[]{:S(2)}) %collective-permute-start) | collective-permute-done | bytes 196640 | tf_op jit(solution)/shard_map/ppermute | solution.py:385
  28.8 3.6 %second.1 = (f32[2,66,80,128]{3,2,1,0:T(8,128)S(1)}, f32[2,66,80,128]{3,2,1,0:T(8,128)S(1)}, f32[512,128]{1,0:T(8,128)S(1)}, f32[2,368,128]{2,1,0:T(8,128)S(1)}, f32[2,368,128]{2,1,0:T(8,128)S(1)}) custom-call(f32[2,66,80,128]{3,2,1,0:T(8,128)S(1)} %get-tuple-element.24.u1p_in, ...), custom_call_target="tpu_custom_call", output_to_operand_aliasing={{0}: (0, {})} | custom-call | tf_op jit(solution)/shard_map/second/pallas_call | solution.py:404
  32.4 0.7 collective-permute-start.5
  33.1 1.4 %collective-permute-start.4 = (f32[2,368,128]{2,1,0:T(8,128)S(1)}, f32[2,368,128]{2,1,0:T(8,128)S(1)}, u32[]{:S(2)}, u32[]{:S(2)}) collective-permute-start(f32[2,368,128]{2,1,0:T(8,128)S(1)} %get-tuple-element.36.qxh), channel_id=1, source_target_pairs={{0,1},{1,2},{2,3},{3,4},{4,5},{5,6},{6,7},{7,0},{8,9},{9,10},{10,1... | collective-permute-start | bytes 1130504 | tf_op jit(solution)/shard_map/ppermute | solution.py:385
  34.5 9.6 %collective-permute-done.5.gxh = f32[2,368,128]{2,1,0:T(8,128)S(1)} collective-permute-done((f32[2,368,128]{2,1,0:T(8,128)S(1)}, f32[2,368,128]{2,1,0:T(8,128)S(1)}, u32[]{:S(2)}, u32[]{:S(2)}) %collective-permute-start.5) | collective-permute-done | bytes 376864 | tf_op jit(solution)/shard_map/ppermute | solution.py:385
  44.1 5.4 %collective-permute-done.4.gxl = f32[2,368,128]{2,1,0:T(8,128)S(1)} collective-permute-done((f32[2,368,128]{2,1,0:T(8,128)S(1)}, f32[2,368,128]{2,1,0:T(8,128)S(1)}, u32[]{:S(2)}, u32[]{:S(2)}) %collective-permute-start.4) | collective-permute-done | bytes 376864 | tf_op jit(solution)/shard_map/ppermute | solution.py:385
  49.5 0.7 third.1
  50.3 0.1 collective-permute-start.6
  50.4 5.3 %collective-permute-start.7 = (f32[2,616,128]{2,1,0:T(8,128)S(1)}, f32[2,616,128]{2,1,0:T(8,128)S(1)}, u32[]{:S(2)}, u32[]{:S(2)}) collective-permute-start(f32[2,616,128]{2,1,0:T(8,128)S(1)} %get-tuple-element.42), channel_id=1, source_target_pairs={{0,120},{8,0},{16,8},{24,16},{32,24},{40,32},{48,40},{56,48},{64,5... | collective-permute-start | bytes 1892360 | tf_op jit(solution)/shard_map/ppermute | solution.py:385
  55.7 14.0 %collective-permute-done.6.gyl = f32[2,616,128]{2,1,0:T(8,128)S(1)} collective-permute-done((f32[2,616,128]{2,1,0:T(8,128)S(1)}, f32[2,616,128]{2,1,0:T(8,128)S(1)}, u32[]{:S(2)}, u32[]{:S(2)}) %collective-permute-start.6) | collective-permute-done | bytes 630816 | tf_op jit(solution)/shard_map/ppermute | solution.py:385
  69.7 0.0 collective-permute-done.7.gyh
  69.7 7.6 %last.1 = f32[64,64,256]{2,1,0:T(8,128)} custom-call(f32[2,16,32,128]{3,2,1,0:T(8,128)S(1)} %get-tuple-element.37.lx, f32[2,16,32,128]{3,2,1,0:T(8,128)S(1)} %get-tuple-element.38.mx, f32[2,32,128]{2,1,0:T(8,128)S(1)} %get-tuple-element.39.s0, f32[2,32,128]{2,1,0:T(8,128)S(1)} %get-tuple-element.40.s1, f32[2,616,128]{2,1,0:T(8,128)S(1)} %collective-permute-done.6.gyl, ...), custom_call_target="tpu_custom_call" | custom-call | tf_op jit(solution)/shard_map/last/pallas_call | solution.py:427
Async XLA Ops:
  7.1 9.2 %collective-permute-start.3 = (f32[2,192,128]{2,1,0:T(8,128)S(1)}, f32[2,192,128]{2,1,0:T(8,128)S(1)}, u32[]{:S(2)}, u32[]{:S(2)}) collective-permute-start(f32[2,192,128]{2,1,0:T(8,128)S(1)} %get-tuple-element.31.pyl), channel_id=1, source_target_pairs={{0,120},{8,0},{16,8},{24,16},{32,24},{40,32},{48,40},{56,48},{64,5... | collective-permute-start | bytes 589832 | tf_op jit(solution)/shard_map/ppermute | solution.py:385
  12.2 9.8 %collective-permute-start.2 = (f32[2,192,128]{2,1,0:T(8,128)S(1)}, f32[2,192,128]{2,1,0:T(8,128)S(1)}, u32[]{:S(2)}, u32[]{:S(2)}) collective-permute-start(f32[2,192,128]{2,1,0:T(8,128)S(1)} %get-tuple-element.32.pyh), channel_id=1, source_target_pairs={{0,8},{8,16},{16,24},{24,32},{32,40},{40,48},{48,56},{56,64},{64,7... | collective-permute-start | bytes 589832 | tf_op jit(solution)/shard_map/ppermute | solution.py:385
  12.2 10.6 %collective-permute-start.1 = (f32[2,192,128]{2,1,0:T(8,128)S(1)}, f32[2,192,128]{2,1,0:T(8,128)S(1)}, u32[]{:S(2)}, u32[]{:S(2)}) collective-permute-start(f32[2,192,128]{2,1,0:T(8,128)S(1)} %get-tuple-element.29.pxl), channel_id=1, source_target_pairs={{0,7},{1,0},{2,1},{3,2},{4,3},{5,4},{6,5},{7,6},{8,15},{9,8},{10,9... | collective-permute-start | bytes 589832 | tf_op jit(solution)/shard_map/ppermute | solution.py:385
  16.3 12.6 %collective-permute-start = (f32[2,192,128]{2,1,0:T(8,128)S(1)}, f32[2,192,128]{2,1,0:T(8,128)S(1)}, u32[]{:S(2)}, u32[]{:S(2)}) collective-permute-start(f32[2,192,128]{2,1,0:T(8,128)S(1)} %get-tuple-element.30.pxh), channel_id=1, source_target_pairs={{0,1},{1,2},{2,3},{3,4},{4,5},{5,6},{6,7},{7,0},{8,9},{9,10},{10,1... | collective-permute-start | bytes 589832 | tf_op jit(solution)/shard_map/ppermute | solution.py:385
  32.4 11.7 %collective-permute-start.5 = (f32[2,368,128]{2,1,0:T(8,128)S(1)}, f32[2,368,128]{2,1,0:T(8,128)S(1)}, u32[]{:S(2)}, u32[]{:S(2)}) collective-permute-start(f32[2,368,128]{2,1,0:T(8,128)S(1)} %get-tuple-element.35.qxl), channel_id=1, source_target_pairs={{0,7},{1,0},{2,1},{3,2},{4,3},{5,4},{6,5},{7,6},{8,15},{9,8},{10,9... | collective-permute-start | bytes 1130504 | tf_op jit(solution)/shard_map/ppermute | solution.py:385
  33.1 16.4 %collective-permute-start.4 = (f32[2,368,128]{2,1,0:T(8,128)S(1)}, f32[2,368,128]{2,1,0:T(8,128)S(1)}, u32[]{:S(2)}, u32[]{:S(2)}) collective-permute-start(f32[2,368,128]{2,1,0:T(8,128)S(1)} %get-tuple-element.36.qxh), channel_id=1, source_target_pairs={{0,1},{1,2},{2,3},{3,4},{4,5},{5,6},{6,7},{7,0},{8,9},{9,10},{10,1... | collective-permute-start | bytes 1130504 | tf_op jit(solution)/shard_map/ppermute | solution.py:385
  50.3 19.4 %collective-permute-start.6 = (f32[2,616,128]{2,1,0:T(8,128)S(1)}, f32[2,616,128]{2,1,0:T(8,128)S(1)}, u32[]{:S(2)}, u32[]{:S(2)}) collective-permute-start(f32[2,616,128]{2,1,0:T(8,128)S(1)} %get-tuple-element.41), channel_id=1, source_target_pairs={{0,8},{8,16},{16,24},{24,32},{32,40},{40,48},{48,56},{56,64},{64,7... | collective-permute-start | bytes 1892360 | tf_op jit(solution)/shard_map/ppermute | solution.py:385
  50.4 19.3 %collective-permute-start.7 = (f32[2,616,128]{2,1,0:T(8,128)S(1)}, f32[2,616,128]{2,1,0:T(8,128)S(1)}, u32[]{:S(2)}, u32[]{:S(2)}) collective-permute-start(f32[2,616,128]{2,1,0:T(8,128)S(1)} %get-tuple-element.42), channel_id=1, source_target_pairs={{0,120},{8,0},{16,8},{24,16},{32,24},{40,32},{48,40},{56,48},{64,5... | collective-permute-start | bytes 1892360 | tf_op jit(solution)/shard_map/ppermute | solution.py:385

commit v2 on v1

--- a/solution.py
+++ b/solution.py
@@ -17,16 +17,14 @@
 PLANE = PR * PC
 CW = 32
 CR = NB + 2 * DEPTH
-QX = 2 * DEPTH * NB + 2 * T + 16
-QY = 2 * DEPTH * CW + CW + 2 * T + 8
-QX_U2, QX_D, QX_S = 2 * DEPTH * NB, 2 * DEPTH * NB + T, 2 * DEPTH * NB + 2 * T
-QY_M, QY_S = DEPTH * CW, 2 * DEPTH * CW
+KX = DEPTH * NB
+KY = sum(CW - 2 * i for i in range(1, DEPTH + 1))
+QX_U2, QX_D, QX_S = KX, KX + T, KX + 2 * T
+QX = QX_S + 16
+QY_S = KY
 QY_U2, QY_D, QY_DIAG = QY_S + CW, QY_S + CW + T, QY_S + CW + 2 * T
+QY = QY_DIAG + 8
 MIB = 2**20
-
-
-def at(refs, *names):
-    return [refs[n] for n in names]
 
 
 def rows(start, size, stride=1):
@@ -64,7 +62,7 @@
             ref[h, pl.ds(1, T), pl.ds(x, 8), :] = jnp.zeros((T, 8, LANES), F)
 
 
-def column(ref2, h, x):
+def column(h, x):
     return rows(h * PLANE + PC + 8 + x, T, PC)
 
 
@@ -81,59 +79,137 @@
     lax.fori_loop(0, n // T, body, 0)
 
 
-def first_kernel(load_h, u_h, m_h, pxl, pxh, pyl, pyh, u1p, b, ld, m, mo, up, part, sems):
+def edge_kernel(load_h, u_h, m_h, pxl, pxh, pyl, pyh, uc, lc, mc, ur, lr, mr, sems):
     copies = []
     for h in range(HALVES):
         lanes = pl.ds(h * LANES, LANES)
-        copies.append(pltpu.make_async_copy(m_h.at[:, :, lanes], m.at[h], sems.at[0, h]))
-        copies.append(
-            pltpu.make_async_copy(u_h.at[:, :, lanes], up.at[h, pl.ds(1, T), pl.ds(8, T), :], sems.at[1, h])
-        )
-        copies.append(pltpu.make_async_copy(load_h.at[:, :, lanes], ld.at[h], sems.at[2, h]))
+        for i in range(2):
+            x, y, yy = (0, T - 8)[i], (0, T - 1)[i], (0, T - 2)[i]
+            for src, dst, n in (
+                (u_h.at[:, pl.ds(x, 8), lanes], uc.at[h, i, pl.ds(1, T)], 0),
+                (load_h.at[:, pl.ds(x, 8), lanes], lc.at[h, i], 1),
+                (m_h.at[:, pl.ds(x, 8), lanes], mc.at[h, i], 2),
+                (u_h.at[pl.ds(yy, 2), :, lanes], ur.at[h, i, :, mid(), :], 3),
+                (load_h.at[pl.ds(y, 1), :, lanes], lr.at[h, i], 4),
+                (m_h.at[pl.ds(y, 1), :, lanes], mr.at[h, i], 5),
+            ):
+                copies.append(pltpu.make_async_copy(src, dst, sems.at[h, i, n]))
     for c in copies:
         c.start()
-    clear_border(up)
+    for h in range(HALVES):
+        for i in range(2):
+            uc[h, i, 0] = jnp.zeros((8, LANES), F)
+            uc[h, i, T + 1] = jnp.zeros((8, LANES), F)
+            for k in range(2):
+                ur[h, i, k, pl.ds(0, 8), :] = jnp.zeros((8, LANES), F)
+                ur[h, i, k, pl.ds(8 + T, 8), :] = jnp.zeros((8, LANES), F)
     for c in copies:
         c.wait()
-
-    def sweep(h, y):
-        bb = 0.8 / (4.0 + m[h, y])
-        b[h, y] = bb
-        u1p[h, y + 1, mid(), :] = 0.2 * up[h, y + 1, mid(), :] + bb * (ld[h, y] + around(up, h, y))
-
-    each_row(sweep)
-
-    def sums(h, y):
-        part[pl.ds(pl.multiple_of((h * NB + y) * T, T), T), :] = (m[h, R * y] + m[h, R * y + 1]) + (
-            m[h, R * y + 2] + m[h, R * y + 3]
-        )
-
-    each_row(sums, NB)
+    uc2 = uc.reshape(HALVES * 2 * (T + 2) * 8, LANES)
+    lc2, mc2 = lc.reshape(HALVES * 2 * T * 8, LANES), mc.reshape(HALVES * 2 * T * 8, LANES)
+    for h in range(HALVES):
+        for i in range(2):
+            px, py = (pxl, pxh)[i], (pyl, pyh)[i]
+            ub, lb = (h * 2 + i) * (T + 2) * 8, (h * 2 + i) * T * 8
+            x, xi = (0, 7)[i], (1, 6)[i]
+            u = uc2[rows(ub + 8 + x, T, 8), :]
+            bb = 0.8 / (4.0 + mc2[rows(lb + x, T, 8), :])
+            near = uc2[rows(ub + 8 + xi, T, 8), :] + (uc2[rows(ub + x, T, 8), :] + uc2[rows(ub + 16 + x, T, 8), :])
+            px[h, pl.ds(0, T), :] = u
+            px[h, pl.ds(T, T), :] = 0.2 * u + bb * (lc2[rows(lb + x, T, 8), :] + near)
+            px[h, pl.ds(2 * T, T), :] = bb
+            k = i
+            u = ur[h, i, k, mid(), :]
+            bb = 0.8 / (4.0 + mr[h, i, 0])
+            near = ur[h, i, 1 - k, mid(), :] + (ur[h, i, k, left(), :] + ur[h, i, k, right(), :])
+            py[h, pl.ds(0, T), :] = u
+            py[h, pl.ds(T, T), :] = 0.2 * u + bb * (lr[h, i, 0] + near)
+            py[h, pl.ds(2 * T, T), :] = bb
+
+
+CHUNKS = 4
+
+
+def first_kernel(load_h, u_h, m_h, u1p, b, ld, m, mo, kxl, kxh, up, part, sems):
+    step = T // CHUNKS
+    copies = {}
+    for h in range(HALVES):
+        lanes = pl.ds(h * LANES, LANES)
+        for q in range(CHUNKS):
+            y = pl.ds(q * step, step)
+            copies[h, q] = [
+                pltpu.make_async_copy(m_h.at[y, :, lanes], m.at[h, y], sems.at[0, h, q]),
+                pltpu.make_async_copy(
+                    u_h.at[y, :, lanes], up.at[h, pl.ds(q * step + 1, step), pl.ds(8, T), :], sems.at[1, h, q]
+                ),
+                pltpu.make_async_copy(load_h.at[y, :, lanes], ld.at[h, y], sems.at[2, h, q]),
+            ]
+            for c in copies[h, q]:
+                c.start()
+    clear_border(up)
+
+    for h in range(HALVES):
+
+        def sweep(y, c, h=h):
+            bb = 0.8 / (4.0 + m[h, y])
+            b[h, y] = bb
+            u1p[h, y + 1, mid(), :] = 0.2 * up[h, y + 1, mid(), :] + bb * (ld[h, y] + around(up, h, y))
+            return c
+
+        def sums(y, c, h=h):
+            part[pl.ds(pl.multiple_of((h * NB + y) * T, T), T), :] = (m[h, R * y] + m[h, R * y + 1]) + (
+                m[h, R * y + 2] + m[h, R * y + 3]
+            )
+            return c
+
+        for q in range(CHUNKS):
+            for c in copies[h, q]:
+                c.wait()
+            lax.fori_loop(q * step // R, (q + 1) * step // R, sums, 0, unroll=2)
+            lax.fori_loop(max(q * step - 1, 0), T if q == CHUNKS - 1 else (q + 1) * step - 1, sweep, 0, unroll=2 if q else 1)
     block_sums(part, mo)
-
-    up2, u1p2, b2 = up.reshape(HALVES * PLANE, LANES), u1p.reshape(HALVES * PLANE, LANES), b.reshape(
-        HALVES * T * T, LANES
-    )
-    for h in range(HALVES):
-        for x, p in ((0, pxl), (T - 1, pxh)):
-            p[h, pl.ds(0, T), :] = up2[column(up2, h, x), :]
-            p[h, pl.ds(T, T), :] = u1p2[column(u1p2, h, x), :]
-            p[h, pl.ds(2 * T, T), :] = b2[rows(h * T * T + x, T, T), :]
-        for y, p in ((0, pyl), (T - 1, pyh)):
-            p[h, pl.ds(0, T), :] = up[h, y + 1, mid(), :]
-            p[h, pl.ds(T, T), :] = u1p[h, y + 1, mid(), :]
-            p[h, pl.ds(2 * T, T), :] = b[h, y]
-
-
-def second_kernel(u1p_in, b, ld, m, mo, pxl, pxh, pyl, pyh, hxl, hxh, hyl, hyh, u1p, u2p, lp, qxl, qxh, part):
+    for h in range(HALVES):
+        for first, q in ((0, kxl), (NB - DEPTH, kxh)):
+            for k in range(DEPTH):
+                q[h, pl.ds(k * NB, NB), :] = mo[rows(h * NB * NB + first + k, NB, NB), :]
+
+
+def spread_x(inner, low, high, ext):
+    ext2 = ext.reshape(HALVES * NB * CW, LANES)
+    for h in range(HALVES):
+        for y in range(NB):
+            ext[h, y, pl.ds(8, NB), :] = inner[pl.ds(h * NB * NB + y * NB, NB), :]
+        for c, g in ((1, low), (8 + NB, high)):
+            for k in range(DEPTH):
+                ext2[rows(h * NB * CW + c + k, NB, CW), :] = g[h, pl.ds(k * NB, NB), :]
+
+
+def wedge(i):
+    return i, CW - 2 * i, sum(CW - 2 * k for k in range(1, i))
+
+
+def cut_wedges(ext, h, low, high):
+    for i in range(1, DEPTH + 1):
+        c, n, at = wedge(i)
+        low[h, pl.ds(at, n), :] = ext[h, i - 1, pl.ds(c, n), :]
+        high[h, pl.ds(at, n), :] = ext[h, NB - i, pl.ds(c, n), :]
+
+
+def mass_kernel(mo, gml, gmh, mx, kyl, kyh):
+    spread_x(mo, gml, gmh, mx)
+    for h in range(HALVES):
+        cut_wedges(mx, h, kyl, kyh)
+
+
+def second_kernel(u1p_in, b, ld, m, pxl, pxh, pyl, pyh, hxl, hxh, hyl, hyh, u1p, u2p, lp, qxl, qxh, part):
     del u1p_in
     u1p2 = u1p.reshape(HALVES * PLANE, LANES)
     U, A, B = pl.ds(0, T), pl.ds(T, T), pl.ds(2 * T, T)
     clear_border(u2p)
     for h in range(HALVES):
         for x, p, g in ((0, pxl, hxl), (T - 1, pxh, hxh)):
-            inner = column(u1p2, h, x)
-            outer = column(u1p2, h, -1 if x == 0 else T)
+            inner = column(h, x)
+            outer = column(h, -1 if x == 0 else T)
             u1p2[inner, :] = u1p2[inner, :] + p[h, B, :] * g[h, U, :]
             u1p2[outer, :] = g[h, A, :] + g[h, B, :] * p[h, U, :]
         for y, p, g in ((0, pyl, hyl), (T - 1, pyh, hyh)):
@@ -161,11 +237,8 @@
         for x, first, s, q in ((0, 0, 0, qxl), (T - 1, NB - DEPTH, 8, qxh)):
             for k in range(DEPTH):
                 q[h, pl.ds(k * NB, NB), :] = lp[rows(h * NB * NB + first + k, NB, NB), :]
-                q[h, pl.ds((DEPTH + k) * NB, NB), :] = mo[rows(h * NB * NB + first + k, NB, NB), :]
-            q[h, pl.ds(QX_U2, T), :] = u2p2[column(u2p2, h, x), :]
-            q[h, pl.ds(QX_D, T), :] = (
-                ld2[rows(h * T * T + x, T, T), :] + u2p2[column(u2p2, h, 1 if x == 0 else T - 2), :]
-            )
+            q[h, pl.ds(QX_U2, T), :] = u2p2[column(h, x), :]
+            q[h, pl.ds(QX_D, T), :] = ld2[rows(h * T * T + x, T, T), :] + u2p2[column(h, 1 if x == 0 else T - 2), :]
             for i, y in enumerate((0, T - 1)):
                 total = None
                 for k in range(R):
@@ -174,8 +247,8 @@
                 q[h, pl.ds(QX_S + 8 * i, 8), :] = total
 
 
-def third_kernel(lp, mo, u2p, ld, qxl, qxh, gxl, gxh, hxl, hxh, lx, mx, s0, s1, qyl, qyh):
-    lx2, mx2 = lx.reshape(HALVES * NB * CW, LANES), mx.reshape(HALVES * NB * CW, LANES)
+def third_kernel(lp, u2p, ld, qxl, qxh, gxl, gxh, hxl, hxh, lx, s0, s1, qyl, qyh):
+    lx2 = lx.reshape(HALVES * NB * CW, LANES)
     flat = lambda r: r.reshape(HALVES * QX, LANES)
     qxl2, qxh2, gxl2, gxh2 = flat(qxl), flat(qxh), flat(gxl), flat(gxh)
 
@@ -185,27 +258,16 @@
             total = total + ref[rows(h * QX + QX_U2 + k, NB, R), :]
         return total * (1.0 / R)
 
+    spread_x(lp, gxl, gxh, lx)
     for h in range(HALVES):
         col = lambda c: rows(h * NB * CW + c, NB, CW)
-        for y in range(NB):
-            lx[h, y, pl.ds(8, NB), :] = lp[pl.ds(h * NB * NB + y * NB, NB), :]
-            mx[h, y, pl.ds(8, NB), :] = mo[pl.ds(h * NB * NB + y * NB, NB), :]
-        for c in (0, CW - 1):
-            lx2[col(c), :] = jnp.zeros((NB, LANES), F)
-            mx2[col(c), :] = jnp.zeros((NB, LANES), F)
-        for c, g in ((1, gxl), (8 + NB, gxh)):
-            for k in range(DEPTH):
-                lx2[col(c + k), :] = g[h, pl.ds(k * NB, NB), :]
-                mx2[col(c + k), :] = g[h, pl.ds((DEPTH + k) * NB, NB), :]
         for c, ref in ((8, gxl2), (7, qxl2), (7 + NB, gxh2), (8 + NB, qxh2)):
             lx2[col(c), :] = lx2[col(c), :] + quarter(ref, h)
         for i, s in enumerate((s0, s1)):
             for c, ref in ((0, gxl), (8, qxl), (16, qxh), (24, gxh)):
                 s[h, pl.ds(c, 8), :] = ref[h, pl.ds(QX_S + 8 * i, 8), :]
-        for y, first, inside, s, q in ((0, 0, 1, s0, qyl), (T - 1, NB - DEPTH, T - 2, s1, qyh)):
-            for k in range(DEPTH):
-                q[h, pl.ds(k * CW, CW), :] = lx[h, first + k]
-                q[h, pl.ds(QY_M + k * CW, CW), :] = mx[h, first + k]
+        cut_wedges(lx, h, qyl, qyh)
+        for y, inside, s, q in ((0, 1, s0, qyl), (T - 1, T - 2, s1, qyh)):
             q[h, pl.ds(QY_S, CW), :] = s[h]
             q[h, pl.ds(QY_U2, T), :] = u2p[h, y + 1, mid(), :]
             q[h, pl.ds(QY_D, T), :] = ld[h, y] + u2p[h, inside + 1, mid(), :]
@@ -217,15 +279,16 @@
 
 
 def last_kernel(
-    lx, mx, s0, s1, gyl, gyh, gxl, gxh, hxl, hxh, hyl, hyh, pxl, pxh, u2p, b, ld,
+    lx, mx, gkl, gkh, s0, s1, gyl, gyh, gxl, gxh, hxl, hxh, hyl, hyh, pxl, pxh, u2p, b, ld,
     out, lg, bc, ca, cb, sp, w0, w1, wh, sh, sems,
 ):
     one = lambda r: pl.ds(r, 1)
     for h in range(HALVES):
-        for k in range(DEPTH):
-            for base, g in ((0, gyl), (DEPTH + NB, gyh)):
-                lg[h, base + k] = g[h, pl.ds(k * CW, CW), :]
-                bc[h, base + k] = 0.8 / (4.0 + g[h, pl.ds(QY_M + k * CW, CW), :])
+        for i in range(1, DEPTH + 1):
+            c, n, at = wedge(i)
+            for r, g, gk in ((DEPTH - i, gyl, gkl), (DEPTH + NB - 1 + i, gyh, gkh)):
+                lg[h, r, pl.ds(c, n), :] = g[h, pl.ds(at, n), :]
+                bc[h, r, pl.ds(c, n), :] = 0.8 / (4.0 + gk[h, pl.ds(at, n), :])
         for y in range(NB):
             lg[h, DEPTH + y] = lx[h, y]
             bc[h, DEPTH + y] = 0.8 / (4.0 + mx[h, y])
@@ -319,11 +382,11 @@
             wh[n, one(7 + T), :] = wh[n, one(7 + T), :] + bumps[h, 1, j][1]
             v = wh[n, mid(), :]
             x = (-1, T)[j]
-            w02[column(w02, h, x), :] = v
-            w12[column(w12, h, x), :] = 0.2 * v + hx[h, BH, :] * (
+            w02[column(h, x), :] = v
+            w12[column(h, x), :] = 0.2 * v + hx[h, BH, :] * (
                 (g[h, DX, :] + add)
                 + (wh[n, left(), :] + wh[n, right(), :])
-                + w02[column(w02, h, (0, T - 1)[j]), :]
+                + w02[column(h, (0, T - 1)[j]), :]
             )
             n += 1
         for i, (g, hy) in enumerate(((gyl, hyl), (gyh, hyh))):
@@ -380,9 +443,14 @@
 H = pl.BlockSpec(memory_space=pltpu.HBM)
 
 
-def shifted(value, axis, step):
+def swapped(axis, low, high):
     size = lax.axis_size(axis)
-    return lax.ppermute(value, axis, [(i, (i + step) % size) for i in range(size)])
+    up = [(i, (i + 1) % size) for i in range(size)]
+    return lax.ppermute(high, axis, up), lax.ppermute(low, axis, [(b, a) for a, b in up])
+
+
+def estimate(flops, size):
+    return pl.CostEstimate(flops=flops, bytes_accessed=size, transcendentals=0)
 
 
 def per_device(load_terms, start_values, reaction_rate):
@@ -390,43 +458,68 @@
     coarse = (HALVES * NB * NB, LANES)
     edge = (HALVES, 3 * T, LANES)
     part = vmem(HALVES * NB * T, LANES)
-    pxl, pxh, pyl, pyh, u1p, b, ld, m, mo = pl.pallas_call(
+    inputs = tuple(
+        pltpu.with_memory_space_constraint(v, pltpu.HBM) for v in (load_terms, start_values, reaction_rate)
+    )
+    strip, line = vmem(HALVES, 2, T, 8, LANES), vmem(HALVES, 2, 1, T, LANES)
+    pxl, pxh, pyl, pyh = pl.pallas_call(
+        edge_kernel,
+        in_specs=[H] * 3,
+        out_specs=[V] * 4,
+        out_shape=[vmem(*edge)] * 4,
+        scratch_shapes=[vmem(HALVES, 2, T + 2, 8, LANES), strip, strip, vmem(HALVES, 2, 2, PC, LANES), line, line]
+        + [pltpu.SemaphoreType.DMA((HALVES, 2, 6))],
+        compiler_params=pltpu.CompilerParams(vmem_limit_bytes=8 * MIB),
+        name="edges",
+    )(*inputs)
+    hxl, hxh = swapped("px", pxl, pxh)
+    hyl, hyh = swapped("py", pyl, pyh)
+    u1p, b, ld, m, mo, kxl, kxh = pl.pallas_call(
         first_kernel,
         in_specs=[H] * 3,
-        out_specs=[V] * 9,
-        out_shape=[vmem(*edge)] * 4 + [vmem(*padded)] + [vmem(*tile)] * 3 + [vmem(*coarse)],
-        scratch_shapes=[vmem(*padded), part, pltpu.SemaphoreType.DMA((3, HALVES))],
+        out_specs=[V] * 7,
+        out_shape=[vmem(*padded)] + [vmem(*tile)] * 3 + [vmem(*coarse)] + [vmem(HALVES, KX, LANES)] * 2,
+        scratch_shapes=[vmem(*padded), part, pltpu.SemaphoreType.DMA((3, HALVES, CHUNKS))],
         compiler_params=pltpu.CompilerParams(vmem_limit_bytes=12 * MIB),
+        cost_estimate=estimate(10**7, 12 * MIB),
         name="first",
-    )(*(pltpu.with_memory_space_constraint(v, pltpu.HBM) for v in (load_terms, start_values, reaction_rate)))
-    hyl, hyh = shifted(pyh, "py", 1), shifted(pyl, "py", -1)
-    hxl, hxh = shifted(pxh, "px", 1), shifted(pxl, "px", -1)
+    )(*inputs)
+    gml, gmh = swapped("px", kxl, kxh)
     _, u2p, lp, qxl, qxh = pl.pallas_call(
         second_kernel,
-        in_specs=[V] * 13,
+        in_specs=[V] * 12,
         out_specs=[V] * 5,
         out_shape=[vmem(*padded)] * 2 + [vmem(*coarse)] + [vmem(HALVES, QX, LANES)] * 2,
         scratch_shapes=[part],
         input_output_aliases={0: 0},
         compiler_params=pltpu.CompilerParams(vmem_limit_bytes=8 * MIB),
         name="second",
-    )(u1p, b, ld, m, mo, pxl, pxh, pyl, pyh, hxl, hxh, hyl, hyh)
-    gxl, gxh = shifted(qxh, "px", 1), shifted(qxl, "px", -1)
-    lx, mx, s0, s1, qyl, qyh = pl.pallas_call(
+    )(u1p, b, ld, m, pxl, pxh, pyl, pyh, hxl, hxh, hyl, hyh)
+    gxl, gxh = swapped("px", qxl, qxh)
+    mx, kyl, kyh = pl.pallas_call(
+        mass_kernel,
+        in_specs=[V] * 3,
+        out_specs=[V] * 3,
+        out_shape=[vmem(HALVES, NB, CW, LANES)] + [vmem(HALVES, KY, LANES)] * 2,
+        compiler_params=pltpu.CompilerParams(vmem_limit_bytes=8 * MIB),
+        name="mass",
+    )(mo, gml, gmh)
+    gkl, gkh = swapped("py", kyl, kyh)
+    lx, s0, s1, qyl, qyh = pl.pallas_call(
         third_kernel,
-        in_specs=[V] * 10,
-        out_specs=[V] * 6,
-        out_shape=[vmem(HALVES, NB, CW, LANES)] * 2
+        in_specs=[V] * 9,
+        out_specs=[V] * 5,
+        out_shape=[vmem(HALVES, NB, CW, LANES)]
         + [vmem(HALVES, CW, LANES)] * 2
         + [vmem(HALVES, QY, LANES)] * 2,
         compiler_params=pltpu.CompilerParams(vmem_limit_bytes=8 * MIB),
         name="third",
-    )(lp, mo, u2p, ld, qxl, qxh, gxl, gxh, hxl, hxh)
-    gyl, gyh = shifted(qyh, "py", 1), shifted(qyl, "py", -1)
+    )(lp, u2p, ld, qxl, qxh, gxl, gxh, hxl, hxh)
+    gyl, gyh = swapped("py", qyl, qyh)
     grid = vmem(HALVES, CR, CW, LANES)
     return pl.pallas_call(
         last_kernel,
-        in_specs=[V] * 17,
+        in_specs=[V] * 19,
         out_specs=H,
         out_shape=jax.ShapeDtypeStruct(load_terms.shape, F),
         scratch_shapes=[grid] * 4
@@ -434,7 +527,7 @@
         + [vmem(8, PC, LANES), vmem(8, T, LANES), pltpu.SemaphoreType.DMA((HALVES, 4))],
         compiler_params=pltpu.CompilerParams(vmem_limit_bytes=20 * MIB),
         name="last",
-    )(lx, mx, s0, s1, gyl, gyh, gxl, gxh, hxl, hxh, hyl, hyh, pxl, pxh, u2p, b, ld)
+    )(lx, mx, gkl, gkh, s0, s1, gyl, gyh, gxl, gxh, hxl, hxh, hyl, hyh, pxl, pxh, u2p, b, ld)
 
 
 def solution(mesh):

time: 77.4 us -> 73.2 us (0.946)
  the two profiles are of different devices: /device:TPU:0 before, /device:TPU:1 now
where the time goes in v2:
time: 73.2 us; the launch traced here: 73.1 us
  starting transfers between devices  29.1 us (40%)
  waiting for transfers between devices  24.5 us (33%)
  Pallas kernels  19.4 us (27%)
    ppermute x6, starting transfers between devices, swapped(): lax.ppermute(high, axis, up)  20 us
    ppermute x6, waiting for transfers between devices, swapped(): lax.ppermute(low, axis, [(b, a) for a, b in up])  14 us
    ppermute x6, waiting for transfers between devices, swapped(): lax.ppermute(high, axis, up)  10.6 us
    ppermute x6, starting transfers between devices, swapped(): lax.ppermute(low, axis, [(b, a) for a, b in up])  9.07 us
    pallas_call x1, Pallas kernels, per_device(): pl.pallas_call(last_kernel, in_specs=[V] * 19, out_specs=H, out_shape=jax...  7.6 us
    pallas_call x1, Pallas kernels, per_device(): pl.pallas_call(first_kernel, in_specs=[H] * 3, out_specs=[V] * 7, out_sha...  5.32 us
    pallas_call x1, Pallas kernels, per_device(): pl.pallas_call(second_kernel, in_specs=[V] * 12, out_specs=[V] * 5, out_s...  3.47 us
    pallas_call x1, Pallas kernels, per_device(): pl.pallas_call(edge_kernel, in_specs=[H] * 3, out_specs=[V] * 4, out_shap...  2.42 us
  transfers between devices with their start and end apart: 12, of which 7 were waited for; matrix products, arithmetic and copies ran while one was open for 0% of the time, Pallas kernels for 8%

profile of v2, /device:TPU:1, one launch (start us, length us, event | category | flops | bytes accessed | tf_op | source)
XLA Modules:
  0.0 73.1 jit_solution(2569484207459612702)
XLA Ops:
  0.0 2.4 %edges.1 = (f32[2,192,128]{2,1,0:T(8,128)S(1)}, f32[2,192,128]{2,1,0:T(8,128)S(1)}, f32[2,192,128]{2,1,0:T(8,128)S(1)}, f32[2,192,128]{2,1,0:T(8,128)S(1)}) custom-call(f32[64,64,256]{2,1,0:T(8,128)} %load_h.3, f32[64,64,256]{2,1,0:T(8,128)} %u_h.3, f32[64,64,256]{2,1,0:T(8,128)} %m_h.3), custom_call_target="tpu_custom_call" | custom-call | tf_op jit(solution)/shard_map/edges/pallas_call | solution.py:465
  2.4 2.1 %collective-permute-start = (f32[2,192,128]{2,1,0:T(8,128)S(1)}, f32[2,192,128]{2,1,0:T(8,128)S(1)}, u32[]{:S(2)}, u32[]{:S(2)}) collective-permute-start(f32[2,192,128]{2,1,0:T(8,128)S(1)} %get-tuple-element.33.pxh), channel_id=1, source_target_pairs={{0,1},{1,2},{2,3},{3,4},{4,5},{5,6},{6,7},{7,0},{8,9},{9,10},{10,1... | collective-permute-start | bytes 589832 | tf_op jit(solution)/shard_map/ppermute | solution.py:449
  4.5 3.6 %collective-permute-start.1 = (f32[2,192,128]{2,1,0:T(8,128)S(1)}, f32[2,192,128]{2,1,0:T(8,128)S(1)}, u32[]{:S(2)}, u32[]{:S(2)}) collective-permute-start(f32[2,192,128]{2,1,0:T(8,128)S(1)} %get-tuple-element.32.pxl), channel_id=1, source_target_pairs={{1,0},{2,1},{3,2},{4,3},{5,4},{6,5},{7,6},{0,7},{9,8},{10,9},{11,1... | collective-permute-start | bytes 589832 | tf_op jit(solution)/shard_map/ppermute | solution.py:449
  8.1 3.3 %collective-permute-start.2 = (f32[2,192,128]{2,1,0:T(8,128)S(1)}, f32[2,192,128]{2,1,0:T(8,128)S(1)}, u32[]{:S(2)}, u32[]{:S(2)}) collective-permute-start(f32[2,192,128]{2,1,0:T(8,128)S(1)} %get-tuple-element.35.pyh), channel_id=1, source_target_pairs={{0,8},{8,16},{16,24},{24,32},{32,40},{40,48},{48,56},{56,64},{64,7... | collective-permute-start | bytes 589832 | tf_op jit(solution)/shard_map/ppermute | solution.py:449
  11.4 0.0 collective-permute-start.3
  11.4 5.3 %first.1 = (f32[2,66,80,128]{3,2,1,0:T(8,128)S(1)}, f32[2,64,64,128]{3,2,1,0:T(8,128)S(1)}, f32[2,64,64,128]{3,2,1,0:T(8,128)S(1)}, f32[2,64,64,128]{3,2,1,0:T(8...) custom-call(f32[64,64,256]{2,1,0:T(8,128)} %load_h.3, ...), custom_call_target="tpu_custom_call" | custom-call | flops 10000000 | bytes 12582912 | tf_op jit(solution)/shard_map/first/pallas_call | solution.py:477
  16.7 0.0 collective-permute-done.hxl
  16.7 0.0 collective-permute-done.1.hxh
  16.7 0.0 collective-permute-done.2.hyl
  16.7 4.1 %collective-permute-done.3.hyh = f32[2,192,128]{2,1,0:T(8,128)S(1)} collective-permute-done((f32[2,192,128]{2,1,0:T(8,128)S(1)}, f32[2,192,128]{2,1,0:T(8,128)S(1)}, u32[]{:S(2)}, u32[]{:S(2)}) %collective-permute-start.3) | collective-permute-done | bytes 196640 | tf_op jit(solution)/shard_map/ppermute | solution.py:449
  20.9 3.5 %second.1 = (f32[2,66,80,128]{3,2,1,0:T(8,128)S(1)}, f32[2,66,80,128]{3,2,1,0:T(8,128)S(1)}, f32[512,128]{1,0:T(8,128)S(1)}, f32[2,256,128]{2,1,0:T(8,128)S(1)}, f32[2,256,128]{2,1,0:T(8,128)S(1)}) custom-call(f32[2,66,80,128]{3,2,1,0:T(8,128)S(1)} %get-tuple-element.28.u1p_in, ...), custom_call_target="tpu_custom_call", output_to_operand_aliasing={{0}: (0, {})} | custom-call | tf_op jit(solution)/shard_map/second/pallas_call | solution.py:488
  24.3 1.4 %collective-permute-start.4 = (f32[2,256,128]{2,1,0:T(8,128)S(1)}, f32[2,256,128]{2,1,0:T(8,128)S(1)}, u32[]{:S(2)}, u32[]{:S(2)}) collective-permute-start(f32[2,256,128]{2,1,0:T(8,128)S(1)} %get-tuple-element.39.qxh), channel_id=1, source_target_pairs={{0,1},{1,2},{2,3},{3,4},{4,5},{5,6},{6,7},{7,0},{8,9},{9,10},{10,1... | collective-permute-start | bytes 786440 | tf_op jit(solution)/shard_map/ppermute | solution.py:449
  25.7 2.3 %collective-permute-start.5 = (f32[2,256,128]{2,1,0:T(8,128)S(1)}, f32[2,256,128]{2,1,0:T(8,128)S(1)}, u32[]{:S(2)}, u32[]{:S(2)}) collective-permute-start(f32[2,256,128]{2,1,0:T(8,128)S(1)} %get-tuple-element.38.qxl), channel_id=1, source_target_pairs={{1,0},{2,1},{3,2},{4,3},{5,4},{6,5},{7,6},{0,7},{9,8},{10,9},{11,1... | collective-permute-start | bytes 786440 | tf_op jit(solution)/shard_map/ppermute | solution.py:449
  28.0 4.2 %collective-permute-done.4.gxl = f32[2,256,128]{2,1,0:T(8,128)S(1)} collective-permute-done((f32[2,256,128]{2,1,0:T(8,128)S(1)}, f32[2,256,128]{2,1,0:T(8,128)S(1)}, u32[]{:S(2)}, u32[]{:S(2)}) %collective-permute-start.4) | collective-permute-done | bytes 262176 | tf_op jit(solution)/shard_map/ppermute | solution.py:449
  32.2 5.3 %collective-permute-done.5.gxh = f32[2,256,128]{2,1,0:T(8,128)S(1)} collective-permute-done((f32[2,256,128]{2,1,0:T(8,128)S(1)}, f32[2,256,128]{2,1,0:T(8,128)S(1)}, u32[]{:S(2)}, u32[]{:S(2)}) %collective-permute-start.5) | collective-permute-done | bytes 262176 | tf_op jit(solution)/shard_map/ppermute | solution.py:449
  37.5 0.4 third.1
  37.9 1.8 %collective-permute-start.10 = (f32[2,336,128]{2,1,0:T(8,128)S(1)}, f32[2,336,128]{2,1,0:T(8,128)S(1)}, u32[]{:S(2)}, u32[]{:S(2)}) collective-permute-start(f32[2,336,128]{2,1,0:T(8,128)S(1)} %get-tuple-element.49), channel_id=1, source_target_pairs={{0,8},{8,16},{16,24},{24,32},{32,40},{40,48},{48,56},{56,64},{64,7... | collective-permute-start | bytes 1032200 | tf_op jit(solution)/shard_map/ppermute | solution.py:449
  39.7 1.0 %collective-permute-start.11 = (f32[2,336,128]{2,1,0:T(8,128)S(1)}, f32[2,336,128]{2,1,0:T(8,128)S(1)}, u32[]{:S(2)}, u32[]{:S(2)}) collective-permute-start(f32[2,336,128]{2,1,0:T(8,128)S(1)} %get-tuple-element.50), channel_id=1, source_target_pairs={{8,0},{16,8},{24,16},{32,24},{40,32},{48,40},{56,48},{64,56},{72,6... | collective-permute-start | bytes 1032200 | tf_op jit(solution)/shard_map/ppermute | solution.py:449
  40.6 1.3 %collective-permute-start.6 = (f32[2,112,128]{2,1,0:T(8,128)S(1)}, f32[2,112,128]{2,1,0:T(8,128)S(1)}, u32[]{:S(2)}, u32[]{:S(2)}) collective-permute-start(f32[2,112,128]{2,1,0:T(8,128)S(1)} %get-tuple-element.42), channel_id=1, source_target_pairs={{0,1},{1,2},{2,3},{3,4},{4,5},{5,6},{6,7},{7,0},{8,9},{9,10},{10,1... | collective-permute-start | bytes 344072 | tf_op jit(solution)/shard_map/ppermute | solution.py:449
  41.9 2.3 %collective-permute-start.7 = (f32[2,112,128]{2,1,0:T(8,128)S(1)}, f32[2,112,128]{2,1,0:T(8,128)S(1)}, u32[]{:S(2)}, u32[]{:S(2)}) collective-permute-start(f32[2,112,128]{2,1,0:T(8,128)S(1)} %get-tuple-element.43), channel_id=1, source_target_pairs={{1,0},{2,1},{3,2},{4,3},{5,4},{6,5},{7,6},{0,7},{9,8},{10,9},{11,1... | collective-permute-start | bytes 344072 | tf_op jit(solution)/shard_map/ppermute | solution.py:449
  44.2 4.0 %collective-permute-done.6.gml = f32[2,112,128]{2,1,0:T(8,128)S(1)} collective-permute-done((f32[2,112,128]{2,1,0:T(8,128)S(1)}, f32[2,112,128]{2,1,0:T(8,128)S(1)}, u32[]{:S(2)}, u32[]{:S(2)}) %collective-permute-start.6) | collective-permute-done | bytes 114720 | tf_op jit(solution)/shard_map/ppermute | solution.py:449
  48.2 0.5 collective-permute-done.7.gmh
  48.7 0.2 mass.1
  49.0 10.2 %collective-permute-start.8 = (f32[2,168,128]{2,1,0:T(8,128)S(1)}, f32[2,168,128]{2,1,0:T(8,128)S(1)}, u32[]{:S(2)}, u32[]{:S(2)}) collective-permute-start(f32[2,168,128]{2,1,0:T(8,128)S(1)} %get-tuple-element.45), channel_id=1, source_target_pairs={{0,8},{8,16},{16,24},{24,32},{32,40},{40,48},{48,56},{56,64},{64,7... | collective-permute-start | bytes 516104 | tf_op jit(solution)/shard_map/ppermute | solution.py:449
  59.2 0.0 collective-permute-start.9
  59.2 2.3 %collective-permute-done.8.gkl = f32[2,168,128]{2,1,0:T(8,128)S(1)} collective-permute-done((f32[2,168,128]{2,1,0:T(8,128)S(1)}, f32[2,168,128]{2,1,0:T(8,128)S(1)}, u32[]{:S(2)}, u32[]{:S(2)}) %collective-permute-start.8) | collective-permute-done | bytes 172064 | tf_op jit(solution)/shard_map/ppermute | solution.py:449
  61.5 4.0 %collective-permute-done.9.gkh = f32[2,168,128]{2,1,0:T(8,128)S(1)} collective-permute-done((f32[2,168,128]{2,1,0:T(8,128)S(1)}, f32[2,168,128]{2,1,0:T(8,128)S(1)}, u32[]{:S(2)}, u32[]{:S(2)}) %collective-permute-start.9) | collective-permute-done | bytes 172064 | tf_op jit(solution)/shard_map/ppermute | solution.py:449
  65.5 0.0 collective-permute-done.10.gyl
  65.5 0.0 collective-permute-done.11.gyh
  65.5 7.6 %last.1 = f32[64,64,256]{2,1,0:T(8,128)} custom-call(f32[2,16,32,128]{3,2,1,0:T(8,128)S(1)} %get-tuple-element.40.lx, f32[2,16,32,128]{3,2,1,0:T(8,128)S(1)} %get-tuple-element.44.mx, f32[2,168,128]{2,1,0:T(8,128)S(1)} %collective-permute-done.8.gkl, f32[2,168,128]{2,1,0:T(8,128)S(1)} %collective-permute-done.9.gkh, f32[2,32,128]{2,1,0:T(8,128)S(1)} %get-tuple-element.47.s0, ...), custom_call_target="tpu_custom_call" | custom-call | tf_op jit(solution)/shard_map/last/pallas_call | solution.py:520
Async XLA Ops:
  2.4 14.3 %collective-permute-start = (f32[2,192,128]{2,1,0:T(8,128)S(1)}, f32[2,192,128]{2,1,0:T(8,128)S(1)}, u32[]{:S(2)}, u32[]{:S(2)}) collective-permute-start(f32[2,192,128]{2,1,0:T(8,128)S(1)} %get-tuple-element.33.pxh), channel_id=1, source_target_pairs={{0,1},{1,2},{2,3},{3,4},{4,5},{5,6},{6,7},{7,0},{8,9},{9,10},{10,1... | collective-permute-start | bytes 589832 | tf_op jit(solution)/shard_map/ppermute | solution.py:449
  4.5 12.2 %collective-permute-start.1 = (f32[2,192,128]{2,1,0:T(8,128)S(1)}, f32[2,192,128]{2,1,0:T(8,128)S(1)}, u32[]{:S(2)}, u32[]{:S(2)}) collective-permute-start(f32[2,192,128]{2,1,0:T(8,128)S(1)} %get-tuple-element.32.pxl), channel_id=1, source_target_pairs={{1,0},{2,1},{3,2},{4,3},{5,4},{6,5},{7,6},{0,7},{9,8},{10,9},{11,1... | collective-permute-start | bytes 589832 | tf_op jit(solution)/shard_map/ppermute | solution.py:449
  8.1 8.6 %collective-permute-start.2 = (f32[2,192,128]{2,1,0:T(8,128)S(1)}, f32[2,192,128]{2,1,0:T(8,128)S(1)}, u32[]{:S(2)}, u32[]{:S(2)}) collective-permute-start(f32[2,192,128]{2,1,0:T(8,128)S(1)} %get-tuple-element.35.pyh), channel_id=1, source_target_pairs={{0,8},{8,16},{16,24},{24,32},{32,40},{40,48},{48,56},{56,64},{64,7... | collective-permute-start | bytes 589832 | tf_op jit(solution)/shard_map/ppermute | solution.py:449
  11.4 9.5 %collective-permute-start.3 = (f32[2,192,128]{2,1,0:T(8,128)S(1)}, f32[2,192,128]{2,1,0:T(8,128)S(1)}, u32[]{:S(2)}, u32[]{:S(2)}) collective-permute-start(f32[2,192,128]{2,1,0:T(8,128)S(1)} %get-tuple-element.34.pyl), channel_id=1, source_target_pairs={{8,0},{16,8},{24,16},{32,24},{40,32},{48,40},{56,48},{64,56},{72,6... | collective-permute-start | bytes 589832 | tf_op jit(solution)/shard_map/ppermute | solution.py:449
  24.3 7.8 %collective-permute-start.4 = (f32[2,256,128]{2,1,0:T(8,128)S(1)}, f32[2,256,128]{2,1,0:T(8,128)S(1)}, u32[]{:S(2)}, u32[]{:S(2)}) collective-permute-start(f32[2,256,128]{2,1,0:T(8,128)S(1)} %get-tuple-element.39.qxh), channel_id=1, source_target_pairs={{0,1},{1,2},{2,3},{3,4},{4,5},{5,6},{6,7},{7,0},{8,9},{9,10},{10,1... | collective-permute-start | bytes 786440 | tf_op jit(solution)/shard_map/ppermute | solution.py:449
  25.7 11.8 %collective-permute-start.5 = (f32[2,256,128]{2,1,0:T(8,128)S(1)}, f32[2,256,128]{2,1,0:T(8,128)S(1)}, u32[]{:S(2)}, u32[]{:S(2)}) collective-permute-start(f32[2,256,128]{2,1,0:T(8,128)S(1)} %get-tuple-element.38.qxl), channel_id=1, source_target_pairs={{1,0},{2,1},{3,2},{4,3},{5,4},{6,5},{7,6},{0,7},{9,8},{10,9},{11,1... | collective-permute-start | bytes 786440 | tf_op jit(solution)/shard_map/ppermute | solution.py:449
  37.9 27.6 %collective-permute-start.10 = (f32[2,336,128]{2,1,0:T(8,128)S(1)}, f32[2,336,128]{2,1,0:T(8,128)S(1)}, u32[]{:S(2)}, u32[]{:S(2)}) collective-permute-start(f32[2,336,128]{2,1,0:T(8,128)S(1)} %get-tuple-element.49), channel_id=1, source_target_pairs={{0,8},{8,16},{16,24},{24,32},{32,40},{40,48},{48,56},{56,64},{64,7... | collective-permute-start | bytes 1032200 | tf_op jit(solution)/shard_map/ppermute | solution.py:449
  39.7 25.8 %collective-permute-start.11 = (f32[2,336,128]{2,1,0:T(8,128)S(1)}, f32[2,336,128]{2,1,0:T(8,128)S(1)}, u32[]{:S(2)}, u32[]{:S(2)}) collective-permute-start(f32[2,336,128]{2,1,0:T(8,128)S(1)} %get-tuple-element.50), channel_id=1, source_target_pairs={{8,0},{16,8},{24,16},{32,24},{40,32},{48,40},{56,48},{64,56},{72,6... | collective-permute-start | bytes 1032200 | tf_op jit(solution)/shard_map/ppermute | solution.py:449
  40.6 7.6 %collective-permute-start.6 = (f32[2,112,128]{2,1,0:T(8,128)S(1)}, f32[2,112,128]{2,1,0:T(8,128)S(1)}, u32[]{:S(2)}, u32[]{:S(2)}) collective-permute-start(f32[2,112,128]{2,1,0:T(8,128)S(1)} %get-tuple-element.42), channel_id=1, source_target_pairs={{0,1},{1,2},{2,3},{3,4},{4,5},{5,6},{6,7},{7,0},{8,9},{9,10},{10,1... | collective-permute-start | bytes 344072 | tf_op jit(solution)/shard_map/ppermute | solution.py:449
  41.9 6.8 %collective-permute-start.7 = (f32[2,112,128]{2,1,0:T(8,128)S(1)}, f32[2,112,128]{2,1,0:T(8,128)S(1)}, u32[]{:S(2)}, u32[]{:S(2)}) collective-permute-start(f32[2,112,128]{2,1,0:T(8,128)S(1)} %get-tuple-element.43), channel_id=1, source_target_pairs={{1,0},{2,1},{3,2},{4,3},{5,4},{6,5},{7,6},{0,7},{9,8},{10,9},{11,1... | collective-permute-start | bytes 344072 | tf_op jit(solution)/shard_map/ppermute | solution.py:449
  49.0 12.6 %collective-permute-start.8 = (f32[2,168,128]{2,1,0:T(8,128)S(1)}, f32[2,168,128]{2,1,0:T(8,128)S(1)}, u32[]{:S(2)}, u32[]{:S(2)}) collective-permute-start(f32[2,168,128]{2,1,0:T(8,128)S(1)} %get-tuple-element.45), channel_id=1, source_target_pairs={{0,8},{8,16},{16,24},{24,32},{32,40},{40,48},{48,56},{56,64},{64,7... | collective-permute-start | bytes 516104 | tf_op jit(solution)/shard_map/ppermute | solution.py:449
  59.2 6.3 %collective-permute-start.9 = (f32[2,168,128]{2,1,0:T(8,128)S(1)}, f32[2,168,128]{2,1,0:T(8,128)S(1)}, u32[]{:S(2)}, u32[]{:S(2)}) collective-permute-start(f32[2,168,128]{2,1,0:T(8,128)S(1)} %get-tuple-element.46), channel_id=1, source_target_pairs={{8,0},{16,8},{24,16},{32,24},{40,32},{48,40},{56,48},{64,56},{72,6... | collective-permute-start | bytes 516104 | tf_op jit(solution)/shard_map/ppermute | solution.py:449

commit v3 on v2

--- a/solution.py
+++ b/solution.py
@@ -19,10 +19,9 @@
 CR = NB + 2 * DEPTH
 KX = DEPTH * NB
 KY = sum(CW - 2 * i for i in range(1, DEPTH + 1))
-QX_U2, QX_D, QX_S = KX, KX + T, KX + 2 * T
-QX = QX_S + 16
-QY_S = KY
-QY_U2, QY_D, QY_DIAG = QY_S + CW, QY_S + CW + T, QY_S + CW + 2 * T
+QX_S, QX_Q = KX, KX + 16
+QX = QX_Q + NB
+QY_S, QY_DIAG = KY, KY + CW
 QY = QY_DIAG + 8
 MIB = 2**20
 
@@ -54,6 +53,16 @@
         lax.fori_loop(0, n, lambda y, c, h=h: (body(h, y), c)[1], 0, unroll=unroll)
 
 
+def carried(h, first, last, src, point, unroll=2):
+    def body(y, c):
+        above, here = c
+        below = src[h, y + 2, mid(), :]
+        point(y, here, (above + below) + (src[h, y + 1, left(), :] + src[h, y + 1, right(), :]))
+        return here, below
+
+    lax.fori_loop(first, last, body, (src[h, first, mid(), :], src[h, first + 1, mid(), :]), unroll=unroll)
+
+
 def clear_border(ref):
     for h in range(HALVES):
         ref[h, 0] = jnp.zeros((PC, LANES), F)
@@ -64,6 +73,24 @@
 
 def column(h, x):
     return rows(h * PLANE + PC + 8 + x, T, PC)
+
+
+SWAPPED = ("py",)
+
+
+def is_even(axis):
+    return lax.rem(lax.axis_index(axis), 2) == 0
+
+
+def order(axis, first, second, a, b):
+    even = is_even(axis) if axis in SWAPPED else False
+    n = first.shape[1]
+    for h in range(HALVES):
+        for r in range(0, n, T):
+            part = pl.ds(r, min(T, n - r))
+            va, vb = a[h, part, :], b[h, part, :]
+            first[h, part, :] = va if even is False else jnp.where(even, vb, va)
+            second[h, part, :] = vb if even is False else jnp.where(even, va, vb)
 
 
 def block_sums(part, out):
@@ -79,7 +106,7 @@
     lax.fori_loop(0, n // T, body, 0)
 
 
-def edge_kernel(load_h, u_h, m_h, pxl, pxh, pyl, pyh, uc, lc, mc, ur, lr, mr, sems):
+def edge_kernel(load_h, u_h, m_h, pxl, pxh, pyl, pyh, pxe, pxo, pye, pyo, uc, lc, mc, ur, lr, mr, sems):
     copies = []
     for h in range(HALVES):
         lanes = pl.ds(h * LANES, LANES)
@@ -125,12 +152,14 @@
             py[h, pl.ds(0, T), :] = u
             py[h, pl.ds(T, T), :] = 0.2 * u + bb * (lr[h, i, 0] + near)
             py[h, pl.ds(2 * T, T), :] = bb
+    order("px", pxe, pxo, pxl, pxh)
+    order("py", pye, pyo, pyl, pyh)
 
 
 CHUNKS = 4
 
 
-def first_kernel(load_h, u_h, m_h, u1p, b, ld, m, mo, kxl, kxh, up, part, sems):
+def first_kernel(load_h, u_h, m_h, u1p, b, ld, m, mo, kxe, kxo, up, part, kxl, kxh, sems):
     step = T // CHUNKS
     copies = {}
     for h in range(HALVES):
@@ -172,6 +201,7 @@
         for first, q in ((0, kxl), (NB - DEPTH, kxh)):
             for k in range(DEPTH):
                 q[h, pl.ds(k * NB, NB), :] = mo[rows(h * NB * NB + first + k, NB, NB), :]
+    order("px", kxe, kxo, kxl, kxh)
 
 
 def spread_x(inner, low, high, ext):
@@ -195,17 +225,50 @@
         high[h, pl.ds(at, n), :] = ext[h, NB - i, pl.ds(c, n), :]
 
 
-def mass_kernel(mo, gml, gmh, mx, kyl, kyh):
+def mass_kernel(mo, gme, gmo, mx, kye, kyo, gml, gmh, kyl, kyh):
+    order("px", gml, gmh, gme, gmo)
     spread_x(mo, gml, gmh, mx)
     for h in range(HALVES):
         cut_wedges(mx, h, kyl, kyh)
-
-
-def second_kernel(u1p_in, b, ld, m, pxl, pxh, pyl, pyh, hxl, hxh, hyl, hyh, u1p, u2p, lp, qxl, qxh, part):
-    del u1p_in
+    order("py", kye, kyo, kyl, kyh)
+
+
+def bulk_kernel(u1p, b, ld, m, u2p, part):
+    clear_border(u2p)
+    for h in range(HALVES):
+
+        def sweep(y, c, near, h=h):
+            u2p[h, y + 1, mid(), :] = 0.2 * c + b[h, y] * (ld[h, y] + near)
+
+        carried(h, 0, T, u1p, sweep)
+    each_row(lambda h, y: defect_rows(h, y, u2p, ld, m, part), NB, unroll=1)
+
+
+def defect_rows(h, y, u2p, ld, m, part):
+    total = None
+    for k in range(R):
+        c = R * y + k
+        d = (ld[h, c] + around(u2p, h, c)) - (4.0 + m[h, c]) * u2p[h, c + 1, mid(), :]
+        total = d if total is None else total + d
+    part[pl.ds(pl.multiple_of((h * NB + y) * T, T), T), :] = total
+
+
+def near_tile(ref, h, y, x):
+    return (ref[h, pl.ds(y, 8), pl.ds(x + 8, 8), :] + ref[h, pl.ds(y + 2, 8), pl.ds(x + 8, 8), :]) + (
+        ref[h, pl.ds(y + 1, 8), pl.ds(x + 7, 8), :] + ref[h, pl.ds(y + 1, 8), pl.ds(x + 9, 8), :]
+    )
+
+
+def second_kernel(
+    u1p_in, u2p_in, part_in, b, ld, m, pxl, pxh, pyl, pyh, hxe, hxo, hye, hyo,
+    u1p, u2p, part, lp, own, qxl, qxh, qxe, qxo, vxe, vxo, vye, vyo, hxl, hxh, hyl, hyh,
+    vxl, vxh, vyl, vyh,
+):
+    del u1p_in, u2p_in, part_in
+    order("px", hxl, hxh, hxe, hxo)
+    order("py", hyl, hyh, hye, hyo)
     u1p2 = u1p.reshape(HALVES * PLANE, LANES)
     U, A, B = pl.ds(0, T), pl.ds(T, T), pl.ds(2 * T, T)
-    clear_border(u2p)
     for h in range(HALVES):
         for x, p, g in ((0, pxl, hxl), (T - 1, pxh, hxh)):
             inner = column(h, x)
@@ -216,82 +279,116 @@
             u1p[h, y + 1, mid(), :] = u1p[h, y + 1, mid(), :] + p[h, B, :] * g[h, U, :]
             u1p[h, 0 if y == 0 else T + 1, mid(), :] = g[h, A, :] + g[h, B, :] * p[h, U, :]
 
-    def sweep(h, y):
-        u2p[h, y + 1, mid(), :] = 0.2 * u1p[h, y + 1, mid(), :] + b[h, y] * (ld[h, y] + around(u1p, h, y))
-
-    each_row(sweep)
-
-    def sums(h, y):
-        total = None
-        for k in range(R):
-            c = R * y + k
-            d = (ld[h, c] + around(u2p, h, c)) - (4.0 + m[h, c]) * u2p[h, c + 1, mid(), :]
-            total = d if total is None else total + d
-        part[pl.ds(pl.multiple_of((h * NB + y) * T, T), T), :] = total
-
-    each_row(sums, NB, unroll=1)
+    for h in range(HALVES):
+        for y in (0, 1, T - 2, T - 1):
+            u2p[h, y + 1, mid(), :] = 0.2 * u1p[h, y + 1, mid(), :] + b[h, y] * (ld[h, y] + around(u1p, h, y))
+
+    def sweep(j, c):
+        y = pl.multiple_of(j * 8, 8)
+        for h in range(HALVES):
+            for x in (0, T - 8):
+                here = (h, pl.ds(y + 1, 8), pl.ds(8 + x, 8))
+                tile = (h, pl.ds(y, 8), pl.ds(x, 8))
+                u2p[here] = 0.2 * u1p[here] + b[tile] * (ld[tile] + near_tile(u1p, h, y, x))
+        return c
+
+    lax.fori_loop(0, T // 8, sweep, 0)
+
+    def sums(j, c):
+        y = pl.multiple_of(j * 8, 8)
+        for h in range(HALVES):
+            for x in (0, T - 8):
+                here = (h, pl.ds(y + 1, 8), pl.ds(8 + x, 8))
+                tile = (h, pl.ds(y, 8), pl.ds(x, 8))
+                d = (ld[tile] + near_tile(u2p, h, y, x)) - (4.0 + m[tile]) * u2p[here]
+                for k in range(2):
+                    at = pl.multiple_of((h * NB + 2 * j + k) * T, T) + x
+                    part[pl.ds(at, 8), :] = (d[R * k] + d[R * k + 1]) + (d[R * k + 2] + d[R * k + 3])
+        return c
+
+    lax.fori_loop(0, T // 8, sums, 0)
+    for h in range(HALVES):
+        for y in (0, NB - 1):
+            defect_rows(h, y, u2p, ld, m, part)
     block_sums(part, lp)
 
     u2p2, ld2 = u2p.reshape(HALVES * PLANE, LANES), ld.reshape(HALVES * T * T, LANES)
     for h in range(HALVES):
-        for x, first, s, q in ((0, 0, 0, qxl), (T - 1, NB - DEPTH, 8, qxh)):
+        for x, first, s, q, v in ((0, 0, 0, qxl, vxl), (T - 1, NB - DEPTH, 8, qxh, vxh)):
             for k in range(DEPTH):
                 q[h, pl.ds(k * NB, NB), :] = lp[rows(h * NB * NB + first + k, NB, NB), :]
-            q[h, pl.ds(QX_U2, T), :] = u2p2[column(h, x), :]
-            q[h, pl.ds(QX_D, T), :] = ld2[rows(h * T * T + x, T, T), :] + u2p2[column(h, 1 if x == 0 else T - 2), :]
             for i, y in enumerate((0, T - 1)):
                 total = None
                 for k in range(R):
-                    v = u2p2[rows(h * PLANE + (y + 1) * PC + 8 + R * s + k, 8, R), :]
-                    total = v if total is None else total + v
+                    e = u2p2[rows(h * PLANE + (y + 1) * PC + 8 + R * s + k, 8, R), :]
+                    total = e if total is None else total + e
                 q[h, pl.ds(QX_S + 8 * i, 8), :] = total
-
-
-def third_kernel(lp, u2p, ld, qxl, qxh, gxl, gxh, hxl, hxh, lx, s0, s1, qyl, qyh):
+                own[h, i, pl.ds(s, 8), :] = total
+                free = QX_S + 8 * i + (7 if x == 0 else 0)
+                q[h, pl.ds(free, 1), :] = u2p[h, y + 1, pl.ds(8 + x, 1), :]
+            total = None
+            for k in range(R):
+                e = u2p2[rows(h * PLANE + (k + 1) * PC + 8 + x, NB, R * PC), :]
+                total = e if total is None else total + e
+            q[h, pl.ds(QX_Q, NB), :] = total * (1.0 / R)
+            v[h, pl.ds(0, T), :] = u2p2[column(h, x), :]
+            v[h, pl.ds(T, T), :] = ld2[rows(h * T * T + x, T, T), :] + u2p2[column(h, 1 if x == 0 else T - 2), :]
+        for y, inside, v in ((0, 1, vyl), (T - 1, T - 2, vyh)):
+            v[h, pl.ds(0, T), :] = u2p[h, y + 1, mid(), :]
+            v[h, pl.ds(T, T), :] = ld[h, y] + u2p[h, inside + 1, mid(), :]
+    order("px", qxe, qxo, qxl, qxh)
+    order("px", vxe, vxo, vxl, vxh)
+    order("py", vye, vyo, vyl, vyh)
+
+
+def third_kernel(lp, own, qxl, qxh, gxe, gxo, hxl, hxh, lx, s0, s1, qye, qyo, gxl, gxh, qyl, qyh):
+    order("px", gxl, gxh, gxe, gxo)
     lx2 = lx.reshape(HALVES * NB * CW, LANES)
-    flat = lambda r: r.reshape(HALVES * QX, LANES)
-    qxl2, qxh2, gxl2, gxh2 = flat(qxl), flat(qxh), flat(gxl), flat(gxh)
-
-    def quarter(ref, h):
-        total = ref[rows(h * QX + QX_U2, NB, R), :]
-        for k in range(1, R):
-            total = total + ref[rows(h * QX + QX_U2 + k, NB, R), :]
-        return total * (1.0 / R)
-
     spread_x(lp, gxl, gxh, lx)
     for h in range(HALVES):
-        col = lambda c: rows(h * NB * CW + c, NB, CW)
-        for c, ref in ((8, gxl2), (7, qxl2), (7 + NB, gxh2), (8 + NB, qxh2)):
-            lx2[col(c), :] = lx2[col(c), :] + quarter(ref, h)
+        for c, ref in ((8, gxl), (7, qxl), (7 + NB, gxh), (8 + NB, qxh)):
+            col = rows(h * NB * CW + c, NB, CW)
+            lx2[col, :] = lx2[col, :] + ref[h, pl.ds(QX_Q, NB), :]
         for i, s in enumerate((s0, s1)):
-            for c, ref in ((0, gxl), (8, qxl), (16, qxh), (24, gxh)):
+            for c, ref in ((0, gxl), (24, gxh)):
                 s[h, pl.ds(c, 8), :] = ref[h, pl.ds(QX_S + 8 * i, 8), :]
+            s[h, pl.ds(8, NB), :] = own[h, i]
         cut_wedges(lx, h, qyl, qyh)
-        for y, inside, s, q in ((0, 1, s0, qyl), (T - 1, T - 2, s1, qyh)):
+        for i, s, q in ((0, s0, qyl), (1, s1, qyh)):
+            y = i * (T - 1)
             q[h, pl.ds(QY_S, CW), :] = s[h]
-            q[h, pl.ds(QY_U2, T), :] = u2p[h, y + 1, mid(), :]
-            q[h, pl.ds(QY_D, T), :] = ld[h, y] + u2p[h, inside + 1, mid(), :]
             for j, (g1, g2) in enumerate(((hxl, gxl), (hxh, gxh))):
                 q[h, pl.ds(QY_DIAG + 3 * j, 1), :] = g1[h, pl.ds(y, 1), :]
                 q[h, pl.ds(QY_DIAG + 3 * j + 1, 1), :] = g1[h, pl.ds(2 * T + y, 1), :]
-                q[h, pl.ds(QY_DIAG + 3 * j + 2, 1), :] = g2[h, pl.ds(QX_U2 + y, 1), :]
+                q[h, pl.ds(QY_DIAG + 3 * j + 2, 1), :] = g2[h, pl.ds(QX_S + 8 * i + 7 * j, 1), :]
             q[h, pl.ds(QY_DIAG + 6, 2), :] = jnp.zeros((2, LANES), F)
-
-
-def last_kernel(
-    lx, mx, gkl, gkh, s0, s1, gyl, gyh, gxl, gxh, hxl, hxh, hyl, hyh, pxl, pxh, u2p, b, ld,
-    out, lg, bc, ca, cb, sp, w0, w1, wh, sh, sems,
-):
-    one = lambda r: pl.ds(r, 1)
+    order("py", qye, qyo, qyl, qyh)
+
+
+def rate_kernel(mx, gke, gko, bc, gkl, gkh):
+    order("py", gkl, gkh, gke, gko)
     for h in range(HALVES):
         for i in range(1, DEPTH + 1):
             c, n, at = wedge(i)
-            for r, g, gk in ((DEPTH - i, gyl, gkl), (DEPTH + NB - 1 + i, gyh, gkh)):
-                lg[h, r, pl.ds(c, n), :] = g[h, pl.ds(at, n), :]
+            for r, gk in ((DEPTH - i, gkl), (DEPTH + NB - 1 + i, gkh)):
                 bc[h, r, pl.ds(c, n), :] = 0.8 / (4.0 + gk[h, pl.ds(at, n), :])
         for y in range(NB):
+            bc[h, DEPTH + y] = 0.8 / (4.0 + mx[h, y])
+
+
+def coarse_kernel(
+    lx, bc, s0, s1, gye, gyo, hxl, hxh, hyl, hyh, pxl, pxh,
+    cv, bumps, gyl, gyh, lg, ca, cb,
+):
+    order("py", gyl, gyh, gye, gyo)
+    one = lambda r: pl.ds(r, 1)
+    for h in range(HALVES):
+        for i in range(1, DEPTH + 1):
+            c, n, at = wedge(i)
+            for r, g in ((DEPTH - i, gyl), (DEPTH + NB - 1 + i, gyh)):
+                lg[h, r, pl.ds(c, n), :] = g[h, pl.ds(at, n), :]
+        for y in range(NB):
             lg[h, DEPTH + y] = lx[h, y]
-            bc[h, DEPTH + y] = 0.8 / (4.0 + mx[h, y])
         quarter = 1.0 / R
         for r, v in (
             (DEPTH - 1, s0[h]),
@@ -301,7 +398,6 @@
         ):
             lg[h, r] = lg[h, r] + quarter * v
 
-    bumps = {}
     for h in range(HALVES):
         for j, (px, hx) in enumerate(((pxl, hxl), (pxh, hxh))):
             for i, (hy, gy) in enumerate(((hyl, gyl), (hyh, gyh))):
@@ -323,26 +419,48 @@
                     lg[h, yy, one(xx), :] = lg[h, yy, one(xx), :] + quarter * (
                         (2.0 - 0.8 / bb) * e + (e1 + e2)
                     )
-                bumps[h, i, j] = (ea, ex, ey, ed + gy[h, one(QY_DIAG + 3 * j + 2), :])
+                at = 4 * (2 * i + j)
+                for k, e in enumerate((ea, ex, ey, ed + gy[h, one(QY_DIAG + 3 * j + 2), :])):
+                    bumps[h, one(at + k), :] = e
+
+    own = pl.ds(8, CW)
 
     def start(h, y):
         v = bc[h, y] * lg[h, y]
         lg[h, y] = v
-        ca[h, y] = v
+        ca[h, y, own, :] = v
 
     each_row(start, CR)
     old, new = ca, cb
     for s in range(1, INNER):
 
-        def inner(h, i, old=old, new=new, s=s):
-            y = i + s
-            c = old[h, y]
-            around_c = (old[h, y - 1] + old[h, y + 1]) + (pltpu.roll(c, 1, 0) + pltpu.roll(c, CW - 1, 0))
-            new[h, y] = (0.2 * c + lg[h, y]) + bc[h, y] * around_c
-
-        each_row(inner, CR - 2 * s)
+        def inner(y, c, old=old, new=new, end=s == INNER - 1):
+            kept = []
+            for h in range(HALVES):
+                above, here = c[h]
+                below = old[h, y + 1, own, :]
+                near = (above + below) + (old[h, y, pl.ds(7, CW), :] + old[h, y, pl.ds(9, CW), :])
+                value = (0.2 * here + lg[h, y]) + bc[h, y] * near
+                if end:
+                    cv[h, y] = value
+                else:
+                    new[h, y, own, :] = value
+                kept.append((here, below))
+            return tuple(kept)
+
+        lax.fori_loop(
+            s, CR - s, inner, tuple((old[h, s - 1, own, :], old[h, s, own, :]) for h in range(HALVES)), unroll=2
+        )
         old, new = new, old
-    cv = old
+
+
+def last_kernel(
+    cv, bumps, vxl, vxh, vye, vyo, hxl, hxh, hyl, hyh, u2p, b, ld,
+    out, vyl, vyh, sp, w0, w1, wh, sh, sems,
+):
+    order("py", vyl, vyh, vye, vyo)
+    one = lambda r: pl.ds(r, 1)
+    bump = lambda h, i, j, k: bumps[h, one(4 * (2 * i + j) + k), :]
     cv2 = cv.reshape(HALVES * CR * CW, LANES)
 
     def correct(h, y):
@@ -361,48 +479,48 @@
         for i in range(2):
             for j in range(2):
                 r, x = (1, T)[i], (8, T + 7)[j]
-                w0[h, r, one(x), :] = w0[h, r, one(x), :] + bumps[h, i, j][0]
-    U2X, DX, U2Y, DY, BH = pl.ds(QX_U2, T), pl.ds(QX_D, T), pl.ds(QY_U2, T), pl.ds(QY_D, T), pl.ds(2 * T, T)
+                w0[h, r, one(x), :] = w0[h, r, one(x), :] + bump(h, i, j, 0)
+    U2, D, BH = pl.ds(0, T), pl.ds(T, T), pl.ds(2 * T, T)
     n = 0
     for h in range(HALVES):
         diag = {}
         for i in range(2):
             for j in range(2):
                 diag[i, j] = (
-                    bumps[h, i, j][3] + cv[h, (DEPTH - 1, DEPTH + NB)[i], one((7, 8 + NB)[j]), :]
+                    bump(h, i, j, 3) + cv[h, (DEPTH - 1, DEPTH + NB)[i], one((7, 8 + NB)[j]), :]
                 )
-        for j, (g, hx) in enumerate(((gxl, hxl), (gxh, hxh))):
+        for j, (g, hx) in enumerate(((vxl, hxl), (vxh, hxh))):
             c = cv2[rows(h * CR * CW + DEPTH * CW + (7, 8 + NB)[j], NB, CW), :]
             for k in range(R):
                 sh[n, rows(k, NB, R), :] = c
             add = sh[n]
-            wh[n, mid(), :] = g[h, U2X, :] + add
+            wh[n, mid(), :] = g[h, U2, :] + add
             wh[n, one(7), :], wh[n, one(8 + T), :] = diag[0, j], diag[1, j]
-            wh[n, one(8), :] = wh[n, one(8), :] + bumps[h, 0, j][1]
-            wh[n, one(7 + T), :] = wh[n, one(7 + T), :] + bumps[h, 1, j][1]
+            wh[n, one(8), :] = wh[n, one(8), :] + bump(h, 0, j, 1)
+            wh[n, one(7 + T), :] = wh[n, one(7 + T), :] + bump(h, 1, j, 1)
             v = wh[n, mid(), :]
             x = (-1, T)[j]
             w02[column(h, x), :] = v
             w12[column(h, x), :] = 0.2 * v + hx[h, BH, :] * (
-                (g[h, DX, :] + add)
+                (g[h, D, :] + add)
                 + (wh[n, left(), :] + wh[n, right(), :])
                 + w02[column(h, (0, T - 1)[j]), :]
             )
             n += 1
-        for i, (g, hy) in enumerate(((gyl, hyl), (gyh, hyh))):
+        for i, (g, hy) in enumerate(((vyl, hyl), (vyh, hyh))):
             c = cv[h, (DEPTH - 1, DEPTH + NB)[i], pl.ds(8, NB), :]
             for k in range(R):
                 sh[n, rows(k, NB, R), :] = c
             add = sh[n]
-            wh[n, mid(), :] = g[h, U2Y, :] + add
+            wh[n, mid(), :] = g[h, U2, :] + add
             wh[n, one(7), :], wh[n, one(8 + T), :] = diag[i, 0], diag[i, 1]
-            wh[n, one(8), :] = wh[n, one(8), :] + bumps[h, i, 0][2]
-            wh[n, one(7 + T), :] = wh[n, one(7 + T), :] + bumps[h, i, 1][2]
+            wh[n, one(8), :] = wh[n, one(8), :] + bump(h, i, 0, 2)
+            wh[n, one(7 + T), :] = wh[n, one(7 + T), :] + bump(h, i, 1, 2)
             v = wh[n, mid(), :]
             r = (0, T + 1)[i]
             w0[h, r, mid(), :] = v
             w1[h, r, mid(), :] = 0.2 * v + hy[h, BH, :] * (
-                (g[h, DY, :] + add)
+                (g[h, D, :] + add)
                 + (wh[n, left(), :] + wh[n, right(), :])
                 + w0[h, (1, T)[i], mid(), :]
             )
@@ -411,18 +529,16 @@
     copies = []
     for h in range(HALVES):
 
-        def one_more(y, c, h=h):
-            w1[h, y + 1, mid(), :] = 0.2 * w0[h, y + 1, mid(), :] + b[h, y] * (ld[h, y] + around(w0, h, y))
-            return c
-
-        def last(y, c, h=h):
-            w0[h, y + 1, mid(), :] = 0.2 * w1[h, y + 1, mid(), :] + b[h, y] * (ld[h, y] + around(w1, h, y))
-            return c
-
-        lax.fori_loop(0, T, one_more, 0, unroll=2)
+        def one_more(y, c, near, h=h):
+            w1[h, y + 1, mid(), :] = 0.2 * c + b[h, y] * (ld[h, y] + near)
+
+        def last(y, c, near, h=h):
+            w0[h, y + 1, mid(), :] = 0.2 * c + b[h, y] * (ld[h, y] + near)
+
+        carried(h, 0, T, w0, one_more)
         step = T // 4
         for q in range(4):
-            lax.fori_loop(q * step, (q + 1) * step, last, 0, unroll=2)
+            carried(h, q * step, (q + 1) * step, w1, last)
             copies.append(
                 pltpu.make_async_copy(
                     w0.at[h, pl.ds(1 + q * step, step), mid(), :],
@@ -443,10 +559,18 @@
 H = pl.BlockSpec(memory_space=pltpu.HBM)
 
 
-def swapped(axis, low, high):
+def swapped(axis, even, odd):
     size = lax.axis_size(axis)
-    up = [(i, (i + 1) % size) for i in range(size)]
-    return lax.ppermute(high, axis, up), lax.ppermute(low, axis, [(b, a) for a, b in up])
+    got = []
+    if axis not in SWAPPED:
+        up = [(i, (i + 1) % size) for i in range(size)]
+        return lax.ppermute(odd, axis, up), lax.ppermute(even, axis, [(b, a) for a, b in up])
+    for first, value in ((0, even), (1, odd)):
+        pairs = []
+        for k in range(first, size, 2):
+            pairs += [(k, (k + 1) % size), ((k + 1) % size, k)]
+        got.append(lax.ppermute(value, axis, pairs))
+    return got
 
 
 def estimate(flops, size):
@@ -462,72 +586,112 @@
         pltpu.with_memory_space_constraint(v, pltpu.HBM) for v in (load_terms, start_values, reaction_rate)
     )
     strip, line = vmem(HALVES, 2, T, 8, LANES), vmem(HALVES, 2, 1, T, LANES)
-    pxl, pxh, pyl, pyh = pl.pallas_call(
+    pxl, pxh, pyl, pyh, pxe, pxo, pye, pyo = pl.pallas_call(
         edge_kernel,
         in_specs=[H] * 3,
-        out_specs=[V] * 4,
-        out_shape=[vmem(*edge)] * 4,
+        out_specs=[V] * 8,
+        out_shape=[vmem(*edge)] * 8,
         scratch_shapes=[vmem(HALVES, 2, T + 2, 8, LANES), strip, strip, vmem(HALVES, 2, 2, PC, LANES), line, line]
         + [pltpu.SemaphoreType.DMA((HALVES, 2, 6))],
         compiler_params=pltpu.CompilerParams(vmem_limit_bytes=8 * MIB),
         name="edges",
     )(*inputs)
-    hxl, hxh = swapped("px", pxl, pxh)
-    hyl, hyh = swapped("py", pyl, pyh)
-    u1p, b, ld, m, mo, kxl, kxh = pl.pallas_call(
+    hxe, hxo = swapped("px", pxe, pxo)
+    hye, hyo = swapped("py", pye, pyo)
+    u1p, b, ld, m, mo, kxe, kxo = pl.pallas_call(
         first_kernel,
         in_specs=[H] * 3,
         out_specs=[V] * 7,
         out_shape=[vmem(*padded)] + [vmem(*tile)] * 3 + [vmem(*coarse)] + [vmem(HALVES, KX, LANES)] * 2,
-        scratch_shapes=[vmem(*padded), part, pltpu.SemaphoreType.DMA((3, HALVES, CHUNKS))],
+        scratch_shapes=[vmem(*padded), part]
+        + [vmem(HALVES, KX, LANES)] * 2
+        + [pltpu.SemaphoreType.DMA((3, HALVES, CHUNKS))],
         compiler_params=pltpu.CompilerParams(vmem_limit_bytes=12 * MIB),
         cost_estimate=estimate(10**7, 12 * MIB),
         name="first",
     )(*inputs)
-    gml, gmh = swapped("px", kxl, kxh)
-    _, u2p, lp, qxl, qxh = pl.pallas_call(
+    gme, gmo = swapped("px", kxe, kxo)
+    outer = vmem(HALVES, 2 * T, LANES)
+    u2p, part_sums = pl.pallas_call(
+        bulk_kernel,
+        in_specs=[V] * 4,
+        out_specs=[V] * 2,
+        out_shape=[vmem(*padded), part],
+        compiler_params=pltpu.CompilerParams(vmem_limit_bytes=4 * MIB),
+        cost_estimate=estimate(10**7, 12 * MIB),
+        name="bulk",
+    )(u1p, b, ld, m)
+    _, u2p, _, lp, own, qxl, qxh, qxe, qxo, vxe, vxo, vye, vyo, hxl, hxh, hyl, hyh = pl.pallas_call(
         second_kernel,
-        in_specs=[V] * 12,
-        out_specs=[V] * 5,
-        out_shape=[vmem(*padded)] * 2 + [vmem(*coarse)] + [vmem(HALVES, QX, LANES)] * 2,
-        scratch_shapes=[part],
-        input_output_aliases={0: 0},
+        in_specs=[V] * 14,
+        out_specs=[V] * 17,
+        out_shape=[vmem(*padded)] * 2
+        + [part, vmem(*coarse), vmem(HALVES, 2, NB, LANES)]
+        + [vmem(HALVES, QX, LANES)] * 4
+        + [outer] * 4
+        + [vmem(*edge)] * 4,
+        scratch_shapes=[outer] * 4,
+        input_output_aliases={0: 0, 1: 1, 2: 2},
         compiler_params=pltpu.CompilerParams(vmem_limit_bytes=8 * MIB),
         name="second",
-    )(u1p, b, ld, m, pxl, pxh, pyl, pyh, hxl, hxh, hyl, hyh)
-    gxl, gxh = swapped("px", qxl, qxh)
-    mx, kyl, kyh = pl.pallas_call(
+    )(u1p, u2p, part_sums, b, ld, m, pxl, pxh, pyl, pyh, hxe, hxo, hye, hyo)
+    gxe, gxo = swapped("px", qxe, qxo)
+    vxl, vxh = swapped("px", vxe, vxo)
+    mx, kye, kyo = pl.pallas_call(
         mass_kernel,
         in_specs=[V] * 3,
         out_specs=[V] * 3,
         out_shape=[vmem(HALVES, NB, CW, LANES)] + [vmem(HALVES, KY, LANES)] * 2,
+        scratch_shapes=[vmem(HALVES, KX, LANES)] * 2 + [vmem(HALVES, KY, LANES)] * 2,
         compiler_params=pltpu.CompilerParams(vmem_limit_bytes=8 * MIB),
         name="mass",
-    )(mo, gml, gmh)
-    gkl, gkh = swapped("py", kyl, kyh)
-    lx, s0, s1, qyl, qyh = pl.pallas_call(
+    )(mo, gme, gmo)
+    gke, gko = swapped("py", kye, kyo)
+    lx, s0, s1, qye, qyo = pl.pallas_call(
         third_kernel,
-        in_specs=[V] * 9,
+        in_specs=[V] * 8,
         out_specs=[V] * 5,
         out_shape=[vmem(HALVES, NB, CW, LANES)]
         + [vmem(HALVES, CW, LANES)] * 2
         + [vmem(HALVES, QY, LANES)] * 2,
+        scratch_shapes=[vmem(HALVES, QX, LANES)] * 2 + [vmem(HALVES, QY, LANES)] * 2,
         compiler_params=pltpu.CompilerParams(vmem_limit_bytes=8 * MIB),
         name="third",
-    )(lp, u2p, ld, qxl, qxh, gxl, gxh, hxl, hxh)
-    gyl, gyh = swapped("py", qyl, qyh)
+    )(lp, own, qxl, qxh, gxe, gxo, hxl, hxh)
+    gye, gyo = swapped("py", qye, qyo)
+    vye, vyo = swapped("py", vye, vyo)
     grid = vmem(HALVES, CR, CW, LANES)
+    bc = pl.pallas_call(
+        rate_kernel,
+        in_specs=[V] * 3,
+        out_specs=V,
+        out_shape=grid,
+        scratch_shapes=[vmem(HALVES, KY, LANES)] * 2,
+        compiler_params=pltpu.CompilerParams(vmem_limit_bytes=8 * MIB),
+        name="rate",
+    )(mx, gke, gko)
+    wide = vmem(HALVES, CR, CW + 16, LANES)
+    cv, bumps = pl.pallas_call(
+        coarse_kernel,
+        in_specs=[V] * 12,
+        out_specs=[V] * 2,
+        out_shape=[grid, vmem(HALVES, 16, LANES)],
+        scratch_shapes=[vmem(HALVES, QY, LANES)] * 2 + [grid, wide, wide],
+        compiler_params=pltpu.CompilerParams(vmem_limit_bytes=8 * MIB),
+        cost_estimate=estimate(10**7, 4 * MIB),
+        name="coarse",
+    )(lx, bc, s0, s1, gye, gyo, hxl, hxh, hyl, hyh, pxl, pxh)
     return pl.pallas_call(
         last_kernel,
-        in_specs=[V] * 19,
+        in_specs=[V] * 13,
         out_specs=H,
         out_shape=jax.ShapeDtypeStruct(load_terms.shape, F),
-        scratch_shapes=[grid] * 4
+        scratch_shapes=[outer] * 2
         + [part, vmem(*padded), vmem(*padded)]
         + [vmem(8, PC, LANES), vmem(8, T, LANES), pltpu.SemaphoreType.DMA((HALVES, 4))],
         compiler_params=pltpu.CompilerParams(vmem_limit_bytes=20 * MIB),
         name="last",
-    )(lx, mx, gkl, gkh, s0, s1, gyl, gyh, gxl, gxh, hxl, hxh, hyl, hyh, pxl, pxh, u2p, b, ld)
+    )(cv, bumps, vxl, vxh, vye, vyo, hxl, hxh, hyl, hyh, u2p, b, ld)
 
 
 def solution(mesh):

time: 73.2 us -> 64.6 us (0.88)
  the two profiles are of different devices: /device:TPU:1 before, /device:TPU:0 now
where the time goes in v3:
time: 64.6 us; the launch traced here: 64.4 us
  starting transfers between devices  31.6 us (49%)
  Pallas kernels  19.5 us (30%)
  waiting for transfers between devices  13.2 us (20%)
    ppermute x8, starting transfers between devices, swapped(): got.append(lax.ppermute(value, axis, pairs))  13.8 us
    ppermute x4, starting transfers between devices, swapped(): lax.ppermute(even, axis, [(b, a) for a, b in up])  13.3 us
    ppermute x8, waiting for transfers between devices, swapped(): got.append(lax.ppermute(value, axis, pairs))  5.33 us
    pallas_call x1, Pallas kernels, per_device(): pl.pallas_call(first_kernel, in_specs=[H] * 3, out_specs=[V] * 7, out_sha...  5.32 us
    ppermute x4, waiting for transfers between devices, swapped(): lax.ppermute(even, axis, [(b, a) for a, b in up])  4.64 us
    ppermute x4, starting transfers between devices, swapped(): lax.ppermute(odd, axis, up)  4.42 us
    pallas_call x1, Pallas kernels, per_device(): pl.pallas_call(last_kernel, in_specs=[V] * 13, out_specs=H, out_shape=jax...  4.41 us
    ppermute x4, waiting for transfers between devices, swapped(): lax.ppermute(odd, axis, up)  3.22 us
  transfers between devices with their start and end apart: 16, of which 10 were waited for; matrix products, arithmetic and copies ran while one was open for 0% of the time, Pallas kernels for 17%

profile of v3, /device:TPU:0, one launch (start us, length us, event | category | flops | bytes accessed | tf_op | source)
XLA Modules:
  0.0 64.4 jit_solution(17369065955856893207)
XLA Ops:
  0.0 2.5 %edges.1 = (f32[2,192,128]{2,1,0:T(8,128)S(1)}, f32[2,192,128]{2,1,0:T(8,128)S(1)}, f32[2,192,128]{2,1,0:T(8,128)S(1)}, f32[2,192,128]{2,1,0:T(8,128)S(1)}, f32[...) custom-call(f32[64,64,256]{2,1,0:T(8,128)} %load_h.3, ...), custom_call_target="tpu_custom_call" | custom-call | tf_op jit(solution)/shard_map/edges/pallas_call | solution.py:589
  2.5 1.7 %collective-permute-start = (f32[2,192,128]{2,1,0:T(8,128)S(1)}, f32[2,192,128]{2,1,0:T(8,128)S(1)}, u32[]{:S(2)}, u32[]{:S(2)}) collective-permute-start(f32[2,192,128]{2,1,0:T(8,128)S(1)} %get-tuple-element.57), channel_id=1, source_target_pairs={{0,1},{1,2},{2,3},{3,4},{4,5},{5,6},{6,7},{7,0},{8,9},{9,10},{10,1... | collective-permute-start | bytes 589832 | tf_op jit(solution)/shard_map/ppermute | solution.py:567
  4.2 3.6 %collective-permute-start.1 = (f32[2,192,128]{2,1,0:T(8,128)S(1)}, f32[2,192,128]{2,1,0:T(8,128)S(1)}, u32[]{:S(2)}, u32[]{:S(2)}) collective-permute-start(f32[2,192,128]{2,1,0:T(8,128)S(1)} %get-tuple-element.58), channel_id=1, source_target_pairs={{1,0},{2,1},{3,2},{4,3},{5,4},{6,5},{7,6},{0,7},{9,8},{10,9},{11,1... | collective-permute-start | bytes 589832 | tf_op jit(solution)/shard_map/ppermute | solution.py:567
  7.7 0.0 collective-permute-start.2
  7.7 5.3 %collective-permute-start.3 = (f32[2,192,128]{2,1,0:T(8,128)S(1)}, f32[2,192,128]{2,1,0:T(8,128)S(1)}, u32[]{:S(2)}, u32[]{:S(2)}) collective-permute-start(f32[2,192,128]{2,1,0:T(8,128)S(1)} %get-tuple-element.60), channel_id=1, source_target_pairs={{8,16},{16,8},{24,32},{32,24},{40,48},{48,40},{56,64},{64,56},{72,... | collective-permute-start | bytes 589832 | tf_op jit(solution)/shard_map/ppermute | solution.py:572
  13.0 5.3 %first.1 = (f32[2,66,80,128]{3,2,1,0:T(8,128)S(1)}, f32[2,64,64,128]{3,2,1,0:T(8,128)S(1)}, f32[2,64,64,128]{3,2,1,0:T(8,128)S(1)}, f32[2,64,64,128]{3,2,1,0:T(8...) custom-call(f32[64,64,256]{2,1,0:T(8,128)} %load_h.3, ...), custom_call_target="tpu_custom_call" | custom-call | flops 10000000 | bytes 12582912 | tf_op jit(solution)/shard_map/first/pallas_call | solution.py:601
  18.3 2.8 %bulk.1 = (f32[2,66,80,128]{3,2,1,0:T(8,128)S(1)}, f32[2048,128]{1,0:T(8,128)S(1)}) custom-call(f32[2,66,80,128]{3,2,1,0:T(8,128)S(1)} %get-tuple-element.47.u1p.u1p_in, f32[2,64,64,128]{3,2,1,0:T(8,128)S(1)} %get-tuple-element.48.b, f32[2,64,64,128]{3,2,1,0:T(8,128)S(1)} %get-tuple-element.49.ld, f32[2,64,64,128]{3,2,1,0:T(8,128)S(1)} %get-tuple-element.50.m), custom_call_target="tpu_custom_call" | custom-call | flops 10000000 | bytes 12582912 | tf_op jit(solution)/shard_map/bulk/pallas_call | solution.py:615
  21.1 0.0 collective-permute-done.hxe
  21.1 0.0 collective-permute-done.1.hxo
  21.1 0.0 collective-permute-done.2.hye
  21.1 0.6 collective-permute-done.3.hyo
  21.7 1.6 %second.1 = (f32[2,66,80,128]{3,2,1,0:T(8,128)S(1)}, f32[2,66,80,128]{3,2,1,0:T(8,128)S(1)}, f32[2048,128]{1,0:T(8,128)S(1)}, f32[512,128]{1,0:T(8,128)S(1)}, f3...) custom-call(f32[2,66,80,128]{3,2,1,0:T(8,128)S(1)} %get-tuple-elemen, ...), custom_call_target="tpu_custom_call", output_to_operand_aliasing={{0}: (0, {}), {1}: (1, {}), {2}: (2, {})} | custom-call | tf_op jit(solution)/shard_map/second/pallas_call | solution.py:624
  23.3 1.2 %collective-permute-start.4 = (f32[2,144,128]{2,1,0:T(8,128)S(1)}, f32[2,144,128]{2,1,0:T(8,128)S(1)}, u32[]{:S(2)}, u32[]{:S(2)}) collective-permute-start(f32[2,144,128]{2,1,0:T(8,128)S(1)} %get-tuple-element.65), channel_id=1, source_target_pairs={{0,1},{1,2},{2,3},{3,4},{4,5},{5,6},{6,7},{7,0},{8,9},{9,10},{10,1... | collective-permute-start | bytes 442376 | tf_op jit(solution)/shard_map/ppermute | solution.py:567
  24.5 3.0 %collective-permute-start.5 = (f32[2,144,128]{2,1,0:T(8,128)S(1)}, f32[2,144,128]{2,1,0:T(8,128)S(1)}, u32[]{:S(2)}, u32[]{:S(2)}) collective-permute-start(f32[2,144,128]{2,1,0:T(8,128)S(1)} %get-tuple-element.66), channel_id=1, source_target_pairs={{1,0},{2,1},{3,2},{4,3},{5,4},{6,5},{7,6},{0,7},{9,8},{10,9},{11,1... | collective-permute-start | bytes 442376 | tf_op jit(solution)/shard_map/ppermute | solution.py:567
  27.5 0.0 collective-permute-start.6
  27.5 4.1 %collective-permute-start.7 = (f32[2,112,128]{2,1,0:T(8,128)S(1)}, f32[2,112,128]{2,1,0:T(8,128)S(1)}, u32[]{:S(2)}, u32[]{:S(2)}) collective-permute-start(f32[2,112,128]{2,1,0:T(8,128)S(1)} %get-tuple-element.72), channel_id=1, source_target_pairs={{1,0},{2,1},{3,2},{4,3},{5,4},{6,5},{7,6},{0,7},{9,8},{10,9},{11,1... | collective-permute-start | bytes 344072 | tf_op jit(solution)/shard_map/ppermute | solution.py:567
  31.7 0.6 collective-permute-done.4.gxe
  32.2 1.9 %collective-permute-done.5.gxo = f32[2,144,128]{2,1,0:T(8,128)S(1)} collective-permute-done((f32[2,144,128]{2,1,0:T(8,128)S(1)}, f32[2,144,128]{2,1,0:T(8,128)S(1)}, u32[]{:S(2)}, u32[]{:S(2)}) %collective-permute-start.5) | collective-permute-done | bytes 147488 | tf_op jit(solution)/shard_map/ppermute | solution.py:567
  34.2 0.4 third.1
  34.5 0.1 collective-permute-start.10
  34.6 1.8 %collective-permute-done.6.gme = f32[2,112,128]{2,1,0:T(8,128)S(1)} collective-permute-done((f32[2,112,128]{2,1,0:T(8,128)S(1)}, f32[2,112,128]{2,1,0:T(8,128)S(1)}, u32[]{:S(2)}, u32[]{:S(2)}) %collective-permute-start.6) | collective-permute-done | bytes 114720 | tf_op jit(solution)/shard_map/ppermute | solution.py:567
  36.4 0.5 collective-permute-done.7.gmo
  36.9 0.3 mass.1
  37.2 0.1 collective-permute-start.8
  37.3 2.7 %collective-permute-start.9 = (f32[2,168,128]{2,1,0:T(8,128)S(1)}, f32[2,168,128]{2,1,0:T(8,128)S(1)}, u32[]{:S(2)}, u32[]{:S(2)}) collective-permute-start(f32[2,168,128]{2,1,0:T(8,128)S(1)} %get-tuple-element.75), channel_id=1, source_target_pairs={{8,16},{16,8},{24,32},{32,24},{40,48},{48,40},{56,64},{64,56},{72,... | collective-permute-start | bytes 516104 | tf_op jit(solution)/shard_map/ppermute | solution.py:572
  40.0 2.7 %collective-permute-start.11 = (f32[2,208,128]{2,1,0:T(8,128)S(1)}, f32[2,208,128]{2,1,0:T(8,128)S(1)}, u32[]{:S(2)}, u32[]{:S(2)}) collective-permute-start(f32[2,208,128]{2,1,0:T(8,128)S(1)} %get-tuple-element.79), channel_id=1, source_target_pairs={{8,16},{16,8},{24,32},{32,24},{40,48},{48,40},{56,64},{64,56},{72,... | collective-permute-start | bytes 638984 | tf_op jit(solution)/shard_map/ppermute | solution.py:572
  42.7 1.6 %collective-permute-start.12 = (f32[2,128,128]{2,1,0:T(8,128)S(1)}, f32[2,128,128]{2,1,0:T(8,128)S(1)}, u32[]{:S(2)}, u32[]{:S(2)}) collective-permute-start(f32[2,128,128]{2,1,0:T(8,128)S(1)} %get-tuple-element.84), channel_id=1, source_target_pairs={{0,1},{1,2},{2,3},{3,4},{4,5},{5,6},{6,7},{7,0},{8,9},{9,10},{10,1... | collective-permute-start | bytes 393224 | tf_op jit(solution)/shard_map/ppermute | solution.py:567
  44.3 0.0 collective-permute-done.8.gke
  44.3 2.6 %collective-permute-start.13 = (f32[2,128,128]{2,1,0:T(8,128)S(1)}, f32[2,128,128]{2,1,0:T(8,128)S(1)}, u32[]{:S(2)}, u32[]{:S(2)}) collective-permute-start(f32[2,128,128]{2,1,0:T(8,128)S(1)} %get-tuple-element.85), channel_id=1, source_target_pairs={{1,0},{2,1},{3,2},{4,3},{5,4},{6,5},{7,6},{0,7},{9,8},{10,9},{11,1... | collective-permute-start | bytes 393224 | tf_op jit(solution)/shard_map/ppermute | solution.py:567
  46.8 0.1 collective-permute-done.9.gko
  47.0 0.0 collective-permute-start.14
  47.0 0.0 collective-permute-done.10.gye
  47.0 2.9 %collective-permute-start.15 = (f32[2,128,128]{2,1,0:T(8,128)S(1)}, f32[2,128,128]{2,1,0:T(8,128)S(1)}, u32[]{:S(2)}, u32[]{:S(2)}) collective-permute-start(f32[2,128,128]{2,1,0:T(8,128)S(1)} %get-tuple-element.87), channel_id=1, source_target_pairs={{8,16},{16,8},{24,32},{32,24},{40,48},{48,40},{56,64},{64,56},{72,... | collective-permute-start | bytes 393224 | tf_op jit(solution)/shard_map/ppermute | solution.py:572
  49.9 0.1 rate.1.bc
  50.1 1.5 %collective-permute-done.11.gyo = f32[2,208,128]{2,1,0:T(8,128)S(1)} collective-permute-done((f32[2,208,128]{2,1,0:T(8,128)S(1)}, f32[2,208,128]{2,1,0:T(8,128)S(1)}, u32[]{:S(2)}, u32[]{:S(2)}) %collective-permute-start.11) | collective-permute-done | bytes 213024 | tf_op jit(solution)/shard_map/ppermute | solution.py:572
  51.6 2.2 %coarse.1 = (f32[2,30,32,128]{3,2,1,0:T(8,128)S(1)}, f32[2,16,128]{2,1,0:T(8,128)S(1)}) custom-call(f32[2,16,32,128]{3,2,1,0:T(8,128)S(1)} %get-tuple-element.69.lx, f32[2,30,32,128]{3,2,1,0:T(8,128)S(1)} %rate.1.bc, f32[2,32,128]{2,1,0:T(8,128)S(1)} %get-tuple-element.76.s0, f32[2,32,128]{2,1,0:T(8,128)S(1)} %get-tuple-element.77.s1, ...), custom_call_target="tpu_custom_call" | custom-call | flops 10000000 | bytes 4194304 | tf_op jit(solution)/shard_map/coarse/pallas_call | solution.py:674
  53.8 0.9 %collective-permute-done.12.vxl = f32[2,128,128]{2,1,0:T(8,128)S(1)} collective-permute-done((f32[2,128,128]{2,1,0:T(8,128)S(1)}, f32[2,128,128]{2,1,0:T(8,128)S(1)}, u32[]{:S(2)}, u32[]{:S(2)}) %collective-permute-start.12) | collective-permute-done | bytes 131104 | tf_op jit(solution)/shard_map/ppermute | solution.py:567
  54.6 2.2 %collective-permute-done.13.vxh = f32[2,128,128]{2,1,0:T(8,128)S(1)} collective-permute-done((f32[2,128,128]{2,1,0:T(8,128)S(1)}, f32[2,128,128]{2,1,0:T(8,128)S(1)}, u32[]{:S(2)}, u32[]{:S(2)}) %collective-permute-start.13) | collective-permute-done | bytes 131104 | tf_op jit(solution)/shard_map/ppermute | solution.py:567
  56.8 0.0 collective-permute-done.14.vye
  56.8 3.1 %collective-permute-done.15.vyo = f32[2,128,128]{2,1,0:T(8,128)S(1)} collective-permute-done((f32[2,128,128]{2,1,0:T(8,128)S(1)}, f32[2,128,128]{2,1,0:T(8,128)S(1)}, u32[]{:S(2)}, u32[]{:S(2)}) %collective-permute-start.15) | collective-permute-done | bytes 131104 | tf_op jit(solution)/shard_map/ppermute | solution.py:572
  60.0 4.4 %last.1 = f32[64,64,256]{2,1,0:T(8,128)} custom-call(f32[2,30,32,128]{3,2,1,0:T(8,128)S(1)} %get-tuple-element.82.cv, f32[2,16,128]{2,1,0:T(8,128)S(1)} %get-tuple-element.83.bumps, f32[2,128,128]{2,1,0:T(8,128)S(1)} %collective-permute-done.12.vxl, f32[2,128,128]{2,1,0:T(8,128)S(1)} %collective-permute-done.13.vxh, ...), custom_call_target="tpu_custom_call" | custom-call | tf_op jit(solution)/shard_map/last/pallas_call | solution.py:684
Async XLA Ops:
  2.5 18.6 %collective-permute-start = (f32[2,192,128]{2,1,0:T(8,128)S(1)}, f32[2,192,128]{2,1,0:T(8,128)S(1)}, u32[]{:S(2)}, u32[]{:S(2)}) collective-permute-start(f32[2,192,128]{2,1,0:T(8,128)S(1)} %get-tuple-element.57), channel_id=1, source_target_pairs={{0,1},{1,2},{2,3},{3,4},{4,5},{5,6},{6,7},{7,0},{8,9},{9,10},{10,1... | collective-permute-start | bytes 589832 | tf_op jit(solution)/shard_map/ppermute | solution.py:567
  4.2 17.0 %collective-permute-start.1 = (f32[2,192,128]{2,1,0:T(8,128)S(1)}, f32[2,192,128]{2,1,0:T(8,128)S(1)}, u32[]{:S(2)}, u32[]{:S(2)}) collective-permute-start(f32[2,192,128]{2,1,0:T(8,128)S(1)} %get-tuple-element.58), channel_id=1, source_target_pairs={{1,0},{2,1},{3,2},{4,3},{5,4},{6,5},{7,6},{0,7},{9,8},{10,9},{11,1... | collective-permute-start | bytes 589832 | tf_op jit(solution)/shard_map/ppermute | solution.py:567
  7.7 13.4 %collective-permute-start.2 = (f32[2,192,128]{2,1,0:T(8,128)S(1)}, f32[2,192,128]{2,1,0:T(8,128)S(1)}, u32[]{:S(2)}, u32[]{:S(2)}) collective-permute-start(f32[2,192,128]{2,1,0:T(8,128)S(1)} %get-tuple-element.59), channel_id=1, source_target_pairs={{0,8},{8,0},{16,24},{24,16},{32,40},{40,32},{48,56},{56,48},{64,72... | collective-permute-start | bytes 589832 | tf_op jit(solution)/shard_map/ppermute | solution.py:572
  7.7 14.0 %collective-permute-start.3 = (f32[2,192,128]{2,1,0:T(8,128)S(1)}, f32[2,192,128]{2,1,0:T(8,128)S(1)}, u32[]{:S(2)}, u32[]{:S(2)}) collective-permute-start(f32[2,192,128]{2,1,0:T(8,128)S(1)} %get-tuple-element.60), channel_id=1, source_target_pairs={{8,16},{16,8},{24,32},{32,24},{40,48},{48,40},{56,64},{64,56},{72,... | collective-permute-start | bytes 589832 | tf_op jit(solution)/shard_map/ppermute | solution.py:572
  23.3 8.9 %collective-permute-start.4 = (f32[2,144,128]{2,1,0:T(8,128)S(1)}, f32[2,144,128]{2,1,0:T(8,128)S(1)}, u32[]{:S(2)}, u32[]{:S(2)}) collective-permute-start(f32[2,144,128]{2,1,0:T(8,128)S(1)} %get-tuple-element.65), channel_id=1, source_target_pairs={{0,1},{1,2},{2,3},{3,4},{4,5},{5,6},{6,7},{7,0},{8,9},{9,10},{10,1... | collective-permute-start | bytes 442376 | tf_op jit(solution)/shard_map/ppermute | solution.py:567
  24.5 9.7 %collective-permute-start.5 = (f32[2,144,128]{2,1,0:T(8,128)S(1)}, f32[2,144,128]{2,1,0:T(8,128)S(1)}, u32[]{:S(2)}, u32[]{:S(2)}) collective-permute-start(f32[2,144,128]{2,1,0:T(8,128)S(1)} %get-tuple-element.66), channel_id=1, source_target_pairs={{1,0},{2,1},{3,2},{4,3},{5,4},{6,5},{7,6},{0,7},{9,8},{10,9},{11,1... | collective-permute-start | bytes 442376 | tf_op jit(solution)/shard_map/ppermute | solution.py:567
  27.5 8.9 %collective-permute-start.6 = (f32[2,112,128]{2,1,0:T(8,128)S(1)}, f32[2,112,128]{2,1,0:T(8,128)S(1)}, u32[]{:S(2)}, u32[]{:S(2)}) collective-permute-start(f32[2,112,128]{2,1,0:T(8,128)S(1)} %get-tuple-element.71), channel_id=1, source_target_pairs={{0,1},{1,2},{2,3},{3,4},{4,5},{5,6},{6,7},{7,0},{8,9},{9,10},{10,1... | collective-permute-start | bytes 344072 | tf_op jit(solution)/shard_map/ppermute | solution.py:567
  27.5 9.4 %collective-permute-start.7 = (f32[2,112,128]{2,1,0:T(8,128)S(1)}, f32[2,112,128]{2,1,0:T(8,128)S(1)}, u32[]{:S(2)}, u32[]{:S(2)}) collective-permute-start(f32[2,112,128]{2,1,0:T(8,128)S(1)} %get-tuple-element.72), channel_id=1, source_target_pairs={{1,0},{2,1},{3,2},{4,3},{5,4},{6,5},{7,6},{0,7},{9,8},{10,9},{11,1... | collective-permute-start | bytes 344072 | tf_op jit(solution)/shard_map/ppermute | solution.py:567
  34.5 12.5 %collective-permute-start.10 = (f32[2,208,128]{2,1,0:T(8,128)S(1)}, f32[2,208,128]{2,1,0:T(8,128)S(1)}, u32[]{:S(2)}, u32[]{:S(2)}) collective-permute-start(f32[2,208,128]{2,1,0:T(8,128)S(1)} %get-tuple-element.78), channel_id=1, source_target_pairs={{0,8},{8,0},{16,24},{24,16},{32,40},{40,32},{48,56},{56,48},{64,72... | collective-permute-start | bytes 638984 | tf_op jit(solution)/shard_map/ppermute | solution.py:572
  37.2 7.1 %collective-permute-start.8 = (f32[2,168,128]{2,1,0:T(8,128)S(1)}, f32[2,168,128]{2,1,0:T(8,128)S(1)}, u32[]{:S(2)}, u32[]{:S(2)}) collective-permute-start(f32[2,168,128]{2,1,0:T(8,128)S(1)} %get-tuple-element.74), channel_id=1, source_target_pairs={{0,8},{8,0},{16,24},{24,16},{32,40},{40,32},{48,56},{56,48},{64,72... | collective-permute-start | bytes 516104 | tf_op jit(solution)/shard_map/ppermute | solution.py:572
  37.3 9.7 %collective-permute-start.9 = (f32[2,168,128]{2,1,0:T(8,128)S(1)}, f32[2,168,128]{2,1,0:T(8,128)S(1)}, u32[]{:S(2)}, u32[]{:S(2)}) collective-permute-start(f32[2,168,128]{2,1,0:T(8,128)S(1)} %get-tuple-element.75), channel_id=1, source_target_pairs={{8,16},{16,8},{24,32},{32,24},{40,48},{48,40},{56,64},{64,56},{72,... | collective-permute-start | bytes 516104 | tf_op jit(solution)/shard_map/ppermute | solution.py:572
  40.0 11.6 %collective-permute-start.11 = (f32[2,208,128]{2,1,0:T(8,128)S(1)}, f32[2,208,128]{2,1,0:T(8,128)S(1)}, u32[]{:S(2)}, u32[]{:S(2)}) collective-permute-start(f32[2,208,128]{2,1,0:T(8,128)S(1)} %get-tuple-element.79), channel_id=1, source_target_pairs={{8,16},{16,8},{24,32},{32,24},{40,48},{48,40},{56,64},{64,56},{72,... | collective-permute-start | bytes 638984 | tf_op jit(solution)/shard_map/ppermute | solution.py:572
  42.7 11.9 %collective-permute-start.12 = (f32[2,128,128]{2,1,0:T(8,128)S(1)}, f32[2,128,128]{2,1,0:T(8,128)S(1)}, u32[]{:S(2)}, u32[]{:S(2)}) collective-permute-start(f32[2,128,128]{2,1,0:T(8,128)S(1)} %get-tuple-element.84), channel_id=1, source_target_pairs={{0,1},{1,2},{2,3},{3,4},{4,5},{5,6},{6,7},{7,0},{8,9},{9,10},{10,1... | collective-permute-start | bytes 393224 | tf_op jit(solution)/shard_map/ppermute | solution.py:567
  44.3 12.6 %collective-permute-start.13 = (f32[2,128,128]{2,1,0:T(8,128)S(1)}, f32[2,128,128]{2,1,0:T(8,128)S(1)}, u32[]{:S(2)}, u32[]{:S(2)}) collective-permute-start(f32[2,128,128]{2,1,0:T(8,128)S(1)} %get-tuple-element.85), channel_id=1, source_target_pairs={{1,0},{2,1},{3,2},{4,3},{5,4},{6,5},{7,6},{0,7},{9,8},{10,9},{11,1... | collective-permute-start | bytes 393224 | tf_op jit(solution)/shard_map/ppermute | solution.py:567
  47.0 9.9 %collective-permute-start.14 = (f32[2,128,128]{2,1,0:T(8,128)S(1)}, f32[2,128,128]{2,1,0:T(8,128)S(1)}, u32[]{:S(2)}, u32[]{:S(2)}) collective-permute-start(f32[2,128,128]{2,1,0:T(8,128)S(1)} %get-tuple-element.86), channel_id=1, source_target_pairs={{0,8},{8,0},{16,24},{24,16},{32,40},{40,32},{48,56},{56,48},{64,72... | collective-permute-start | bytes 393224 | tf_op jit(solution)/shard_map/ppermute | solution.py:572
  47.0 13.0 %collective-permute-start.15 = (f32[2,128,128]{2,1,0:T(8,128)S(1)}, f32[2,128,128]{2,1,0:T(8,128)S(1)}, u32[]{:S(2)}, u32[]{:S(2)}) collective-permute-start(f32[2,128,128]{2,1,0:T(8,128)S(1)} %get-tuple-element.87), channel_id=1, source_target_pairs={{8,16},{16,8},{24,32},{32,24},{40,48},{48,40},{56,64},{64,56},{72,... | collective-permute-start | bytes 393224 | tf_op jit(solution)/shard_map/ppermute | solution.py:572

commit v4 on v3

--- a/solution.py
+++ b/solution.py
@@ -106,19 +106,18 @@
     lax.fori_loop(0, n // T, body, 0)
 
 
-def edge_kernel(load_h, u_h, m_h, pxl, pxh, pyl, pyh, pxe, pxo, pye, pyo, uc, lc, mc, ur, lr, mr, sems):
+def column_edges(load_h, u_h, m_h, pxl, pxh, pxe, pxo, uc, lc, mc, sems):
     copies = []
     for h in range(HALVES):
         lanes = pl.ds(h * LANES, LANES)
         for i in range(2):
-            x, y, yy = (0, T - 8)[i], (0, T - 1)[i], (0, T - 2)[i]
-            for src, dst, n in (
-                (u_h.at[:, pl.ds(x, 8), lanes], uc.at[h, i, pl.ds(1, T)], 0),
-                (load_h.at[:, pl.ds(x, 8), lanes], lc.at[h, i], 1),
-                (m_h.at[:, pl.ds(x, 8), lanes], mc.at[h, i], 2),
-                (u_h.at[pl.ds(yy, 2), :, lanes], ur.at[h, i, :, mid(), :], 3),
-                (load_h.at[pl.ds(y, 1), :, lanes], lr.at[h, i], 4),
-                (m_h.at[pl.ds(y, 1), :, lanes], mr.at[h, i], 5),
+            x = (0, T - 8)[i]
+            for n, (src, dst) in enumerate(
+                (
+                    (u_h.at[:, pl.ds(x, 8), lanes], uc.at[h, i, pl.ds(1, T)]),
+                    (load_h.at[:, pl.ds(x, 8), lanes], lc.at[h, i]),
+                    (m_h.at[:, pl.ds(x, 8), lanes], mc.at[h, i]),
+                )
             ):
                 copies.append(pltpu.make_async_copy(src, dst, sems.at[h, i, n]))
     for c in copies:
@@ -127,16 +126,13 @@
         for i in range(2):
             uc[h, i, 0] = jnp.zeros((8, LANES), F)
             uc[h, i, T + 1] = jnp.zeros((8, LANES), F)
-            for k in range(2):
-                ur[h, i, k, pl.ds(0, 8), :] = jnp.zeros((8, LANES), F)
-                ur[h, i, k, pl.ds(8 + T, 8), :] = jnp.zeros((8, LANES), F)
     for c in copies:
         c.wait()
     uc2 = uc.reshape(HALVES * 2 * (T + 2) * 8, LANES)
     lc2, mc2 = lc.reshape(HALVES * 2 * T * 8, LANES), mc.reshape(HALVES * 2 * T * 8, LANES)
     for h in range(HALVES):
         for i in range(2):
-            px, py = (pxl, pxh)[i], (pyl, pyh)[i]
+            px = (pxl, pxh)[i]
             ub, lb = (h * 2 + i) * (T + 2) * 8, (h * 2 + i) * T * 8
             x, xi = (0, 7)[i], (1, 6)[i]
             u = uc2[rows(ub + 8 + x, T, 8), :]
@@ -145,14 +141,41 @@
             px[h, pl.ds(0, T), :] = u
             px[h, pl.ds(T, T), :] = 0.2 * u + bb * (lc2[rows(lb + x, T, 8), :] + near)
             px[h, pl.ds(2 * T, T), :] = bb
-            k = i
-            u = ur[h, i, k, mid(), :]
-            bb = 0.8 / (4.0 + mr[h, i, 0])
-            near = ur[h, i, 1 - k, mid(), :] + (ur[h, i, k, left(), :] + ur[h, i, k, right(), :])
+    order("px", pxe, pxo, pxl, pxh)
+
+
+def row_edges(load_h, u_h, m_h, pyl, pyh, pye, pyo, ur, lr, mr, sems):
+    copies = []
+    for h in range(HALVES):
+        lanes = pl.ds(h * LANES, LANES)
+        for i in range(2):
+            y, yy = (0, T - 1)[i], (0, T - 2)[i]
+            for n, (src, dst) in enumerate(
+                (
+                    (u_h.at[pl.ds(yy, 2), :, lanes], ur.at[h, i, :, mid(), :]),
+                    (load_h.at[pl.ds(y, 1), :, lanes], lr.at[h, i]),
+                    (m_h.at[pl.ds(y, 1), :, lanes], mr.at[h, i]),
+                )
+            ):
+                copies.append(pltpu.make_async_copy(src, dst, sems.at[h, i, n]))
+    for c in copies:
+        c.start()
+    for h in range(HALVES):
+        for i in range(2):
+            for k in range(2):
+                ur[h, i, k, pl.ds(0, 8), :] = jnp.zeros((8, LANES), F)
+                ur[h, i, k, pl.ds(8 + T, 8), :] = jnp.zeros((8, LANES), F)
+    for c in copies:
+        c.wait()
+    for h in range(HALVES):
+        for k in range(2):
+            py = (pyl, pyh)[k]
+            u = ur[h, k, k, mid(), :]
+            bb = 0.8 / (4.0 + mr[h, k, 0])
+            near = ur[h, k, 1 - k, mid(), :] + (ur[h, k, k, left(), :] + ur[h, k, k, right(), :])
             py[h, pl.ds(0, T), :] = u
-            py[h, pl.ds(T, T), :] = 0.2 * u + bb * (lr[h, i, 0] + near)
+            py[h, pl.ds(T, T), :] = 0.2 * u + bb * (lr[h, k, 0] + near)
             py[h, pl.ds(2 * T, T), :] = bb
-    order("px", pxe, pxo, pxl, pxh)
     order("py", pye, pyo, pyl, pyh)
 
 
@@ -377,9 +400,10 @@
 
 
 def coarse_kernel(
-    lx, bc, s0, s1, gye, gyo, hxl, hxh, hyl, hyh, pxl, pxh,
-    cv, bumps, gyl, gyh, lg, ca, cb,
+    lx, bc, s0, s1, gye, gyo, hxl, hxh, hyl, hyh, pxl, pxh, b, w1_in,
+    w1, sp, bumps, gyl, gyh, lg, ca, cb, cv,
 ):
+    del w1_in
     order("py", gyl, gyh, gye, gyo)
     one = lambda r: pl.ds(r, 1)
     for h in range(HALVES):
@@ -453,89 +477,113 @@
         )
         old, new = new, old
 
+    for h in range(HALVES):
+        for y in range(NB + 2):
+            c = cv[h, y + DEPTH - 1, pl.ds(6, NB + 4), :]
+            for k in range(R):
+                sp[h, y, rows(k, NB + 4, R), :] = c
+
+    def correct(h, y):
+        c = sp[h, y + 1, mid(), :]
+        sides = sp[h, y + 1, left(), :] + sp[h, y + 1, right(), :]
+        above, below = sp[h, y, mid(), :], sp[h, y + 2, mid(), :]
+        base = 0.2 * c
+        inside = sides + (c + c)
+        for k, near in ((0, sides + (c + above)), (1, inside), (2, inside), (3, sides + (c + below))):
+            r = R * y + k
+            w1[h, r + 1, mid(), :] = w1[h, r + 1, mid(), :] + (base + b[h, r] * near)
+
+    each_row(correct, NB, unroll=1)
+
+
+def ahead_kernel(u2p, b, ld, w1):
+    for h in range(HALVES):
+
+        def sweep(y, c, near, h=h):
+            w1[h, y + 1, mid(), :] = 0.2 * c + b[h, y] * (ld[h, y] + near)
+
+        carried(h, 0, T, u2p, sweep)
+
 
 def last_kernel(
-    cv, bumps, vxl, vxh, vye, vyo, hxl, hxh, hyl, hyh, u2p, b, ld,
-    out, vyl, vyh, sp, w0, w1, wh, sh, sems,
+    w1_in, sp, bumps, vxl, vxh, vye, vyo, hxl, hxh, hyl, hyh, u2p, b, ld,
+    w1, out, vyl, vyh, w0, wh, sh, oh, sems,
 ):
+    del w1_in
     order("py", vyl, vyh, vye, vyo)
     one = lambda r: pl.ds(r, 1)
     bump = lambda h, i, j, k: bumps[h, one(4 * (2 * i + j) + k), :]
-    cv2 = cv.reshape(HALVES * CR * CW, LANES)
-
-    def correct(h, y):
-        base = pl.multiple_of((h * NB + y) * T, T)
-        c = cv[h, y + DEPTH, pl.ds(8, NB), :]
-        for k in range(R):
-            sp[rows(base + k, NB, R), :] = c
-        add = sp[pl.ds(base, T), :]
-        for k in range(R):
-            w0[h, R * y + k + 1, mid(), :] = u2p[h, R * y + k + 1, mid(), :] + add
-
-    each_row(correct, NB)
-
-    w02, w12 = w0.reshape(HALVES * PLANE, LANES), w1.reshape(HALVES * PLANE, LANES)
+    stride = (NB + 2) * PC
+    sp2, b2 = sp.reshape(HALVES * stride, LANES), b.reshape(HALVES * T * T, LANES)
+    w12, u2p2 = w1.reshape(HALVES * PLANE, LANES), u2p.reshape(HALVES * PLANE, LANES)
+    U2, D, BH = pl.ds(0, T), pl.ds(T, T), pl.ds(2 * T, T)
+    n = 0
     for h in range(HALVES):
         for i in range(2):
             for j in range(2):
-                r, x = (1, T)[i], (8, T + 7)[j]
-                w0[h, r, one(x), :] = w0[h, r, one(x), :] + bump(h, i, j, 0)
-    U2, D, BH = pl.ds(0, T), pl.ds(T, T), pl.ds(2 * T, T)
-    n = 0
-    for h in range(HALVES):
-        diag = {}
-        for i in range(2):
-            for j in range(2):
-                diag[i, j] = (
-                    bump(h, i, j, 3) + cv[h, (DEPTH - 1, DEPTH + NB)[i], one((7, 8 + NB)[j]), :]
-                )
-        for j, (g, hx) in enumerate(((vxl, hxl), (vxh, hxh))):
-            c = cv2[rows(h * CR * CW + DEPTH * CW + (7, 8 + NB)[j], NB, CW), :]
+                e, y, x = bump(h, i, j, 0), (0, T - 1)[i], (0, T - 1)[j]
+                yi, xi = (1, T - 2)[i], (1, T - 2)[j]
+                for yy, xx, f in ((y, x, None), (y, xi, b), (yi, x, b)):
+                    f = 0.2 if f is None else b[h, yy, one(xx), :]
+                    w1[h, yy + 1, one(xx + 8), :] = w1[h, yy + 1, one(xx + 8), :] + f * e
+        diag = {
+            (i, j): bump(h, i, j, 3) + sp[h, (0, NB + 1)[i], one((7, 8 + T)[j]), :] for i in range(2) for j in range(2)
+        }
+
+        def ring(n, v, bh, c, here, to, ends, corners, h=h):
+            wh[n, mid(), :] = v[h, U2, :]
+            for r, (outside, inside) in zip((0, T - 1), ends):
+                wh[n, one(8 + r), :] = wh[n, one(8 + r), :] + outside
+                oh[n, one(r), :] = oh[n, one(r), :] + inside
+            u2h = wh[n, mid(), :]
+            w0h = u2h + c
+            wh[n, mid(), :] = w0h
+            wh[n, one(7), :], wh[n, one(8 + T), :] = corners
+            near = (wh[n, left(), :] + wh[n, right(), :]) + oh[n]
+            here(u2h)
+            to(0.2 * w0h + bh * ((v[h, D, :] + c) + near))
+
+        for j, (v, hx) in enumerate(((vxl, hxl), (vxh, hxh))):
+            x, xo = (0, T - 1)[j], (-1, T)[j]
             for k in range(R):
-                sh[n, rows(k, NB, R), :] = c
-            add = sh[n]
-            wh[n, mid(), :] = g[h, U2, :] + add
-            wh[n, one(7), :], wh[n, one(8 + T), :] = diag[0, j], diag[1, j]
-            wh[n, one(8), :] = wh[n, one(8), :] + bump(h, 0, j, 1)
-            wh[n, one(7 + T), :] = wh[n, one(7 + T), :] + bump(h, 1, j, 1)
-            v = wh[n, mid(), :]
-            x = (-1, T)[j]
-            w02[column(h, x), :] = v
-            w12[column(h, x), :] = 0.2 * v + hx[h, BH, :] * (
-                (g[h, D, :] + add)
-                + (wh[n, left(), :] + wh[n, right(), :])
-                + w02[column(h, (0, T - 1)[j]), :]
+                sh[n, 0, rows(k, NB, R), :] = sp2[rows(h * stride + PC + 8 + xo, NB, PC), :]
+                sh[n, 1, rows(k, NB, R), :] = sp2[rows(h * stride + PC + 8 + x, NB, PC), :]
+            oh[n] = u2p2[column(h, x), :] + sh[n, 1]
+
+            def here(u2h, h=h, x=x):
+                at = column(h, x)
+                w12[at, :] = w12[at, :] + b2[rows(h * T * T + x, T, T), :] * u2h
+
+            def to(value, h=h, xo=xo):
+                w12[column(h, xo), :] = value
+
+            ring(
+                n, v, hx[h, BH, :], sh[n, 0], here, to,
+                [(bump(h, i, j, 1), bump(h, i, j, 0)) for i in range(2)], (diag[0, j], diag[1, j]),
             )
             n += 1
-        for i, (g, hy) in enumerate(((vyl, hyl), (vyh, hyh))):
-            c = cv[h, (DEPTH - 1, DEPTH + NB)[i], pl.ds(8, NB), :]
-            for k in range(R):
-                sh[n, rows(k, NB, R), :] = c
-            add = sh[n]
-            wh[n, mid(), :] = g[h, U2, :] + add
-            wh[n, one(7), :], wh[n, one(8 + T), :] = diag[i, 0], diag[i, 1]
-            wh[n, one(8), :] = wh[n, one(8), :] + bump(h, i, 0, 2)
-            wh[n, one(7 + T), :] = wh[n, one(7 + T), :] + bump(h, i, 1, 2)
-            v = wh[n, mid(), :]
-            r = (0, T + 1)[i]
-            w0[h, r, mid(), :] = v
-            w1[h, r, mid(), :] = 0.2 * v + hy[h, BH, :] * (
-                (g[h, D, :] + add)
-                + (wh[n, left(), :] + wh[n, right(), :])
-                + w0[h, (1, T)[i], mid(), :]
+        for i, (v, hy) in enumerate(((vyl, hyl), (vyh, hyh))):
+            y = (0, T - 1)[i]
+            oh[n] = u2p[h, y + 1, mid(), :] + sp[h, (1, NB)[i], mid(), :]
+
+            def here(u2h, h=h, y=y):
+                w1[h, y + 1, mid(), :] = w1[h, y + 1, mid(), :] + b[h, y] * u2h
+
+            def to(value, h=h, i=i):
+                w1[h, (0, T + 1)[i], mid(), :] = value
+
+            ring(
+                n, v, hy[h, BH, :], sp[h, (0, NB + 1)[i], mid(), :], here, to,
+                [(bump(h, i, j, 2), bump(h, i, j, 0)) for j in range(2)], (diag[i, 0], diag[i, 1]),
             )
             n += 1
 
     copies = []
     for h in range(HALVES):
 
-        def one_more(y, c, near, h=h):
-            w1[h, y + 1, mid(), :] = 0.2 * c + b[h, y] * (ld[h, y] + near)
-
         def last(y, c, near, h=h):
             w0[h, y + 1, mid(), :] = 0.2 * c + b[h, y] * (ld[h, y] + near)
 
-        carried(h, 0, T, w0, one_more)
         step = T // 4
         for q in range(4):
             carried(h, q * step, (q + 1) * step, w1, last)
@@ -586,18 +634,26 @@
         pltpu.with_memory_space_constraint(v, pltpu.HBM) for v in (load_terms, start_values, reaction_rate)
     )
     strip, line = vmem(HALVES, 2, T, 8, LANES), vmem(HALVES, 2, 1, T, LANES)
-    pxl, pxh, pyl, pyh, pxe, pxo, pye, pyo = pl.pallas_call(
-        edge_kernel,
+    pyl, pyh, pye, pyo = pl.pallas_call(
+        row_edges,
         in_specs=[H] * 3,
-        out_specs=[V] * 8,
-        out_shape=[vmem(*edge)] * 8,
-        scratch_shapes=[vmem(HALVES, 2, T + 2, 8, LANES), strip, strip, vmem(HALVES, 2, 2, PC, LANES), line, line]
-        + [pltpu.SemaphoreType.DMA((HALVES, 2, 6))],
+        out_specs=[V] * 4,
+        out_shape=[vmem(*edge)] * 4,
+        scratch_shapes=[vmem(HALVES, 2, 2, PC, LANES), line, line, pltpu.SemaphoreType.DMA((HALVES, 2, 3))],
+        compiler_params=pltpu.CompilerParams(vmem_limit_bytes=4 * MIB),
+        name="rowedges",
+    )(*inputs)
+    hye, hyo = swapped("py", pye, pyo)
+    pxl, pxh, pxe, pxo = pl.pallas_call(
+        column_edges,
+        in_specs=[H] * 3,
+        out_specs=[V] * 4,
+        out_shape=[vmem(*edge)] * 4,
+        scratch_shapes=[vmem(HALVES, 2, T + 2, 8, LANES), strip, strip, pltpu.SemaphoreType.DMA((HALVES, 2, 3))],
         compiler_params=pltpu.CompilerParams(vmem_limit_bytes=8 * MIB),
-        name="edges",
+        name="columnedges",
     )(*inputs)
     hxe, hxo = swapped("px", pxe, pxo)
-    hye, hyo = swapped("py", pye, pyo)
     u1p, b, ld, m, mo, kxe, kxo = pl.pallas_call(
         first_kernel,
         in_specs=[H] * 3,
@@ -671,27 +727,38 @@
         name="rate",
     )(mx, gke, gko)
     wide = vmem(HALVES, CR, CW + 16, LANES)
-    cv, bumps = pl.pallas_call(
+    u3 = pl.pallas_call(
+        ahead_kernel,
+        in_specs=[V] * 3,
+        out_specs=V,
+        out_shape=vmem(*padded),
+        compiler_params=pltpu.CompilerParams(vmem_limit_bytes=4 * MIB),
+        name="ahead",
+    )(u2p, b, ld)
+    w1, sp, bumps = pl.pallas_call(
         coarse_kernel,
-        in_specs=[V] * 12,
-        out_specs=[V] * 2,
-        out_shape=[grid, vmem(HALVES, 16, LANES)],
-        scratch_shapes=[vmem(HALVES, QY, LANES)] * 2 + [grid, wide, wide],
+        in_specs=[V] * 14,
+        out_specs=[V] * 3,
+        out_shape=[vmem(*padded), vmem(HALVES, NB + 2, PC, LANES), vmem(HALVES, 16, LANES)],
+        scratch_shapes=[vmem(HALVES, QY, LANES)] * 2 + [grid, wide, wide, grid],
+        input_output_aliases={13: 0},
         compiler_params=pltpu.CompilerParams(vmem_limit_bytes=8 * MIB),
         cost_estimate=estimate(10**7, 4 * MIB),
         name="coarse",
-    )(lx, bc, s0, s1, gye, gyo, hxl, hxh, hyl, hyh, pxl, pxh)
-    return pl.pallas_call(
+    )(lx, bc, s0, s1, gye, gyo, hxl, hxh, hyl, hyh, pxl, pxh, b, u3)
+    _, corrected = pl.pallas_call(
         last_kernel,
-        in_specs=[V] * 13,
-        out_specs=H,
-        out_shape=jax.ShapeDtypeStruct(load_terms.shape, F),
+        in_specs=[V] * 14,
+        out_specs=[V, H],
+        out_shape=[vmem(*padded), jax.ShapeDtypeStruct(load_terms.shape, F)],
         scratch_shapes=[outer] * 2
-        + [part, vmem(*padded), vmem(*padded)]
-        + [vmem(8, PC, LANES), vmem(8, T, LANES), pltpu.SemaphoreType.DMA((HALVES, 4))],
-        compiler_params=pltpu.CompilerParams(vmem_limit_bytes=20 * MIB),
+        + [vmem(*padded)]
+        + [vmem(8, PC, LANES), vmem(8, 2, T, LANES), vmem(8, T, LANES), pltpu.SemaphoreType.DMA((HALVES, 4))],
+        input_output_aliases={0: 0},
+        compiler_params=pltpu.CompilerParams(vmem_limit_bytes=12 * MIB),
         name="last",
-    )(cv, bumps, vxl, vxh, vye, vyo, hxl, hxh, hyl, hyh, u2p, b, ld)
+    )(w1, sp, bumps, vxl, vxh, vye, vyo, hxl, hxh, hyl, hyh, u2p, b, ld)
+    return corrected
 
 
 def solution(mesh):

time: 64.6 us -> 62.7 us (0.971)
  waiting for transfers between devices: 13.2 us -> 9.4 us
  Pallas kernels: 19.5 us -> 21.3 us
    ppermute x8, waiting for transfers between devices: 5.33 us -> 3.37 us  [swapped(): got.append(lax.ppermute(value, axis, pairs))]
    pallas_call x3 -> x5, Pallas kernels: 9.08 us -> 10.8 us  [the longest x1 3.26 us: per_device(): pl.pallas_call(coarse_kernel, in_specs=[V] * 14, out_specs=[V] * 3, out_s...]
    ppermute x4, waiting for transfers between devices: 4.64 us -> 3.66 us  [swapped(): lax.ppermute(even, axis, [(b, a) for a, b in up])]
    ppermute x4, waiting for transfers between devices: 3.22 us -> 2.37 us  [swapped(): lax.ppermute(odd, axis, up)]
    ppermute x4, starting transfers between devices: 4.42 us -> 3.66 us  [swapped(): lax.ppermute(odd, axis, up)]
    ppermute x4, starting transfers between devices: 13.3 us -> 14 us  [swapped(): lax.ppermute(even, axis, [(b, a) for a, b in up])]
  transfers between devices with their start and end apart: 16 -> 16, of which waited for: 10 -> 8; matrix products, arithmetic and copies ran while one was open for 0% -> 0% of each run, Pallas kernels for 17% -> 24%
where the time goes in v4:
time: 62.7 us; the launch traced here: 62.4 us
  starting transfers between devices  31.6 us (50%)
  Pallas kernels  21.3 us (34%)
  waiting for transfers between devices  9.4 us (15%)
    ppermute x4, starting transfers between devices, swapped(): lax.ppermute(even, axis, [(b, a) for a, b in up])  14 us
    ppermute x8, starting transfers between devices, swapped(): got.append(lax.ppermute(value, axis, pairs))  13.9 us
    pallas_call x1, Pallas kernels, per_device(): pl.pallas_call(first_kernel, in_specs=[H] * 3, out_specs=[V] * 7, out_sha...  5.32 us
    ppermute x4, starting transfers between devices, swapped(): lax.ppermute(odd, axis, up)  3.66 us
    ppermute x4, waiting for transfers between devices, swapped(): lax.ppermute(even, axis, [(b, a) for a, b in up])  3.66 us
    ppermute x8, waiting for transfers between devices, swapped(): got.append(lax.ppermute(value, axis, pairs))  3.37 us
    pallas_call x1, Pallas kernels, per_device(): pl.pallas_call(coarse_kernel, in_specs=[V] * 14, out_specs=[V] * 3, out_s...  3.26 us
    pallas_call x1, Pallas kernels, per_device(): pl.pallas_call(last_kernel, in_specs=[V] * 14, out_specs=[V, H], out_shap...  2.78 us
  transfers between devices with their start and end apart: 16, of which 8 were waited for; matrix products, arithmetic and copies ran while one was open for 0% of the time, Pallas kernels for 24%

profile of v4, /device:TPU:0, one launch (start us, length us, event | category | flops | bytes accessed | tf_op | source)
XLA Modules:
  0.0 62.4 jit_solution(17031383348446577664)
XLA Ops:
  0.0 2.1 %columnedges.1 = (f32[2,192,128]{2,1,0:T(8,128)S(1)}, f32[2,192,128]{2,1,0:T(8,128)S(1)}, f32[2,192,128]{2,1,0:T(8,128)S(1)}, f32[2,192,128]{2,1,0:T(8,128)S(1)}) custom-call(f32[64,64,256]{2,1,0:T(8,128)} %load_h.5, f32[64,64,256]{2,1,0:T(8,128)} %u_h.5, f32[64,64,256]{2,1,0:T(8,128)} %m_h.5), custom_call_target="tpu_custom_call" | custom-call | tf_op jit(solution)/shard_map/columnedges/pallas_call | solution.py:647
  2.2 1.7 %collective-permute-start = (f32[2,192,128]{2,1,0:T(8,128)S(1)}, f32[2,192,128]{2,1,0:T(8,128)S(1)}, u32[]{:S(2)}, u32[]{:S(2)}) collective-permute-start(f32[2,192,128]{2,1,0:T(8,128)S(1)} %get-tuple-element.59), channel_id=1, source_target_pairs={{0,1},{1,2},{2,3},{3,4},{4,5},{5,6},{6,7},{7,0},{8,9},{9,10},{10,1... | collective-permute-start | bytes 589832 | tf_op jit(solution)/shard_map/ppermute | solution.py:615
  3.8 3.6 %collective-permute-start.1 = (f32[2,192,128]{2,1,0:T(8,128)S(1)}, f32[2,192,128]{2,1,0:T(8,128)S(1)}, u32[]{:S(2)}, u32[]{:S(2)}) collective-permute-start(f32[2,192,128]{2,1,0:T(8,128)S(1)} %get-tuple-element.60), channel_id=1, source_target_pairs={{1,0},{2,1},{3,2},{4,3},{5,4},{6,5},{7,6},{0,7},{9,8},{10,9},{11,1... | collective-permute-start | bytes 589832 | tf_op jit(solution)/shard_map/ppermute | solution.py:615
  7.4 1.2 %rowedges.1 = (f32[2,192,128]{2,1,0:T(8,128)S(1)}, f32[2,192,128]{2,1,0:T(8,128)S(1)}, f32[2,192,128]{2,1,0:T(8,128)S(1)}, f32[2,192,128]{2,1,0:T(8,128)S(1)}) custom-call(f32[64,64,256]{2,1,0:T(8,128)} %load_h.5, f32[64,64,256]{2,1,0:T(8,128)} %u_h.5, f32[64,64,256]{2,1,0:T(8,128)} %m_h.5), custom_call_target="tpu_custom_call" | custom-call | tf_op jit(solution)/shard_map/rowedges/pallas_call | solution.py:637
  8.6 0.1 collective-permute-start.2
  8.7 5.3 %collective-permute-start.3 = (f32[2,192,128]{2,1,0:T(8,128)S(1)}, f32[2,192,128]{2,1,0:T(8,128)S(1)}, u32[]{:S(2)}, u32[]{:S(2)}) collective-permute-start(f32[2,192,128]{2,1,0:T(8,128)S(1)} %get-tuple-element.62), channel_id=1, source_target_pairs={{8,16},{16,8},{24,32},{32,24},{40,48},{48,40},{56,64},{64,56},{72,... | collective-permute-start | bytes 589832 | tf_op jit(solution)/shard_map/ppermute | solution.py:620
  14.0 5.3 %first.1 = (f32[2,66,80,128]{3,2,1,0:T(8,128)S(1)}, f32[2,64,64,128]{3,2,1,0:T(8,128)S(1)}, f32[2,64,64,128]{3,2,1,0:T(8,128)S(1)}, f32[2,64,64,128]{3,2,1,0:T(8...) custom-call(f32[64,64,256]{2,1,0:T(8,128)} %load_h.5, ...), custom_call_target="tpu_custom_call" | custom-call | flops 10000000 | bytes 12582912 | tf_op jit(solution)/shard_map/first/pallas_call | solution.py:657
  19.3 2.8 %bulk.1 = (f32[2,66,80,128]{3,2,1,0:T(8,128)S(1)}, f32[2048,128]{1,0:T(8,128)S(1)}) custom-call(f32[2,66,80,128]{3,2,1,0:T(8,128)S(1)} %get-tuple-element.49.u1p.u1p_in, f32[2,64,64,128]{3,2,1,0:T(8,128)S(1)} %get-tuple-element.50.b, f32[2,64,64,128]{3,2,1,0:T(8,128)S(1)} %get-tuple-element.51.ld, f32[2,64,64,128]{3,2,1,0:T(8,128)S(1)} %get-tuple-element.52.m), custom_call_target="tpu_custom_call" | custom-call | flops 10000000 | bytes 12582912 | tf_op jit(solution)/shard_map/bulk/pallas_call | solution.py:671
  22.1 0.0 collective-permute-done.hxe
  22.1 0.0 collective-permute-done.1.hxo
  22.1 0.0 collective-permute-done.2.hye
  22.1 0.0 collective-permute-done.3.hyo
  22.1 1.6 %second.1 = (f32[2,66,80,128]{3,2,1,0:T(8,128)S(1)}, f32[2,66,80,128]{3,2,1,0:T(8,128)S(1)}, f32[2048,128]{1,0:T(8,128)S(1)}, f32[512,128]{1,0:T(8,128)S(1)}, f3...) custom-call(f32[2,66,80,128]{3,2,1,0:T(8,128)S(1)} %get-tuple-elemen, ...), custom_call_target="tpu_custom_call", output_to_operand_aliasing={{0}: (0, {}), {1}: (1, {}), {2}: (2, {})} | custom-call | tf_op jit(solution)/shard_map/second/pallas_call | solution.py:680
  23.8 0.4 collective-permute-start.4
  24.2 3.8 %collective-permute-start.5 = (f32[2,144,128]{2,1,0:T(8,128)S(1)}, f32[2,144,128]{2,1,0:T(8,128)S(1)}, u32[]{:S(2)}, u32[]{:S(2)}) collective-permute-start(f32[2,144,128]{2,1,0:T(8,128)S(1)} %get-tuple-element.68), channel_id=1, source_target_pairs={{1,0},{2,1},{3,2},{4,3},{5,4},{6,5},{7,6},{0,7},{9,8},{10,9},{11,1... | collective-permute-start | bytes 442376 | tf_op jit(solution)/shard_map/ppermute | solution.py:615
  28.0 0.0 collective-permute-start.6
  28.0 4.1 %collective-permute-start.7 = (f32[2,112,128]{2,1,0:T(8,128)S(1)}, f32[2,112,128]{2,1,0:T(8,128)S(1)}, u32[]{:S(2)}, u32[]{:S(2)}) collective-permute-start(f32[2,112,128]{2,1,0:T(8,128)S(1)} %get-tuple-element.74), channel_id=1, source_target_pairs={{1,0},{2,1},{3,2},{4,3},{5,4},{6,5},{7,6},{0,7},{9,8},{10,9},{11,1... | collective-permute-start | bytes 344072 | tf_op jit(solution)/shard_map/ppermute | solution.py:615
  32.1 0.3 collective-permute-done.4.gxe
  32.4 1.4 %collective-permute-done.5.gxo = f32[2,144,128]{2,1,0:T(8,128)S(1)} collective-permute-done((f32[2,144,128]{2,1,0:T(8,128)S(1)}, f32[2,144,128]{2,1,0:T(8,128)S(1)}, u32[]{:S(2)}, u32[]{:S(2)}) %collective-permute-start.5) | collective-permute-done | bytes 147488 | tf_op jit(solution)/shard_map/ppermute | solution.py:615
  33.8 0.4 third.1
  34.2 0.1 collective-permute-start.10
  34.3 2.1 %collective-permute-done.6.gme = f32[2,112,128]{2,1,0:T(8,128)S(1)} collective-permute-done((f32[2,112,128]{2,1,0:T(8,128)S(1)}, f32[2,112,128]{2,1,0:T(8,128)S(1)}, u32[]{:S(2)}, u32[]{:S(2)}) %collective-permute-start.6) | collective-permute-done | bytes 114720 | tf_op jit(solution)/shard_map/ppermute | solution.py:615
  36.4 0.2 collective-permute-done.7.gmo
  36.6 0.3 mass.1
  36.8 0.1 collective-permute-start.8
  36.9 2.7 %collective-permute-start.9 = (f32[2,168,128]{2,1,0:T(8,128)S(1)}, f32[2,168,128]{2,1,0:T(8,128)S(1)}, u32[]{:S(2)}, u32[]{:S(2)}) collective-permute-start(f32[2,168,128]{2,1,0:T(8,128)S(1)} %get-tuple-element.77), channel_id=1, source_target_pairs={{8,16},{16,8},{24,32},{32,24},{40,48},{48,40},{56,64},{64,56},{72,... | collective-permute-start | bytes 516104 | tf_op jit(solution)/shard_map/ppermute | solution.py:620
  39.6 2.7 %collective-permute-start.11 = (f32[2,208,128]{2,1,0:T(8,128)S(1)}, f32[2,208,128]{2,1,0:T(8,128)S(1)}, u32[]{:S(2)}, u32[]{:S(2)}) collective-permute-start(f32[2,208,128]{2,1,0:T(8,128)S(1)} %get-tuple-element.81), channel_id=1, source_target_pairs={{8,16},{16,8},{24,32},{32,24},{40,48},{48,40},{56,64},{64,56},{72,... | collective-permute-start | bytes 638984 | tf_op jit(solution)/shard_map/ppermute | solution.py:620
  42.4 1.6 %collective-permute-start.12 = (f32[2,128,128]{2,1,0:T(8,128)S(1)}, f32[2,128,128]{2,1,0:T(8,128)S(1)}, u32[]{:S(2)}, u32[]{:S(2)}) collective-permute-start(f32[2,128,128]{2,1,0:T(8,128)S(1)} %get-tuple-element.88), channel_id=1, source_target_pairs={{0,1},{1,2},{2,3},{3,4},{4,5},{5,6},{6,7},{7,0},{8,9},{9,10},{10,1... | collective-permute-start | bytes 393224 | tf_op jit(solution)/shard_map/ppermute | solution.py:615
  44.0 0.0 collective-permute-done.8.gke
  44.0 2.6 %collective-permute-start.13 = (f32[2,128,128]{2,1,0:T(8,128)S(1)}, f32[2,128,128]{2,1,0:T(8,128)S(1)}, u32[]{:S(2)}, u32[]{:S(2)}) collective-permute-start(f32[2,128,128]{2,1,0:T(8,128)S(1)} %get-tuple-element.89), channel_id=1, source_target_pairs={{1,0},{2,1},{3,2},{4,3},{5,4},{6,5},{7,6},{0,7},{9,8},{10,9},{11,1... | collective-permute-start | bytes 393224 | tf_op jit(solution)/shard_map/ppermute | solution.py:615
  46.5 0.1 collective-permute-done.9.gko
  46.7 0.0 collective-permute-start.14
  46.7 0.0 collective-permute-done.10.gye
  46.7 2.9 %collective-permute-start.15 = (f32[2,128,128]{2,1,0:T(8,128)S(1)}, f32[2,128,128]{2,1,0:T(8,128)S(1)}, u32[]{:S(2)}, u32[]{:S(2)}) collective-permute-start(f32[2,128,128]{2,1,0:T(8,128)S(1)} %get-tuple-element.91), channel_id=1, source_target_pairs={{8,16},{16,8},{24,32},{32,24},{40,48},{48,40},{56,64},{64,56},{72,... | collective-permute-start | bytes 393224 | tf_op jit(solution)/shard_map/ppermute | solution.py:620
  49.6 1.4 %ahead.1.w1_in = f32[2,66,80,128]{3,2,1,0:T(8,128)S(1)} custom-call(f32[2,66,80,128]{3,2,1,0:T(8,128)S(1)} %get-tuple-element.84.u2p, f32[2,64,64,128]{3,2,1,0:T(8,128)S(1)} %get-tuple-element.50.b, f32[2,64,64,128]{3,2,1,0:T(8,128)S(1)} %get-tuple-element.51.ld), custom_call_target="tpu_custom_call" | custom-call | tf_op jit(solution)/shard_map/ahead/pallas_call | solution.py:730
  51.0 0.2 rate.1.bc
  51.1 0.1 collective-permute-done.11.gyo
  51.2 3.3 %coarse.1 = (f32[2,66,80,128]{3,2,1,0:T(8,128)S(1)}, f32[2,18,80,128]{3,2,1,0:T(8,128)S(1)}, f32[2,16,128]{2,1,0:T(8,128)S(1)}) custom-call(f32[2,16,32,128]{3,2,1,0:T(8,128)S(1)} %get-tuple-element.71.lx, f32[2,30,32,128]{3,2,1,0:T(8,128)S(1)} %rate.1.bc, f32[2,32,128]{2,1,0:T(8,128)S(1)} %get-tuple-element.78.s0, ...), custom_call_target="tpu_custom_call", output_to_operand_aliasing={{0}: (13, {})} | custom-call | flops 10000000 | bytes 4194304 | tf_op jit(solution)/shard_map/coarse/pallas_call | solution.py:738
  54.5 0.0 collective-permute-done.12.vxl
  54.5 2.0 %collective-permute-done.13.vxh = f32[2,128,128]{2,1,0:T(8,128)S(1)} collective-permute-done((f32[2,128,128]{2,1,0:T(8,128)S(1)}, f32[2,128,128]{2,1,0:T(8,128)S(1)}, u32[]{:S(2)}, u32[]{:S(2)}) %collective-permute-start.13) | collective-permute-done | bytes 131104 | tf_op jit(solution)/shard_map/ppermute | solution.py:615
  56.5 0.0 collective-permute-done.14.vye
  56.5 3.1 %collective-permute-done.15.vyo = f32[2,128,128]{2,1,0:T(8,128)S(1)} collective-permute-done((f32[2,128,128]{2,1,0:T(8,128)S(1)}, f32[2,128,128]{2,1,0:T(8,128)S(1)}, u32[]{:S(2)}, u32[]{:S(2)}) %collective-permute-start.15) | collective-permute-done | bytes 131104 | tf_op jit(solution)/shard_map/ppermute | solution.py:620
  59.6 2.8 %last.1 = (f32[2,66,80,128]{3,2,1,0:T(8,128)S(1)}, f32[64,64,256]{2,1,0:T(8,128)}) custom-call(f32[2,66,80,128]{3,2,1,0:T(8,128)S(1)} %get-tuple-element.85.w1_in, f32[2,18,80,128]{3,2,1,0:T(8,128)S(1)} %get-tuple-element.86.sp, f32[2,16,128]{2,1,0:T(8,128)S(1)} %get-tuple-element.87.bumps, ...), custom_call_target="tpu_custom_call", output_to_operand_aliasing={{0}: (0, {})} | custom-call | tf_op jit(solution)/shard_map/last/pallas_call | solution.py:749
Async XLA Ops:
  2.2 19.9 %collective-permute-start = (f32[2,192,128]{2,1,0:T(8,128)S(1)}, f32[2,192,128]{2,1,0:T(8,128)S(1)}, u32[]{:S(2)}, u32[]{:S(2)}) collective-permute-start(f32[2,192,128]{2,1,0:T(8,128)S(1)} %get-tuple-element.59), channel_id=1, source_target_pairs={{0,1},{1,2},{2,3},{3,4},{4,5},{5,6},{6,7},{7,0},{8,9},{9,10},{10,1... | collective-permute-start | bytes 589832 | tf_op jit(solution)/shard_map/ppermute | solution.py:615
  3.8 18.3 %collective-permute-start.1 = (f32[2,192,128]{2,1,0:T(8,128)S(1)}, f32[2,192,128]{2,1,0:T(8,128)S(1)}, u32[]{:S(2)}, u32[]{:S(2)}) collective-permute-start(f32[2,192,128]{2,1,0:T(8,128)S(1)} %get-tuple-element.60), channel_id=1, source_target_pairs={{1,0},{2,1},{3,2},{4,3},{5,4},{6,5},{7,6},{0,7},{9,8},{10,9},{11,1... | collective-permute-start | bytes 589832 | tf_op jit(solution)/shard_map/ppermute | solution.py:615
  8.6 13.5 %collective-permute-start.2 = (f32[2,192,128]{2,1,0:T(8,128)S(1)}, f32[2,192,128]{2,1,0:T(8,128)S(1)}, u32[]{:S(2)}, u32[]{:S(2)}) collective-permute-start(f32[2,192,128]{2,1,0:T(8,128)S(1)} %get-tuple-element.61), channel_id=1, source_target_pairs={{0,8},{8,0},{16,24},{24,16},{32,40},{40,32},{48,56},{56,48},{64,72... | collective-permute-start | bytes 589832 | tf_op jit(solution)/shard_map/ppermute | solution.py:620
  8.7 13.4 %collective-permute-start.3 = (f32[2,192,128]{2,1,0:T(8,128)S(1)}, f32[2,192,128]{2,1,0:T(8,128)S(1)}, u32[]{:S(2)}, u32[]{:S(2)}) collective-permute-start(f32[2,192,128]{2,1,0:T(8,128)S(1)} %get-tuple-element.62), channel_id=1, source_target_pairs={{8,16},{16,8},{24,32},{32,24},{40,48},{48,40},{56,64},{64,56},{72,... | collective-permute-start | bytes 589832 | tf_op jit(solution)/shard_map/ppermute | solution.py:620
  23.8 8.6 %collective-permute-start.4 = (f32[2,144,128]{2,1,0:T(8,128)S(1)}, f32[2,144,128]{2,1,0:T(8,128)S(1)}, u32[]{:S(2)}, u32[]{:S(2)}) collective-permute-start(f32[2,144,128]{2,1,0:T(8,128)S(1)} %get-tuple-element.67), channel_id=1, source_target_pairs={{0,1},{1,2},{2,3},{3,4},{4,5},{5,6},{6,7},{7,0},{8,9},{9,10},{10,1... | collective-permute-start | bytes 442376 | tf_op jit(solution)/shard_map/ppermute | solution.py:615
  24.2 9.7 %collective-permute-start.5 = (f32[2,144,128]{2,1,0:T(8,128)S(1)}, f32[2,144,128]{2,1,0:T(8,128)S(1)}, u32[]{:S(2)}, u32[]{:S(2)}) collective-permute-start(f32[2,144,128]{2,1,0:T(8,128)S(1)} %get-tuple-element.68), channel_id=1, source_target_pairs={{1,0},{2,1},{3,2},{4,3},{5,4},{6,5},{7,6},{0,7},{9,8},{10,9},{11,1... | collective-permute-start | bytes 442376 | tf_op jit(solution)/shard_map/ppermute | solution.py:615
  28.0 8.4 %collective-permute-start.6 = (f32[2,112,128]{2,1,0:T(8,128)S(1)}, f32[2,112,128]{2,1,0:T(8,128)S(1)}, u32[]{:S(2)}, u32[]{:S(2)}) collective-permute-start(f32[2,112,128]{2,1,0:T(8,128)S(1)} %get-tuple-element.73), channel_id=1, source_target_pairs={{0,1},{1,2},{2,3},{3,4},{4,5},{5,6},{6,7},{7,0},{8,9},{9,10},{10,1... | collective-permute-start | bytes 344072 | tf_op jit(solution)/shard_map/ppermute | solution.py:615
  28.0 8.6 %collective-permute-start.7 = (f32[2,112,128]{2,1,0:T(8,128)S(1)}, f32[2,112,128]{2,1,0:T(8,128)S(1)}, u32[]{:S(2)}, u32[]{:S(2)}) collective-permute-start(f32[2,112,128]{2,1,0:T(8,128)S(1)} %get-tuple-element.74), channel_id=1, source_target_pairs={{1,0},{2,1},{3,2},{4,3},{5,4},{6,5},{7,6},{0,7},{9,8},{10,9},{11,1... | collective-permute-start | bytes 344072 | tf_op jit(solution)/shard_map/ppermute | solution.py:615
  34.2 12.5 %collective-permute-start.10 = (f32[2,208,128]{2,1,0:T(8,128)S(1)}, f32[2,208,128]{2,1,0:T(8,128)S(1)}, u32[]{:S(2)}, u32[]{:S(2)}) collective-permute-start(f32[2,208,128]{2,1,0:T(8,128)S(1)} %get-tuple-element.80), channel_id=1, source_target_pairs={{0,8},{8,0},{16,24},{24,16},{32,40},{40,32},{48,56},{56,48},{64,72... | collective-permute-start | bytes 638984 | tf_op jit(solution)/shard_map/ppermute | solution.py:620
  36.8 7.1 %collective-permute-start.8 = (f32[2,168,128]{2,1,0:T(8,128)S(1)}, f32[2,168,128]{2,1,0:T(8,128)S(1)}, u32[]{:S(2)}, u32[]{:S(2)}) collective-permute-start(f32[2,168,128]{2,1,0:T(8,128)S(1)} %get-tuple-element.76), channel_id=1, source_target_pairs={{0,8},{8,0},{16,24},{24,16},{32,40},{40,32},{48,56},{56,48},{64,72... | collective-permute-start | bytes 516104 | tf_op jit(solution)/shard_map/ppermute | solution.py:620
  36.9 9.7 %collective-permute-start.9 = (f32[2,168,128]{2,1,0:T(8,128)S(1)}, f32[2,168,128]{2,1,0:T(8,128)S(1)}, u32[]{:S(2)}, u32[]{:S(2)}) collective-permute-start(f32[2,168,128]{2,1,0:T(8,128)S(1)} %get-tuple-element.77), channel_id=1, source_target_pairs={{8,16},{16,8},{24,32},{32,24},{40,48},{48,40},{56,64},{64,56},{72,... | collective-permute-start | bytes 516104 | tf_op jit(solution)/shard_map/ppermute | solution.py:620
  39.6 11.6 %collective-permute-start.11 = (f32[2,208,128]{2,1,0:T(8,128)S(1)}, f32[2,208,128]{2,1,0:T(8,128)S(1)}, u32[]{:S(2)}, u32[]{:S(2)}) collective-permute-start(f32[2,208,128]{2,1,0:T(8,128)S(1)} %get-tuple-element.81), channel_id=1, source_target_pairs={{8,16},{16,8},{24,32},{32,24},{40,48},{48,40},{56,64},{64,56},{72,... | collective-permute-start | bytes 638984 | tf_op jit(solution)/shard_map/ppermute | solution.py:620
  42.4 12.1 %collective-permute-start.12 = (f32[2,128,128]{2,1,0:T(8,128)S(1)}, f32[2,128,128]{2,1,0:T(8,128)S(1)}, u32[]{:S(2)}, u32[]{:S(2)}) collective-permute-start(f32[2,128,128]{2,1,0:T(8,128)S(1)} %get-tuple-element.88), channel_id=1, source_target_pairs={{0,1},{1,2},{2,3},{3,4},{4,5},{5,6},{6,7},{7,0},{8,9},{9,10},{10,1... | collective-permute-start | bytes 393224 | tf_op jit(solution)/shard_map/ppermute | solution.py:615
  44.0 12.6 %collective-permute-start.13 = (f32[2,128,128]{2,1,0:T(8,128)S(1)}, f32[2,128,128]{2,1,0:T(8,128)S(1)}, u32[]{:S(2)}, u32[]{:S(2)}) collective-permute-start(f32[2,128,128]{2,1,0:T(8,128)S(1)} %get-tuple-element.89), channel_id=1, source_target_pairs={{1,0},{2,1},{3,2},{4,3},{5,4},{6,5},{7,6},{0,7},{9,8},{10,9},{11,1... | collective-permute-start | bytes 393224 | tf_op jit(solution)/shard_map/ppermute | solution.py:615
  46.7 9.9 %collective-permute-start.14 = (f32[2,128,128]{2,1,0:T(8,128)S(1)}, f32[2,128,128]{2,1,0:T(8,128)S(1)}, u32[]{:S(2)}, u32[]{:S(2)}) collective-permute-start(f32[2,128,128]{2,1,0:T(8,128)S(1)} %get-tuple-element.90), channel_id=1, source_target_pairs={{0,8},{8,0},{16,24},{24,16},{32,40},{40,32},{48,56},{56,48},{64,72... | collective-permute-start | bytes 393224 | tf_op jit(solution)/shard_map/ppermute | solution.py:620
  46.7 13.0 %collective-permute-start.15 = (f32[2,128,128]{2,1,0:T(8,128)S(1)}, f32[2,128,128]{2,1,0:T(8,128)S(1)}, u32[]{:S(2)}, u32[]{:S(2)}) collective-permute-start(f32[2,128,128]{2,1,0:T(8,128)S(1)} %get-tuple-element.91), channel_id=1, source_target_pairs={{8,16},{16,8},{24,32},{32,24},{40,48},{48,40},{56,64},{64,56},{72,... | collective-permute-start | bytes 393224 | tf_op jit(solution)/shard_map/ppermute | solution.py:620

commit v5 on v4

--- a/solution.py
+++ b/solution.py
@@ -53,14 +53,16 @@
         lax.fori_loop(0, n, lambda y, c, h=h: (body(h, y), c)[1], 0, unroll=unroll)
 
 
-def carried(h, first, last, src, point, unroll=2):
+def carried(h, first, last, src, point, x=0, n=T, unroll=2):
+    here_x, left_x, right_x = pl.ds(8 + x, n), pl.ds(7 + x, n), pl.ds(9 + x, n)
+
     def body(y, c):
         above, here = c
-        below = src[h, y + 2, mid(), :]
-        point(y, here, (above + below) + (src[h, y + 1, left(), :] + src[h, y + 1, right(), :]))
+        below = src[h, y + 2, here_x, :]
+        point(y, here, (above + below) + (src[h, y + 1, left_x, :] + src[h, y + 1, right_x, :]))
         return here, below
 
-    lax.fori_loop(first, last, body, (src[h, first, mid(), :], src[h, first + 1, mid(), :]), unroll=unroll)
+    lax.fori_loop(first, last, body, (src[h, first, here_x, :], src[h, first + 1, here_x, :]), unroll=unroll)
 
 
 def clear_border(ref):
@@ -75,15 +77,16 @@
     return rows(h * PLANE + PC + 8 + x, T, PC)
 
 
-SWAPPED = ("py",)
+AXIS = {"r1x": "px", "massx": "px", "r2x": "px", "u2x": "px", "r1y": "py", "massy": "py", "r2y": "py", "u2y": "py"}
+SWAPPED = ("r1x", "massx", "r2x", "u2x", "r1y", "massy", "r2y", "u2y")
 
 
 def is_even(axis):
     return lax.rem(lax.axis_index(axis), 2) == 0
 
 
-def order(axis, first, second, a, b):
-    even = is_even(axis) if axis in SWAPPED else False
+def order(name, first, second, a, b):
+    even = is_even(AXIS[name]) if name in SWAPPED else False
     n = first.shape[1]
     for h in range(HALVES):
         for r in range(0, n, T):
@@ -141,7 +144,7 @@
             px[h, pl.ds(0, T), :] = u
             px[h, pl.ds(T, T), :] = 0.2 * u + bb * (lc2[rows(lb + x, T, 8), :] + near)
             px[h, pl.ds(2 * T, T), :] = bb
-    order("px", pxe, pxo, pxl, pxh)
+    order("r1x", pxe, pxo, pxl, pxh)
 
 
 def row_edges(load_h, u_h, m_h, pyl, pyh, pye, pyo, ur, lr, mr, sems):
@@ -176,7 +179,7 @@
             py[h, pl.ds(0, T), :] = u
             py[h, pl.ds(T, T), :] = 0.2 * u + bb * (lr[h, k, 0] + near)
             py[h, pl.ds(2 * T, T), :] = bb
-    order("py", pye, pyo, pyl, pyh)
+    order("r1y", pye, pyo, pyl, pyh)
 
 
 CHUNKS = 4
@@ -224,7 +227,7 @@
         for first, q in ((0, kxl), (NB - DEPTH, kxh)):
             for k in range(DEPTH):
                 q[h, pl.ds(k * NB, NB), :] = mo[rows(h * NB * NB + first + k, NB, NB), :]
-    order("px", kxe, kxo, kxl, kxh)
+    order("massx", kxe, kxo, kxl, kxh)
 
 
 def spread_x(inner, low, high, ext):
@@ -249,11 +252,11 @@
 
 
 def mass_kernel(mo, gme, gmo, mx, kye, kyo, gml, gmh, kyl, kyh):
-    order("px", gml, gmh, gme, gmo)
+    order("massx", gml, gmh, gme, gmo)
     spread_x(mo, gml, gmh, mx)
     for h in range(HALVES):
         cut_wedges(mx, h, kyl, kyh)
-    order("py", kye, kyo, kyl, kyh)
+    order("massy", kye, kyo, kyl, kyh)
 
 
 def bulk_kernel(u1p, b, ld, m, u2p, part):
@@ -264,7 +267,22 @@
             u2p[h, y + 1, mid(), :] = 0.2 * c + b[h, y] * (ld[h, y] + near)
 
         carried(h, 0, T, u1p, sweep)
-    each_row(lambda h, y: defect_rows(h, y, u2p, ld, m, part), NB, unroll=1)
+    for h in range(HALVES):
+
+        def sums(y, c, h=h):
+            above, here = c
+            total = None
+            for k in range(R):
+                r = R * y + k
+                below = u2p[h, r + 2, mid(), :]
+                near = (above + below) + (u2p[h, r + 1, left(), :] + u2p[h, r + 1, right(), :])
+                d = (ld[h, r] + near) - (4.0 + m[h, r]) * here
+                total = d if total is None else total + d
+                above, here = here, below
+            part[pl.ds(pl.multiple_of((h * NB + y) * T, T), T), :] = total
+            return above, here
+
+        lax.fori_loop(0, NB, sums, (u2p[h, 0, mid(), :], u2p[h, 1, mid(), :]))
 
 
 def defect_rows(h, y, u2p, ld, m, part):
@@ -288,8 +306,8 @@
     vxl, vxh, vyl, vyh,
 ):
     del u1p_in, u2p_in, part_in
-    order("px", hxl, hxh, hxe, hxo)
-    order("py", hyl, hyh, hye, hyo)
+    order("r1x", hxl, hxh, hxe, hxo)
+    order("r1y", hyl, hyh, hye, hyo)
     u1p2 = u1p.reshape(HALVES * PLANE, LANES)
     U, A, B = pl.ds(0, T), pl.ds(T, T), pl.ds(2 * T, T)
     for h in range(HALVES):
@@ -359,13 +377,13 @@
         for y, inside, v in ((0, 1, vyl), (T - 1, T - 2, vyh)):
             v[h, pl.ds(0, T), :] = u2p[h, y + 1, mid(), :]
             v[h, pl.ds(T, T), :] = ld[h, y] + u2p[h, inside + 1, mid(), :]
-    order("px", qxe, qxo, qxl, qxh)
-    order("px", vxe, vxo, vxl, vxh)
-    order("py", vye, vyo, vyl, vyh)
+    order("r2x", qxe, qxo, qxl, qxh)
+    order("u2x", vxe, vxo, vxl, vxh)
+    order("u2y", vye, vyo, vyl, vyh)
 
 
 def third_kernel(lp, own, qxl, qxh, gxe, gxo, hxl, hxh, lx, s0, s1, qye, qyo, gxl, gxh, qyl, qyh):
-    order("px", gxl, gxh, gxe, gxo)
+    order("r2x", gxl, gxh, gxe, gxo)
     lx2 = lx.reshape(HALVES * NB * CW, LANES)
     spread_x(lp, gxl, gxh, lx)
     for h in range(HALVES):
@@ -385,11 +403,11 @@
                 q[h, pl.ds(QY_DIAG + 3 * j + 1, 1), :] = g1[h, pl.ds(2 * T + y, 1), :]
                 q[h, pl.ds(QY_DIAG + 3 * j + 2, 1), :] = g2[h, pl.ds(QX_S + 8 * i + 7 * j, 1), :]
             q[h, pl.ds(QY_DIAG + 6, 2), :] = jnp.zeros((2, LANES), F)
-    order("py", qye, qyo, qyl, qyh)
+    order("r2y", qye, qyo, qyl, qyh)
 
 
 def rate_kernel(mx, gke, gko, bc, gkl, gkh):
-    order("py", gkl, gkh, gke, gko)
+    order("massy", gkl, gkh, gke, gko)
     for h in range(HALVES):
         for i in range(1, DEPTH + 1):
             c, n, at = wedge(i)
@@ -404,7 +422,7 @@
     w1, sp, bumps, gyl, gyh, lg, ca, cb, cv,
 ):
     del w1_in
-    order("py", gyl, gyh, gye, gyo)
+    order("r2y", gyl, gyh, gye, gyo)
     one = lambda r: pl.ds(r, 1)
     for h in range(HALVES):
         for i in range(1, DEPTH + 1):
@@ -505,44 +523,91 @@
         carried(h, 0, T, u2p, sweep)
 
 
-def last_kernel(
-    w1_in, sp, bumps, vxl, vxh, vye, vyo, hxl, hxh, hyl, hyh, u2p, b, ld,
-    w1, out, vyl, vyh, w0, wh, sh, oh, sems,
-):
+def ring(n, h, v, bh, c, wh, oh, ends, corners, here, to):
+    one = lambda r: pl.ds(r, 1)
+    wh[n, mid(), :] = v[h, pl.ds(0, T), :]
+    for r, (outside, inside) in zip((0, T - 1), ends):
+        wh[n, one(8 + r), :] = wh[n, one(8 + r), :] + outside
+        oh[n, one(r), :] = oh[n, one(r), :] + inside
+    u2h = wh[n, mid(), :]
+    w0h = u2h + c
+    wh[n, mid(), :] = w0h
+    wh[n, one(7), :], wh[n, one(8 + T), :] = corners
+    near = (wh[n, left(), :] + wh[n, right(), :]) + oh[n]
+    here(u2h)
+    to(0.2 * w0h + bh * ((v[h, pl.ds(T, T), :] + c) + near))
+
+
+def corner_values(bumps, sp, h):
+    bump = lambda i, j, k: bumps[h, pl.ds(4 * (2 * i + j) + k, 1), :]
+    diag = {
+        (i, j): bump(i, j, 3) + sp[h, (0, NB + 1)[i], pl.ds((7, 8 + T)[j], 1), :] for i in range(2) for j in range(2)
+    }
+    return bump, diag
+
+
+INNER_X = T - 16
+
+
+def inner_kernel(w1_in, sp, bumps, vye, vyo, hyl, hyh, u2p, b, ld, w1, out, vyl, vyh, w0, wh, oh, sems):
     del w1_in
-    order("py", vyl, vyh, vye, vyo)
+    order("u2y", vyl, vyh, vye, vyo)
     one = lambda r: pl.ds(r, 1)
-    bump = lambda h, i, j, k: bumps[h, one(4 * (2 * i + j) + k), :]
-    stride = (NB + 2) * PC
-    sp2, b2 = sp.reshape(HALVES * stride, LANES), b.reshape(HALVES * T * T, LANES)
-    w12, u2p2 = w1.reshape(HALVES * PLANE, LANES), u2p.reshape(HALVES * PLANE, LANES)
-    U2, D, BH = pl.ds(0, T), pl.ds(T, T), pl.ds(2 * T, T)
     n = 0
-    for h in range(HALVES):
+    copies = []
+    for h in range(HALVES):
+        bump, diag = corner_values(bumps, sp, h)
         for i in range(2):
             for j in range(2):
-                e, y, x = bump(h, i, j, 0), (0, T - 1)[i], (0, T - 1)[j]
+                e, y, x = bump(i, j, 0), (0, T - 1)[i], (0, T - 1)[j]
                 yi, xi = (1, T - 2)[i], (1, T - 2)[j]
                 for yy, xx, f in ((y, x, None), (y, xi, b), (yi, x, b)):
                     f = 0.2 if f is None else b[h, yy, one(xx), :]
                     w1[h, yy + 1, one(xx + 8), :] = w1[h, yy + 1, one(xx + 8), :] + f * e
-        diag = {
-            (i, j): bump(h, i, j, 3) + sp[h, (0, NB + 1)[i], one((7, 8 + T)[j]), :] for i in range(2) for j in range(2)
-        }
-
-        def ring(n, v, bh, c, here, to, ends, corners, h=h):
-            wh[n, mid(), :] = v[h, U2, :]
-            for r, (outside, inside) in zip((0, T - 1), ends):
-                wh[n, one(8 + r), :] = wh[n, one(8 + r), :] + outside
-                oh[n, one(r), :] = oh[n, one(r), :] + inside
-            u2h = wh[n, mid(), :]
-            w0h = u2h + c
-            wh[n, mid(), :] = w0h
-            wh[n, one(7), :], wh[n, one(8 + T), :] = corners
-            near = (wh[n, left(), :] + wh[n, right(), :]) + oh[n]
-            here(u2h)
-            to(0.2 * w0h + bh * ((v[h, D, :] + c) + near))
-
+        for i, (v, hy) in enumerate(((vyl, hyl), (vyh, hyh))):
+            y = (0, T - 1)[i]
+            oh[n] = u2p[h, y + 1, mid(), :] + sp[h, (1, NB)[i], mid(), :]
+
+            def here(u2h, h=h, y=y):
+                w1[h, y + 1, mid(), :] = w1[h, y + 1, mid(), :] + b[h, y] * u2h
+
+            def to(value, h=h, i=i):
+                w1[h, (0, T + 1)[i], mid(), :] = value
+
+            ring(
+                n, h, v, hy[h, pl.ds(2 * T, T), :], sp[h, (0, NB + 1)[i], mid(), :], wh, oh,
+                [(bump(i, j, 2), bump(i, j, 0)) for j in range(2)], (diag[i, 0], diag[i, 1]), here, to,
+            )
+            n += 1
+
+        def last(y, c, near, h=h):
+            w0[h, y] = 0.2 * c + b[h, y, pl.ds(8, INNER_X), :] * (ld[h, y, pl.ds(8, INNER_X), :] + near)
+
+        step = T // 4
+        for q in range(4):
+            carried(h, q * step, (q + 1) * step, w1, last, 8, INNER_X)
+            copies.append(
+                pltpu.make_async_copy(
+                    w0.at[h, pl.ds(q * step, step)],
+                    out.at[pl.ds(q * step, step), pl.ds(8, INNER_X), pl.ds(h * LANES, LANES)],
+                    sems.at[h, q],
+                )
+            )
+            copies[-1].start()
+    for c in copies:
+        c.wait()
+
+
+def last_kernel(w1_in, out_in, sp, bumps, vxe, vxo, hxl, hxh, u2p, b, ld, w1, out, vxl, vxh, w0, wh, sh, oh, sems):
+    del w1_in, out_in
+    order("u2x", vxl, vxh, vxe, vxo)
+    stride = (NB + 2) * PC
+    sp2, b2 = sp.reshape(HALVES * stride, LANES), b.reshape(HALVES * T * T, LANES)
+    w12, u2p2 = w1.reshape(HALVES * PLANE, LANES), u2p.reshape(HALVES * PLANE, LANES)
+    n = 0
+    copies = []
+    for h in range(HALVES):
+        bump, diag = corner_values(bumps, sp, h)
         for j, (v, hx) in enumerate(((vxl, hxl), (vxh, hxh))):
             x, xo = (0, T - 1)[j], (-1, T)[j]
             for k in range(R):
@@ -558,40 +623,24 @@
                 w12[column(h, xo), :] = value
 
             ring(
-                n, v, hx[h, BH, :], sh[n, 0], here, to,
-                [(bump(h, i, j, 1), bump(h, i, j, 0)) for i in range(2)], (diag[0, j], diag[1, j]),
+                n, h, v, hx[h, pl.ds(2 * T, T), :], sh[n, 0], wh, oh,
+                [(bump(i, j, 1), bump(i, j, 0)) for i in range(2)], (diag[0, j], diag[1, j]), here, to,
             )
             n += 1
-        for i, (v, hy) in enumerate(((vyl, hyl), (vyh, hyh))):
-            y = (0, T - 1)[i]
-            oh[n] = u2p[h, y + 1, mid(), :] + sp[h, (1, NB)[i], mid(), :]
-
-            def here(u2h, h=h, y=y):
-                w1[h, y + 1, mid(), :] = w1[h, y + 1, mid(), :] + b[h, y] * u2h
-
-            def to(value, h=h, i=i):
-                w1[h, (0, T + 1)[i], mid(), :] = value
-
-            ring(
-                n, v, hy[h, BH, :], sp[h, (0, NB + 1)[i], mid(), :], here, to,
-                [(bump(h, i, j, 2), bump(h, i, j, 0)) for j in range(2)], (diag[i, 0], diag[i, 1]),
-            )
-            n += 1
-
-    copies = []
-    for h in range(HALVES):
-
-        def last(y, c, near, h=h):
-            w0[h, y + 1, mid(), :] = 0.2 * c + b[h, y] * (ld[h, y] + near)
-
-        step = T // 4
-        for q in range(4):
-            carried(h, q * step, (q + 1) * step, w1, last)
+
+        for j, x in enumerate((0, T - 8)):
+
+            def sweep(k, c, h=h, j=j, x=x):
+                y = pl.multiple_of(k * 8, 8)
+                tile = (h, pl.ds(y, 8), pl.ds(x, 8))
+                near = near_tile(w1, h, y, x)
+                w0[h, j, pl.ds(y, 8)] = 0.2 * w1[h, pl.ds(y + 1, 8), pl.ds(8 + x, 8)] + b[tile] * (ld[tile] + near)
+                return c
+
+            lax.fori_loop(0, T // 8, sweep, 0, unroll=2)
             copies.append(
                 pltpu.make_async_copy(
-                    w0.at[h, pl.ds(1 + q * step, step), mid(), :],
-                    out.at[pl.ds(q * step, step), :, pl.ds(h * LANES, LANES)],
-                    sems.at[h, q],
+                    w0.at[h, j], out.at[:, pl.ds(x, 8), pl.ds(h * LANES, LANES)], sems.at[h, j]
                 )
             )
             copies[-1].start()
@@ -607,18 +656,14 @@
 H = pl.BlockSpec(memory_space=pltpu.HBM)
 
 
-def swapped(axis, even, odd):
+def exchange(name, even, odd):
+    axis = AXIS[name]
     size = lax.axis_size(axis)
-    got = []
-    if axis not in SWAPPED:
-        up = [(i, (i + 1) % size) for i in range(size)]
+    up = [(i, (i + 1) % size) for i in range(size)]
+    if name not in SWAPPED:
         return lax.ppermute(odd, axis, up), lax.ppermute(even, axis, [(b, a) for a, b in up])
-    for first, value in ((0, even), (1, odd)):
-        pairs = []
-        for k in range(first, size, 2):
-            pairs += [(k, (k + 1) % size), ((k + 1) % size, k)]
-        got.append(lax.ppermute(value, axis, pairs))
-    return got
+    pairs = [[p for a, b in up[k::2] for p in ((a, b), (b, a))] for k in range(2)]
+    return lax.ppermute(even, axis, pairs[0]), lax.ppermute(odd, axis, pairs[1])
 
 
 def estimate(flops, size):
@@ -643,7 +688,7 @@
         compiler_params=pltpu.CompilerParams(vmem_limit_bytes=4 * MIB),
         name="rowedges",
     )(*inputs)
-    hye, hyo = swapped("py", pye, pyo)
+    hye, hyo = exchange("r1y", pye, pyo)
     pxl, pxh, pxe, pxo = pl.pallas_call(
         column_edges,
         in_specs=[H] * 3,
@@ -653,7 +698,7 @@
         compiler_params=pltpu.CompilerParams(vmem_limit_bytes=8 * MIB),
         name="columnedges",
     )(*inputs)
-    hxe, hxo = swapped("px", pxe, pxo)
+    hxe, hxo = exchange("r1x", pxe, pxo)
     u1p, b, ld, m, mo, kxe, kxo = pl.pallas_call(
         first_kernel,
         in_specs=[H] * 3,
@@ -666,7 +711,7 @@
         cost_estimate=estimate(10**7, 12 * MIB),
         name="first",
     )(*inputs)
-    gme, gmo = swapped("px", kxe, kxo)
+    gme, gmo = exchange("massx", kxe, kxo)
     outer = vmem(HALVES, 2 * T, LANES)
     u2p, part_sums = pl.pallas_call(
         bulk_kernel,
@@ -691,8 +736,8 @@
         compiler_params=pltpu.CompilerParams(vmem_limit_bytes=8 * MIB),
         name="second",
     )(u1p, u2p, part_sums, b, ld, m, pxl, pxh, pyl, pyh, hxe, hxo, hye, hyo)
-    gxe, gxo = swapped("px", qxe, qxo)
-    vxl, vxh = swapped("px", vxe, vxo)
+    gxe, gxo = exchange("r2x", qxe, qxo)
+    vxe, vxo = exchange("u2x", vxe, vxo)
     mx, kye, kyo = pl.pallas_call(
         mass_kernel,
         in_specs=[V] * 3,
@@ -702,7 +747,7 @@
         compiler_params=pltpu.CompilerParams(vmem_limit_bytes=8 * MIB),
         name="mass",
     )(mo, gme, gmo)
-    gke, gko = swapped("py", kye, kyo)
+    gke, gko = exchange("massy", kye, kyo)
     lx, s0, s1, qye, qyo = pl.pallas_call(
         third_kernel,
         in_specs=[V] * 8,
@@ -714,8 +759,8 @@
         compiler_params=pltpu.CompilerParams(vmem_limit_bytes=8 * MIB),
         name="third",
     )(lp, own, qxl, qxh, gxe, gxo, hxl, hxh)
-    gye, gyo = swapped("py", qye, qyo)
-    vye, vyo = swapped("py", vye, vyo)
+    gye, gyo = exchange("r2y", qye, qyo)
+    vye, vyo = exchange("u2y", vye, vyo)
     grid = vmem(HALVES, CR, CW, LANES)
     bc = pl.pallas_call(
         rate_kernel,
@@ -746,18 +791,34 @@
         cost_estimate=estimate(10**7, 4 * MIB),
         name="coarse",
     )(lx, bc, s0, s1, gye, gyo, hxl, hxh, hyl, hyh, pxl, pxh, b, u3)
+    result = jax.ShapeDtypeStruct(load_terms.shape, F)
+    sides = [vmem(4, PC, LANES), vmem(4, T, LANES)]
+    w1, partial = pl.pallas_call(
+        inner_kernel,
+        in_specs=[V] * 10,
+        out_specs=[V, H],
+        out_shape=[vmem(*padded), result],
+        scratch_shapes=[outer] * 2
+        + [vmem(HALVES, T, INNER_X, LANES)]
+        + sides
+        + [pltpu.SemaphoreType.DMA((HALVES, 4))],
+        input_output_aliases={0: 0},
+        compiler_params=pltpu.CompilerParams(vmem_limit_bytes=12 * MIB),
+        cost_estimate=estimate(10**7, 4 * MIB),
+        name="inner",
+    )(w1, sp, bumps, vye, vyo, hyl, hyh, u2p, b, ld)
     _, corrected = pl.pallas_call(
         last_kernel,
-        in_specs=[V] * 14,
+        in_specs=[V, H] + [V] * 9,
         out_specs=[V, H],
-        out_shape=[vmem(*padded), jax.ShapeDtypeStruct(load_terms.shape, F)],
+        out_shape=[vmem(*padded), result],
         scratch_shapes=[outer] * 2
-        + [vmem(*padded)]
-        + [vmem(8, PC, LANES), vmem(8, 2, T, LANES), vmem(8, T, LANES), pltpu.SemaphoreType.DMA((HALVES, 4))],
-        input_output_aliases={0: 0},
+        + [vmem(HALVES, 2, T, 8, LANES), sides[0], vmem(4, 2, T, LANES), sides[1]]
+        + [pltpu.SemaphoreType.DMA((HALVES, 2))],
+        input_output_aliases={0: 0, 1: 1},
         compiler_params=pltpu.CompilerParams(vmem_limit_bytes=12 * MIB),
         name="last",
-    )(w1, sp, bumps, vxl, vxh, vye, vyo, hxl, hxh, hyl, hyh, u2p, b, ld)
+    )(w1, partial, sp, bumps, vxe, vxo, hxl, hxh, u2p, b, ld)
     return corrected
 
 

time: 62.7 us -> 60.9 us (0.971)
  starting transfers between devices: 31.6 us -> 26.9 us
  waiting for transfers between devices: 9.4 us -> 11.1 us
  Pallas kernels: 21.3 us -> 22.1 us
    ppermute x16, starting transfers between devices: 31.6 us -> 26.9 us  [the longest x8 24.9 us: exchange(): lax.ppermute(odd, axis, pairs[1])]
    ppermute x16, waiting for transfers between devices: 9.4 us -> 11.1 us  [the longest x8 10.5 us: exchange(): lax.ppermute(odd, axis, pairs[1])]
    pallas_call x1 -> x2, Pallas kernels: 2.78 us -> 3.68 us  [the longest x1 2.14 us: per_device(): pl.pallas_call(inner_kernel, in_specs=[V] * 10, out_specs=[V, H], out_sha...]
  transfers between devices with their start and end apart: 16 -> 16, of which waited for: 8 -> 5; matrix products, arithmetic and copies ran while one was open for 0% -> 0% of each run, Pallas kernels for 24% -> 28%
where the time goes in v5:
time: 60.9 us; the launch traced here: 60.4 us
  starting transfers between devices  26.9 us (44%)
  Pallas kernels  22.1 us (36%)
  waiting for transfers between devices  11.1 us (18%)
    ppermute x8, starting transfers between devices, exchange(): lax.ppermute(odd, axis, pairs[1])  24.9 us
    ppermute x8, waiting for transfers between devices, exchange(): lax.ppermute(odd, axis, pairs[1])  10.5 us
    pallas_call x1, Pallas kernels, per_device(): pl.pallas_call(first_kernel, in_specs=[H] * 3, out_specs=[V] * 7, out_sha...  5.32 us
    pallas_call x1, Pallas kernels, per_device(): pl.pallas_call(coarse_kernel, in_specs=[V] * 14, out_specs=[V] * 3, out_s...  3.26 us
    pallas_call x1, Pallas kernels, per_device(): pl.pallas_call(bulk_kernel, in_specs=[V] * 4, out_specs=[V] * 2, out_shap...  2.74 us
    pallas_call x1, Pallas kernels, per_device(): pl.pallas_call(column_edges, in_specs=[H] * 3, out_specs=[V] * 4, out_sha...  2.15 us
    pallas_call x1, Pallas kernels, per_device(): pl.pallas_call(inner_kernel, in_specs=[V] * 10, out_specs=[V, H], out_sha...  2.14 us
    ppermute x8, starting transfers between devices, exchange(): lax.ppermute(even, axis, pairs[0])  2.03 us
  transfers between devices with their start and end apart: 16, of which 5 were waited for; matrix products, arithmetic and copies ran while one was open for 0% of the time, Pallas kernels for 28%

profile of v5, /device:TPU:0, one launch (start us, length us, event | category | flops | bytes accessed | tf_op | source)
XLA Modules:
  0.0 60.4 jit_solution(15892536556861186126)
XLA Ops:
  0.0 2.2 %columnedges.1 = (f32[2,192,128]{2,1,0:T(8,128)S(1)}, f32[2,192,128]{2,1,0:T(8,128)S(1)}, f32[2,192,128]{2,1,0:T(8,128)S(1)}, f32[2,192,128]{2,1,0:T(8,128)S(1)}) custom-call(f32[64,64,256]{2,1,0:T(8,128)} %load_h.5, f32[64,64,256]{2,1,0:T(8,128)} %u_h.5, f32[64,64,256]{2,1,0:T(8,128)} %m_h.5), custom_call_target="tpu_custom_call" | custom-call | tf_op jit(solution)/shard_map/columnedges/pallas_call | solution.py:692
  2.2 1.7 %collective-permute-start = (f32[2,192,128]{2,1,0:T(8,128)S(1)}, f32[2,192,128]{2,1,0:T(8,128)S(1)}, u32[]{:S(2)}, u32[]{:S(2)}) collective-permute-start(f32[2,192,128]{2,1,0:T(8,128)S(1)} %get-tuple-element.61), channel_id=1, source_target_pairs={{0,1},{1,0},{2,3},{3,2},{4,5},{5,4},{6,7},{7,6},{8,9},{9,8},{10,11... | collective-permute-start | bytes 589832 | tf_op jit(solution)/shard_map/ppermute | solution.py:666
  3.8 4.0 %collective-permute-start.1 = (f32[2,192,128]{2,1,0:T(8,128)S(1)}, f32[2,192,128]{2,1,0:T(8,128)S(1)}, u32[]{:S(2)}, u32[]{:S(2)}) collective-permute-start(f32[2,192,128]{2,1,0:T(8,128)S(1)} %get-tuple-element.62), channel_id=1, source_target_pairs={{1,2},{2,1},{3,4},{4,3},{5,6},{6,5},{7,0},{0,7},{9,10},{10,9},{11,... | collective-permute-start | bytes 589832 | tf_op jit(solution)/shard_map/ppermute | solution.py:666
  7.9 1.2 %rowedges.1 = (f32[2,192,128]{2,1,0:T(8,128)S(1)}, f32[2,192,128]{2,1,0:T(8,128)S(1)}, f32[2,192,128]{2,1,0:T(8,128)S(1)}, f32[2,192,128]{2,1,0:T(8,128)S(1)}) custom-call(f32[64,64,256]{2,1,0:T(8,128)} %load_h.5, f32[64,64,256]{2,1,0:T(8,128)} %u_h.5, f32[64,64,256]{2,1,0:T(8,128)} %m_h.5), custom_call_target="tpu_custom_call" | custom-call | tf_op jit(solution)/shard_map/rowedges/pallas_call | solution.py:682
  9.1 0.1 collective-permute-start.2
  9.2 5.6 %collective-permute-start.3 = (f32[2,192,128]{2,1,0:T(8,128)S(1)}, f32[2,192,128]{2,1,0:T(8,128)S(1)}, u32[]{:S(2)}, u32[]{:S(2)}) collective-permute-start(f32[2,192,128]{2,1,0:T(8,128)S(1)} %get-tuple-element.64), channel_id=1, source_target_pairs={{8,16},{16,8},{24,32},{32,24},{40,48},{48,40},{56,64},{64,56},{72,... | collective-permute-start | bytes 589832 | tf_op jit(solution)/shard_map/ppermute | solution.py:666
  14.8 5.3 %first.1 = (f32[2,66,80,128]{3,2,1,0:T(8,128)S(1)}, f32[2,64,64,128]{3,2,1,0:T(8,128)S(1)}, f32[2,64,64,128]{3,2,1,0:T(8,128)S(1)}, f32[2,64,64,128]{3,2,1,0:T(8...) custom-call(f32[64,64,256]{2,1,0:T(8,128)} %load_h.5, ...), custom_call_target="tpu_custom_call" | custom-call | flops 10000000 | bytes 12582912 | tf_op jit(solution)/shard_map/first/pallas_call | solution.py:702
  20.1 2.7 %bulk.1 = (f32[2,66,80,128]{3,2,1,0:T(8,128)S(1)}, f32[2048,128]{1,0:T(8,128)S(1)}) custom-call(f32[2,66,80,128]{3,2,1,0:T(8,128)S(1)} %get-tuple-element.51.u1p.u1p_in, f32[2,64,64,128]{3,2,1,0:T(8,128)S(1)} %get-tuple-element.52.b, f32[2,64,64,128]{3,2,1,0:T(8,128)S(1)} %get-tuple-element.53.ld, f32[2,64,64,128]{3,2,1,0:T(8,128)S(1)} %get-tuple-element.54.m), custom_call_target="tpu_custom_call" | custom-call | flops 10000000 | bytes 12582912 | tf_op jit(solution)/shard_map/bulk/pallas_call | solution.py:716
  22.8 0.0 collective-permute-done.hxe
  22.8 0.0 collective-permute-done.1.hxo
  22.9 0.0 collective-permute-done.2.hye
  22.9 0.0 collective-permute-done.3.hyo
  22.9 1.6 %second.1 = (f32[2,66,80,128]{3,2,1,0:T(8,128)S(1)}, f32[2,66,80,128]{3,2,1,0:T(8,128)S(1)}, f32[2048,128]{1,0:T(8,128)S(1)}, f32[512,128]{1,0:T(8,128)S(1)}, f3...) custom-call(f32[2,66,80,128]{3,2,1,0:T(8,128)S(1)} %get-tuple-elemen, ...), custom_call_target="tpu_custom_call", output_to_operand_aliasing={{0}: (0, {}), {1}: (1, {}), {2}: (2, {})} | custom-call | tf_op jit(solution)/shard_map/second/pallas_call | solution.py:725
  24.5 0.1 collective-permute-start.4
  24.6 3.5 %collective-permute-start.5 = (f32[2,144,128]{2,1,0:T(8,128)S(1)}, f32[2,144,128]{2,1,0:T(8,128)S(1)}, u32[]{:S(2)}, u32[]{:S(2)}) collective-permute-start(f32[2,144,128]{2,1,0:T(8,128)S(1)} %get-tuple-element.70), channel_id=1, source_target_pairs={{1,2},{2,1},{3,4},{4,3},{5,6},{6,5},{7,0},{0,7},{9,10},{10,9},{11,... | collective-permute-start | bytes 442376 | tf_op jit(solution)/shard_map/ppermute | solution.py:666
  28.1 0.0 collective-permute-start.6
  28.1 1.9 %collective-permute-start.7 = (f32[2,112,128]{2,1,0:T(8,128)S(1)}, f32[2,112,128]{2,1,0:T(8,128)S(1)}, u32[]{:S(2)}, u32[]{:S(2)}) collective-permute-start(f32[2,112,128]{2,1,0:T(8,128)S(1)} %get-tuple-element.76), channel_id=1, source_target_pairs={{1,2},{2,1},{3,4},{4,3},{5,6},{6,5},{7,0},{0,7},{9,10},{10,9},{11,... | collective-permute-start | bytes 344072 | tf_op jit(solution)/shard_map/ppermute | solution.py:666
  30.0 0.5 collective-permute-done.4.gxe
  30.5 5.5 %collective-permute-done.5.gxo = f32[2,144,128]{2,1,0:T(8,128)S(1)} collective-permute-done((f32[2,144,128]{2,1,0:T(8,128)S(1)}, f32[2,144,128]{2,1,0:T(8,128)S(1)}, u32[]{:S(2)}, u32[]{:S(2)}) %collective-permute-start.5) | collective-permute-done | bytes 147488 | tf_op jit(solution)/shard_map/ppermute | solution.py:666
  36.0 0.4 third.1
  36.4 0.1 collective-permute-start.10
  36.5 0.0 collective-permute-done.6.gme
  36.5 2.3 %collective-permute-done.7.gmo = f32[2,112,128]{2,1,0:T(8,128)S(1)} collective-permute-done((f32[2,112,128]{2,1,0:T(8,128)S(1)}, f32[2,112,128]{2,1,0:T(8,128)S(1)}, u32[]{:S(2)}, u32[]{:S(2)}) %collective-permute-start.7) | collective-permute-done | bytes 114720 | tf_op jit(solution)/shard_map/ppermute | solution.py:666
  38.7 0.3 mass.1
  39.0 0.1 collective-permute-start.8
  39.1 2.7 %collective-permute-start.9 = (f32[2,168,128]{2,1,0:T(8,128)S(1)}, f32[2,168,128]{2,1,0:T(8,128)S(1)}, u32[]{:S(2)}, u32[]{:S(2)}) collective-permute-start(f32[2,168,128]{2,1,0:T(8,128)S(1)} %get-tuple-element.79), channel_id=1, source_target_pairs={{8,16},{16,8},{24,32},{32,24},{40,48},{48,40},{56,64},{64,56},{72,... | collective-permute-start | bytes 516104 | tf_op jit(solution)/shard_map/ppermute | solution.py:666
  41.8 2.7 %collective-permute-start.11 = (f32[2,208,128]{2,1,0:T(8,128)S(1)}, f32[2,208,128]{2,1,0:T(8,128)S(1)}, u32[]{:S(2)}, u32[]{:S(2)}) collective-permute-start(f32[2,208,128]{2,1,0:T(8,128)S(1)} %get-tuple-element.83), channel_id=1, source_target_pairs={{8,16},{16,8},{24,32},{32,24},{40,48},{48,40},{56,64},{64,56},{72,... | collective-permute-start | bytes 638984 | tf_op jit(solution)/shard_map/ppermute | solution.py:666
  44.5 0.0 collective-permute-start.12
  44.5 0.0 collective-permute-done.8.gke
  44.5 2.6 %collective-permute-start.13 = (f32[2,128,128]{2,1,0:T(8,128)S(1)}, f32[2,128,128]{2,1,0:T(8,128)S(1)}, u32[]{:S(2)}, u32[]{:S(2)}) collective-permute-start(f32[2,128,128]{2,1,0:T(8,128)S(1)} %get-tuple-element.91), channel_id=1, source_target_pairs={{8,16},{16,8},{24,32},{32,24},{40,48},{48,40},{56,64},{64,56},{72,... | collective-permute-start | bytes 393224 | tf_op jit(solution)/shard_map/ppermute | solution.py:666
  47.2 1.6 %collective-permute-done.9.gko = f32[2,168,128]{2,1,0:T(8,128)S(1)} collective-permute-done((f32[2,168,128]{2,1,0:T(8,128)S(1)}, f32[2,168,128]{2,1,0:T(8,128)S(1)}, u32[]{:S(2)}, u32[]{:S(2)}) %collective-permute-start.9) | collective-permute-done | bytes 172064 | tf_op jit(solution)/shard_map/ppermute | solution.py:666
  48.8 0.0 collective-permute-start.14
  48.8 0.0 collective-permute-done.10.gye
  48.8 1.9 %collective-permute-start.15 = (f32[2,128,128]{2,1,0:T(8,128)S(1)}, f32[2,128,128]{2,1,0:T(8,128)S(1)}, u32[]{:S(2)}, u32[]{:S(2)}) collective-permute-start(f32[2,128,128]{2,1,0:T(8,128)S(1)} %get-tuple-element.95), channel_id=1, source_target_pairs={{1,2},{2,1},{3,4},{4,3},{5,6},{6,5},{7,0},{0,7},{9,10},{10,9},{11,... | collective-permute-start | bytes 393224 | tf_op jit(solution)/shard_map/ppermute | solution.py:666
  50.7 1.4 %ahead.1.w1_in = f32[2,66,80,128]{3,2,1,0:T(8,128)S(1)} custom-call(f32[2,66,80,128]{3,2,1,0:T(8,128)S(1)} %get-tuple-element.86.u2p, f32[2,64,64,128]{3,2,1,0:T(8,128)S(1)} %get-tuple-element.52.b, f32[2,64,64,128]{3,2,1,0:T(8,128)S(1)} %get-tuple-element.53.ld), custom_call_target="tpu_custom_call" | custom-call | tf_op jit(solution)/shard_map/ahead/pallas_call | solution.py:775
  52.0 0.2 rate.1.bc
  52.2 1.2 %collective-permute-done.11.gyo = f32[2,208,128]{2,1,0:T(8,128)S(1)} collective-permute-done((f32[2,208,128]{2,1,0:T(8,128)S(1)}, f32[2,208,128]{2,1,0:T(8,128)S(1)}, u32[]{:S(2)}, u32[]{:S(2)}) %collective-permute-start.11) | collective-permute-done | bytes 213024 | tf_op jit(solution)/shard_map/ppermute | solution.py:666
  53.4 3.3 %coarse.1 = (f32[2,66,80,128]{3,2,1,0:T(8,128)S(1)}, f32[2,18,80,128]{3,2,1,0:T(8,128)S(1)}, f32[2,16,128]{2,1,0:T(8,128)S(1)}) custom-call(f32[2,16,32,128]{3,2,1,0:T(8,128)S(1)} %get-tuple-element.73.lx, f32[2,30,32,128]{3,2,1,0:T(8,128)S(1)} %rate.1.bc, f32[2,32,128]{2,1,0:T(8,128)S(1)} %get-tuple-element.80.s0, ...), custom_call_target="tpu_custom_call", output_to_operand_aliasing={{0}: (13, {})} | custom-call | flops 10000000 | bytes 4194304 | tf_op jit(solution)/shard_map/coarse/pallas_call | solution.py:783
  56.6 0.0 collective-permute-done.12.vye
  56.6 0.0 collective-permute-done.13.vyo
  56.6 2.1 %inner.1 = (f32[2,66,80,128]{3,2,1,0:T(8,128)S(1)}, f32[64,64,256]{2,1,0:T(8,128)}) custom-call(f32[2,66,80,128]{3,2,1,0:T(8,128)S(1)} %get-tuple-element.87.w1_in, f32[2,18,80,128]{3,2,1,0:T(8,128)S(1)} %get-tuple-element.88.sp, f32[2,16,128]{2,1,0:T(8,128)S(1)} %get-tuple-element.89.bumps, ...), custom_call_target="tpu_custom_call", output_to_operand_aliasing={{0}: (0, {})} | custom-call | flops 10000000 | bytes 4194304 | tf_op jit(solution)/shard_map/inner/pallas_call | solution.py:796
  58.8 0.0 collective-permute-done.14.vxe
  58.8 0.0 collective-permute-done.15.vxo
  58.8 1.5 %last.1 = (f32[2,66,80,128]{3,2,1,0:T(8,128)S(1)}, f32[64,64,256]{2,1,0:T(8,128)}) custom-call(f32[2,66,80,128]{3,2,1,0:T(8,128)S(1)} %get-tuple-element.92.w1_in, f32[64,64,256]{2,1,0:T(8,128)} %get-tuple-element.93.out_in, f32[2,18,80,128]{3,2,1,0:T(8,128)S(1)} %get-tuple-element.88.sp, ...), custom_call_target="tpu_custom_call", output_to_operand_aliasing={{0}: (0, {}), {1}: (1, {})} | custom-call | tf_op jit(solution)/shard_map/last/pallas_call | solution.py:810
Async XLA Ops:
  2.2 20.7 %collective-permute-start = (f32[2,192,128]{2,1,0:T(8,128)S(1)}, f32[2,192,128]{2,1,0:T(8,128)S(1)}, u32[]{:S(2)}, u32[]{:S(2)}) collective-permute-start(f32[2,192,128]{2,1,0:T(8,128)S(1)} %get-tuple-element.61), channel_id=1, source_target_pairs={{0,1},{1,0},{2,3},{3,2},{4,5},{5,4},{6,7},{7,6},{8,9},{9,8},{10,11... | collective-permute-start | bytes 589832 | tf_op jit(solution)/shard_map/ppermute | solution.py:666
  3.8 19.0 %collective-permute-start.1 = (f32[2,192,128]{2,1,0:T(8,128)S(1)}, f32[2,192,128]{2,1,0:T(8,128)S(1)}, u32[]{:S(2)}, u32[]{:S(2)}) collective-permute-start(f32[2,192,128]{2,1,0:T(8,128)S(1)} %get-tuple-element.62), channel_id=1, source_target_pairs={{1,2},{2,1},{3,4},{4,3},{5,6},{6,5},{7,0},{0,7},{9,10},{10,9},{11,... | collective-permute-start | bytes 589832 | tf_op jit(solution)/shard_map/ppermute | solution.py:666
  9.1 13.8 %collective-permute-start.2 = (f32[2,192,128]{2,1,0:T(8,128)S(1)}, f32[2,192,128]{2,1,0:T(8,128)S(1)}, u32[]{:S(2)}, u32[]{:S(2)}) collective-permute-start(f32[2,192,128]{2,1,0:T(8,128)S(1)} %get-tuple-element.63), channel_id=1, source_target_pairs={{0,8},{8,0},{16,24},{24,16},{32,40},{40,32},{48,56},{56,48},{64,72... | collective-permute-start | bytes 589832 | tf_op jit(solution)/shard_map/ppermute | solution.py:666
  9.2 13.7 %collective-permute-start.3 = (f32[2,192,128]{2,1,0:T(8,128)S(1)}, f32[2,192,128]{2,1,0:T(8,128)S(1)}, u32[]{:S(2)}, u32[]{:S(2)}) collective-permute-start(f32[2,192,128]{2,1,0:T(8,128)S(1)} %get-tuple-element.64), channel_id=1, source_target_pairs={{8,16},{16,8},{24,32},{32,24},{40,48},{48,40},{56,64},{64,56},{72,... | collective-permute-start | bytes 589832 | tf_op jit(solution)/shard_map/ppermute | solution.py:666
  24.5 6.0 %collective-permute-start.4 = (f32[2,144,128]{2,1,0:T(8,128)S(1)}, f32[2,144,128]{2,1,0:T(8,128)S(1)}, u32[]{:S(2)}, u32[]{:S(2)}) collective-permute-start(f32[2,144,128]{2,1,0:T(8,128)S(1)} %get-tuple-element.69), channel_id=1, source_target_pairs={{0,1},{1,0},{2,3},{3,2},{4,5},{5,4},{6,7},{7,6},{8,9},{9,8},{10,11... | collective-permute-start | bytes 442376 | tf_op jit(solution)/shard_map/ppermute | solution.py:666
  24.6 11.4 %collective-permute-start.5 = (f32[2,144,128]{2,1,0:T(8,128)S(1)}, f32[2,144,128]{2,1,0:T(8,128)S(1)}, u32[]{:S(2)}, u32[]{:S(2)}) collective-permute-start(f32[2,144,128]{2,1,0:T(8,128)S(1)} %get-tuple-element.70), channel_id=1, source_target_pairs={{1,2},{2,1},{3,4},{4,3},{5,6},{6,5},{7,0},{0,7},{9,10},{10,9},{11,... | collective-permute-start | bytes 442376 | tf_op jit(solution)/shard_map/ppermute | solution.py:666
  28.1 8.3 %collective-permute-start.6 = (f32[2,112,128]{2,1,0:T(8,128)S(1)}, f32[2,112,128]{2,1,0:T(8,128)S(1)}, u32[]{:S(2)}, u32[]{:S(2)}) collective-permute-start(f32[2,112,128]{2,1,0:T(8,128)S(1)} %get-tuple-element.75), channel_id=1, source_target_pairs={{0,1},{1,0},{2,3},{3,2},{4,5},{5,4},{6,7},{7,6},{8,9},{9,8},{10,11... | collective-permute-start | bytes 344072 | tf_op jit(solution)/shard_map/ppermute | solution.py:666
  28.1 10.6 %collective-permute-start.7 = (f32[2,112,128]{2,1,0:T(8,128)S(1)}, f32[2,112,128]{2,1,0:T(8,128)S(1)}, u32[]{:S(2)}, u32[]{:S(2)}) collective-permute-start(f32[2,112,128]{2,1,0:T(8,128)S(1)} %get-tuple-element.76), channel_id=1, source_target_pairs={{1,2},{2,1},{3,4},{4,3},{5,6},{6,5},{7,0},{0,7},{9,10},{10,9},{11,... | collective-permute-start | bytes 344072 | tf_op jit(solution)/shard_map/ppermute | solution.py:666
  36.4 12.5 %collective-permute-start.10 = (f32[2,208,128]{2,1,0:T(8,128)S(1)}, f32[2,208,128]{2,1,0:T(8,128)S(1)}, u32[]{:S(2)}, u32[]{:S(2)}) collective-permute-start(f32[2,208,128]{2,1,0:T(8,128)S(1)} %get-tuple-element.82), channel_id=1, source_target_pairs={{0,8},{8,0},{16,24},{24,16},{32,40},{40,32},{48,56},{56,48},{64,72... | collective-permute-start | bytes 638984 | tf_op jit(solution)/shard_map/ppermute | solution.py:666
  39.0 5.5 %collective-permute-start.8 = (f32[2,168,128]{2,1,0:T(8,128)S(1)}, f32[2,168,128]{2,1,0:T(8,128)S(1)}, u32[]{:S(2)}, u32[]{:S(2)}) collective-permute-start(f32[2,168,128]{2,1,0:T(8,128)S(1)} %get-tuple-element.78), channel_id=1, source_target_pairs={{0,8},{8,0},{16,24},{24,16},{32,40},{40,32},{48,56},{56,48},{64,72... | collective-permute-start | bytes 516104 | tf_op jit(solution)/shard_map/ppermute | solution.py:666
  39.1 9.7 %collective-permute-start.9 = (f32[2,168,128]{2,1,0:T(8,128)S(1)}, f32[2,168,128]{2,1,0:T(8,128)S(1)}, u32[]{:S(2)}, u32[]{:S(2)}) collective-permute-start(f32[2,168,128]{2,1,0:T(8,128)S(1)} %get-tuple-element.79), channel_id=1, source_target_pairs={{8,16},{16,8},{24,32},{32,24},{40,48},{48,40},{56,64},{64,56},{72,... | collective-permute-start | bytes 516104 | tf_op jit(solution)/shard_map/ppermute | solution.py:666
  41.8 11.6 %collective-permute-start.11 = (f32[2,208,128]{2,1,0:T(8,128)S(1)}, f32[2,208,128]{2,1,0:T(8,128)S(1)}, u32[]{:S(2)}, u32[]{:S(2)}) collective-permute-start(f32[2,208,128]{2,1,0:T(8,128)S(1)} %get-tuple-element.83), channel_id=1, source_target_pairs={{8,16},{16,8},{24,32},{32,24},{40,48},{48,40},{56,64},{64,56},{72,... | collective-permute-start | bytes 638984 | tf_op jit(solution)/shard_map/ppermute | solution.py:666
  44.5 12.1 %collective-permute-start.12 = (f32[2,128,128]{2,1,0:T(8,128)S(1)}, f32[2,128,128]{2,1,0:T(8,128)S(1)}, u32[]{:S(2)}, u32[]{:S(2)}) collective-permute-start(f32[2,128,128]{2,1,0:T(8,128)S(1)} %get-tuple-element.90), channel_id=1, source_target_pairs={{0,8},{8,0},{16,24},{24,16},{32,40},{40,32},{48,56},{56,48},{64,72... | collective-permute-start | bytes 393224 | tf_op jit(solution)/shard_map/ppermute | solution.py:666
  44.5 12.1 %collective-permute-start.13 = (f32[2,128,128]{2,1,0:T(8,128)S(1)}, f32[2,128,128]{2,1,0:T(8,128)S(1)}, u32[]{:S(2)}, u32[]{:S(2)}) collective-permute-start(f32[2,128,128]{2,1,0:T(8,128)S(1)} %get-tuple-element.91), channel_id=1, source_target_pairs={{8,16},{16,8},{24,32},{32,24},{40,48},{48,40},{56,64},{64,56},{72,... | collective-permute-start | bytes 393224 | tf_op jit(solution)/shard_map/ppermute | solution.py:666
  48.8 10.0 %collective-permute-start.14 = (f32[2,128,128]{2,1,0:T(8,128)S(1)}, f32[2,128,128]{2,1,0:T(8,128)S(1)}, u32[]{:S(2)}, u32[]{:S(2)}) collective-permute-start(f32[2,128,128]{2,1,0:T(8,128)S(1)} %get-tuple-element.94), channel_id=1, source_target_pairs={{0,1},{1,0},{2,3},{3,2},{4,5},{5,4},{6,7},{7,6},{8,9},{9,8},{10,11... | collective-permute-start | bytes 393224 | tf_op jit(solution)/shard_map/ppermute | solution.py:666
  48.8 10.0 %collective-permute-start.15 = (f32[2,128,128]{2,1,0:T(8,128)S(1)}, f32[2,128,128]{2,1,0:T(8,128)S(1)}, u32[]{:S(2)}, u32[]{:S(2)}) collective-permute-start(f32[2,128,128]{2,1,0:T(8,128)S(1)} %get-tuple-element.95), channel_id=1, source_target_pairs={{1,2},{2,1},{3,4},{4,3},{5,6},{6,5},{7,0},{0,7},{9,10},{10,9},{11,... | collective-permute-start | bytes 393224 | tf_op jit(solution)/shard_map/ppermute | solution.py:666
